TPU v7x, 32 devices: a whole 2x2x4 slice. The times are simulated.
32 devices in a mesh: src: 2 (over x), space: 16 (over z, y, core).
Axes of the slice: x: 2, y: 2, z: 4, core: 2. Of those that a mesh axis runs over, the one named last changes fastest.
Arguments:
- adjoint_source: float32 [2, 6, 64, 64, 128], P('src', None, 'space'), may hold values from -6 to 6
- forward_field: bfloat16 [2, 6, 64, 64, 128], P('src', None, 'space'), may hold values from -6 to 6
- medium: float32 [2, 64, 64, 128], P(None, 'space'), may hold values from 0.3 to 3
- plane_map: int32 [64, 64], P('space'), may hold values from 0 to 15, as said below
- depth: int32 [2, 64, 64], P('src', 'space'), may hold values from 1 to 128
- rough: float32 [9, 16, 32, 128], P(None, 'space'), may hold values from 0.2 to 1
Outputs:
- gradient: float32 [16, 32, 128], P('space')
Inputs may be any that keep to these rules, and one draw needn't show every extreme that they name: plane_map[x, y] differs from x // 4 by at most 2.
All inputs are finite; a program needn't handle non-finite values.
Results may differ from a plain program's by a relative error of at most 0.0003.
Values sent between devices are 32-bit elements; how exact they have to be, the bound alone decides.
No kernel may reach another device: no remote copies, remote signals or barrier semaphores. Data moves between devices by JAX's collectives and lax.ppermute only.
A program may use at most 64 MiB of HBM per device.

v0:
```python
import jax
import jax.numpy as jnp
from jax import lax
from jax.sharding import PartitionSpec as P

SWEEPS = 4
REACH = 2


sweep_steps = (0.323, 1.658, 0.422, 0.752)


def padded_2(shard, sides, width):
    for axis, dim in sides:
        size, length = (lax.axis_size(axis), shard.shape[dim])
        up = [(i, (i + 1) % size) for i in range(size - 1)]
        down = [(j, i) for i, j in up]
        last = lax.slice_in_dim(shard, length - width, length, axis=dim)
        first = lax.slice_in_dim(shard, 0, width, axis=dim)
        before = lax.ppermute(last, axis, up)
        after = lax.ppermute(first, axis, down)
        shard = jnp.concatenate([before, shard, after], axis=dim)
    return shard


def shifted(value, axis, steps):
    count = lax.axis_size(axis)
    first, last = (max(0, -steps), min(count, count - steps))
    return lax.ppermute(value, axis, [(source, source + steps) for source in range(first, last)])


def ahead_rows(value):
    return jnp.concatenate([value[..., 1:, :], jnp.zeros_like(value[..., :1, :])], axis=-2)


def ahead_depth(value):
    return jnp.concatenate([value[..., 1:], jnp.zeros_like(value[..., :1])], axis=-1)


def behind_rows(value):
    return jnp.concatenate([jnp.zeros_like(value[..., :1, :]), value[..., :-1, :]], axis=-2) - value


def behind_depth(value):
    return jnp.concatenate([jnp.zeros_like(value[..., :1]), value[..., :-1]], axis=-1) - value


def lower_planes(value):
    return value[..., :-1, :, :]


def upper_planes(value):
    return value[..., 1:, :, :]


def step_planes(value):
    return value[..., 1:, :, :] - value[..., :-1, :, :]


def back_planes(value):
    return value[..., :-1, :, :] - value[..., 1:, :, :]


def curl_curl(padded, inside):
    shape = padded.shape
    planes = shape[-3]
    split = padded.reshape(shape[:-4] + (2, 3) + shape[-3:])
    field_x = split[..., 0, :, :, :]
    field_y = split[..., 1, :, :, :]
    field_z = split[..., 2, :, :, :]
    front = inside[:-1][:, None, None]
    curl_x = (
        ahead_rows(lower_planes(field_z))
        - lower_planes(field_z)
        - (ahead_depth(lower_planes(field_y)) - lower_planes(field_y))
    )
    curl_y = ahead_depth(lower_planes(field_x)) - lower_planes(field_x) - step_planes(field_z)
    curl_z = step_planes(field_y) - (ahead_rows(lower_planes(field_x)) - lower_planes(field_x))
    curl_x = curl_x * front
    curl_y = curl_y * front
    curl_z = curl_z * front
    out_x = behind_depth(upper_planes(curl_y)) - behind_rows(upper_planes(curl_z))
    out_y = back_planes(curl_z) - behind_depth(upper_planes(curl_x))
    out_z = behind_rows(upper_planes(curl_x)) - back_planes(curl_y)
    stacked = jnp.stack([out_x, out_y, out_z], axis=-4)
    return stacked.reshape(shape[:-4] + (6, planes - 2) + shape[-2:])


def sweep(padded, source, mass_real, mass_imag, inside, weight):
    image = curl_curl(padded, inside)
    center = padded[..., 1:-1, :, :]
    real_part = center[..., 0:3, :, :, :]
    imag_part = center[..., 3:6, :, :, :]
    applied = jnp.concatenate(
        [
            image[..., 0:3, :, :, :] + mass_real * real_part - mass_imag * imag_part,
            image[..., 3:6, :, :, :] + mass_real * imag_part + mass_imag * real_part,
        ],
        axis=-4,
    )
    residual = source - applied
    diagonal = 4.0 + mass_real
    return (center + weight * residual / diagonal) * inside[1:-1][:, None, None]


def edge_parts(adjoint, saved):
    saved_wide = saved.astype(jnp.float32)
    moment = (
        saved_wide[..., 0:3, :, :, :] * adjoint[..., 3:6, :, :, :]
        + saved_wide[..., 3:6, :, :, :] * adjoint[..., 0:3, :, :, :]
    )
    moment_x = moment[..., 0, :, :, :]
    moment_y = moment[..., 1, :, :, :]
    moment_z = moment[..., 2, :, :, :]
    part_x = moment_x + ahead_depth(moment_x)
    part_x = part_x + ahead_rows(part_x)
    part_y = moment_y + ahead_depth(moment_y)
    part_z = moment_z + ahead_rows(moment_z)
    return (part_x, part_y, part_z)


def transposed_smooth(summed, rough):
    rows_in = summed.shape[-2]
    depth_in = summed.shape[-1]
    total = jnp.zeros_like(summed)
    for vertical in range(3):
        for lateral in range(3):
            product = rough[vertical * 3 + lateral] * summed
            padded = jnp.pad(product, ((0, 0), (1, 1), (1, 1)))
            total = (
                total
                + padded[
                    :, 2 - vertical : 2 - vertical + rows_in, 2 - lateral : 2 - lateral + depth_in
                ]
            )
    return total


def inside_mask(first, margin, planes, whole):
    position = first - margin + lax.iota(jnp.int32, planes + 2 * margin)
    return ((position >= 0) & (position < whole)).astype(jnp.float32)


def shards(adjoint_source, forward_field, medium, plane_map, depth, rough):
    planes = adjoint_source.shape[2]
    rows_all = adjoint_source.shape[3]
    depth_all = adjoint_source.shape[4]
    count = lax.axis_size("space")
    index = lax.axis_index("space")
    first = index * planes
    whole = planes * count
    margin = SWEEPS - 1
    joined = jnp.concatenate([adjoint_source, medium[None]], axis=1)
    widened = padded_2(joined, (("space", 2),), margin)
    source_wide = widened[:, 0:6]
    real_wide = widened[:, 6:7]
    imag_wide = widened[:, 7:8]
    inside_wide = inside_mask(first, margin, planes, whole)
    extent = planes + 2 * margin
    adjoint = sweep_steps[0] * source_wide / (4.0 + real_wide)
    for sweep_index in range(1, SWEEPS):
        stop = extent - sweep_index
        adjoint = sweep(
            adjoint,
            source_wide[:, :, sweep_index:stop],
            real_wide[:, :, sweep_index:stop],
            imag_wide[:, :, sweep_index:stop],
            inside_wide[sweep_index - 1 : stop + 1],
            sweep_steps[sweep_index],
        )
    part_x, part_y, part_z = edge_parts(adjoint, forward_field)
    next_y, next_z = shifted((part_y[..., :1, :, :], part_z[..., :1, :, :]), "space", -1)
    shifted_y = jnp.concatenate([part_y[..., 1:, :, :], next_y], axis=-3)
    shifted_z = jnp.concatenate([part_z[..., 1:, :, :], next_z], axis=-3)
    cell = 0.25 * (part_x + (part_y + shifted_y) + (part_z + shifted_z))
    keep = (lax.iota(jnp.int32, depth_all)[None, None, None, :] < depth[..., None]).astype(
        jnp.float32
    )
    local = jnp.sum(cell * keep, axis=0)
    offsets = plane_map - index
    targets = lax.iota(jnp.int32, 2 * REACH + 1) - REACH
    select = (offsets[None] == targets[:, None, None]).astype(jnp.float32)
    window = jnp.einsum("oxy,xyz->oyz", select, local, precision=lax.Precision.HIGHEST)
    window = jnp.sum(window.reshape(2 * REACH + 1, rows_all // 2, 2, depth_all), axis=2)
    owned = window[REACH]
    for offset in range(-REACH, REACH + 1):
        if offset != 0:
            owned = owned + shifted(window[REACH + offset], "space", offset)
    total = lax.psum(owned, "src")
    return transposed_smooth(total[None], rough)


def solution(mesh):
    in_specs = (
        P("src", None, "space", None, None),
        P("src", None, "space", None, None),
        P(None, "space", None, None),
        P("space", None),
        P("src", "space", None),
        P(None, "space", None, None),
    )
    out_specs = P("space", None, None)
    return jax.shard_map(shards, mesh=mesh, in_specs=in_specs, out_specs=out_specs, check_vma=False)
```

profile of v0, /device:TPU:8, one launch (start us, length us, event | category | flops | bytes accessed | tf_op | source)
XLA Modules:
  0.0 65.0 jit_solution(6996587929974599519)
XLA Ops:
  0.0 2.4 %fusion.9 = (f32[1,8,3,64,128]{4,3,2,1,0:T(8,128)}, f32[1,8,3,64,128]{4,3,2,1,0:T(8,128)S(1)}) fusion(f32[1,6,4,64,128]{4,3,2,1,0:T(8,128)} %param.6, f32[1,2,4,64,128]{4,3,2,1,0:T(8,128)} %bitcast.181), kind=kLoop, calls=%fused_computation.17 | loop fusion | flops 393216 | bytes 2621440 | tf_op jit(solution)/shard_map/concatenate | solution.py:153
  2.4 2.0 %collective-permute-start = (f32[1,8,3,64,128]{4,3,2,1,0:T(8,128)}, f32[1,8,3,64,128]{4,3,2,1,0:T(8,128)S(1)}, u32[]{:S(2)}, u32[]{:S(2)}) collective-permute-start(f32[1,8,3,64,128]{4,3,2,1,0:T(8,128)} %get-tuple-element.26), channel_id=1, source_target_pairs={{0,1},{1,2},{2,3},{3,4},{4,5},{5,6},{6,7},{7,8},{8,9},{9,10},{10,1... | collective-permute-start | bytes 2359304 | tf_op jit(solution)/shard_map/ppermute | solution.py:20
  4.5 4.5 %collective-permute-start.1 = (f32[1,8,3,64,128]{4,3,2,1,0:T(8,128)S(1)}, f32[1,8,3,64,128]{4,3,2,1,0:T(8,128)S(1)}, u32[]{:S(2)}, u32[]{:S(2)}) collective-permute-start(f32[1,8,3,64,128]{4,3,2,1,0:T(8,128)S(1)} %get-tuple-element.27), channel_id=1, source_target_pairs={{1,0},{2,1},{3,2},{4,3},{5,4},{6,5},{7,6},{8,7},{9,8},{10,9},{11,1... | collective-permute-start | bytes 2359304 | tf_op jit(solution)/shard_map/ppermute | solution.py:21
  9.4 1.1 %convert_element_type.18 = f32[1,6,4,64,128]{4,3,2,1,0:T(8,128)S(1)} convert(bf16[1,6,4,64,128]{4,3,2,1,0:T(8,128)(2,1)} %param.7) | non-fusion elementwise | flops 196608 | bytes 1179648 | tf_op jit(solution)/shard_map/convert_element_type | solution.py:107
  10.5 6.5 %collective-permute-done = f32[1,8,3,64,128]{4,3,2,1,0:T(8,128)S(1)} collective-permute-done((f32[1,8,3,64,128]{4,3,2,1,0:T(8,128)}, f32[1,8,3,64,128]{4,3,2,1,0:T(8,128)S(1)}, u32[]{:S(2)}, u32[]{:S(2)}) %collective-permute-start) | collective-permute-done | bytes 786464 | tf_op jit(solution)/shard_map/ppermute | solution.py:20
  17.1 1.5 %collective-permute-done.1 = f32[1,8,3,64,128]{4,3,2,1,0:T(8,128)S(1)} collective-permute-done((f32[1,8,3,64,128]{4,3,2,1,0:T(8,128)S(1)}, f32[1,8,3,64,128]{4,3,2,1,0:T(8,128)S(1)}, u32[]{:S(2)}, u32[]{:S(2)}) %collective-permute-start.1) | collective-permute-done | bytes 786464 | tf_op jit(solution)/shard_map/ppermute | solution.py:21
  18.8 0.4 fusion
  19.3 0.2 slice.623
  19.7 0.2 slice.638
  19.9 0.6 fusion.18
  20.6 0.5 subtract_bitcast_fusion
  21.4 0.4 fusion.12
  21.9 0.6 fusion.4
  23.1 0.5 fusion.26
  23.7 0.4 subtract_bitcast_fusion.1
  24.3 0.3 fusion.16
  24.6 0.4 fusion.8
  25.5 0.3 fusion.37
  26.0 0.3 subtract_bitcast_fusion.2
  26.5 0.3 fusion.10
  27.3 4.9 %collective-permute-start.2 = (f32[1,1,64,128]{3,2,1,0:T(8,128)S(1)}, f32[1,1,64,128]{3,2,1,0:T(8,128)S(1)}, u32[]{:S(2)}, u32[]{:S(2)}) collective-permute-start(f32[1,1,64,128]{3,2,1,0:T(8,128)S(1)} %slice.711), channel_id=1, source_target_pairs={{1,0},{2,1},{3,2},{4,3},{5,4},{6,5},{7,6},{8,7},{9,8},{10,9},{11,1... | collective-permute-start | bytes 98312 | tf_op jit(solution)/shard_map/ppermute | solution.py:29
  32.2 6.5 %collective-permute-start.3 = (f32[1,1,64,128]{3,2,1,0:T(8,128)S(1)}, f32[1,1,64,128]{3,2,1,0:T(8,128)S(1)}, u32[]{:S(2)}, u32[]{:S(2)}) collective-permute-start(f32[1,1,64,128]{3,2,1,0:T(8,128)S(1)} %slice.715), channel_id=1, source_target_pairs={{1,0},{2,1},{3,2},{4,3},{5,4},{6,5},{7,6},{8,7},{9,8},{10,9},{11,1... | collective-permute-start | bytes 98312 | tf_op jit(solution)/shard_map/ppermute | solution.py:29
  38.9 1.4 %collective-permute-done.3 = f32[1,1,64,128]{3,2,1,0:T(8,128)S(1)} collective-permute-done((f32[1,1,64,128]{3,2,1,0:T(8,128)S(1)}, f32[1,1,64,128]{3,2,1,0:T(8,128)S(1)}, u32[]{:S(2)}, u32[]{:S(2)}) %collective-permute-start.3) | collective-permute-done | bytes 32800 | tf_op jit(solution)/shard_map/ppermute | solution.py:29
  40.4 0.6 bitcast_reduce_fusion
  41.1 1.9 %collective-permute-start.4 = (f32[32,128]{1,0:T(8,128)S(1)}, f32[32,128]{1,0:T(8,128)S(1)}, u32[]{:S(2)}, u32[]{:S(2)}) collective-permute-start(f32[32,128]{1,0:T(8,128)S(1)} %bitcast.195), channel_id=1, source_target_pairs={{2,0},{3,1},{4,2},{5,3},{6,4},{7,5},{8,6},{9,7},{10,8},{11,9},{12,... | collective-permute-start | bytes 49160 | tf_op jit(solution)/shard_map/ppermute | solution.py:29
  43.0 4.5 %collective-permute-start.5 = (f32[32,128]{1,0:T(8,128)S(1)}, f32[32,128]{1,0:T(8,128)S(1)}, u32[]{:S(2)}, u32[]{:S(2)}) collective-permute-start(f32[32,128]{1,0:T(8,128)S(1)} %bitcast.194), channel_id=1, source_target_pairs={{1,0},{2,1},{3,2},{4,3},{5,4},{6,5},{7,6},{8,7},{9,8},{10,9},{11,1... | collective-permute-start | bytes 49160 | tf_op jit(solution)/shard_map/ppermute | solution.py:29
  47.6 2.0 %collective-permute-start.6 = (f32[32,128]{1,0:T(8,128)S(1)}, f32[32,128]{1,0:T(8,128)S(1)}, u32[]{:S(2)}, u32[]{:S(2)}) collective-permute-start(f32[32,128]{1,0:T(8,128)S(1)} %bitcast.193), channel_id=1, source_target_pairs={{0,1},{1,2},{2,3},{3,4},{4,5},{5,6},{6,7},{7,8},{8,9},{9,10},{10,1... | collective-permute-start | bytes 49160 | tf_op jit(solution)/shard_map/ppermute | solution.py:29
  49.6 3.5 %collective-permute-start.7 = (f32[32,128]{1,0:T(8,128)S(1)}, f32[32,128]{1,0:T(8,128)S(1)}, u32[]{:S(2)}, u32[]{:S(2)}) collective-permute-start(f32[32,128]{1,0:T(8,128)S(1)} %bitcast.192), channel_id=1, source_target_pairs={{0,2},{1,3},{2,4},{3,5},{4,6},{5,7},{6,8},{7,9},{8,10},{9,11},{10,... | collective-permute-start | bytes 49160 | tf_op jit(solution)/shard_map/ppermute | solution.py:29
  53.2 0.4 collective-permute-done.6
  53.6 2.6 %collective-permute-done.7 = f32[32,128]{1,0:T(8,128)S(1)} collective-permute-done((f32[32,128]{1,0:T(8,128)S(1)}, f32[32,128]{1,0:T(8,128)S(1)}, u32[]{:S(2)}, u32[]{:S(2)}) %collective-permute-start.7) | collective-permute-done | bytes 16416 | tf_op jit(solution)/shard_map/ppermute | solution.py:29
  56.2 8.1 %psum.7 = f32[32,128]{1,0:T(8,128)S(1)} all-reduce(f32[32,128]{1,0:T(8,128)S(1)} %add_add_fusion), channel_id=1, replica_groups=mesh['src'=2,'space'=16] {'src'}, use_global_device_ids=true, to_apply=%region_1.0 | all-reduce | flops 4096 | bytes 32768 | tf_op jit(solution)/shard_map/psum | solution.py:189
  64.3 0.7 %fusion.64 = f32[1,32,128]{2,1,0:T(8,128)} fusion(f32[1,32,128]{2,1,0:T(8,128)S(1)} %get-tuple-element.62, f32[1,32,128]{2,1,0:T(8,128)S(1)} %get-tuple-element.61, f32[1,32,128]{2,1,0:T(8,128)S(1)} %get-tuple-element.60, f32[1,32,128]{2,1,0:T(8,128)S(1)} %get-tuple-element.59, f32[1,32,128]{2,1,0:T(8,128)S(1)} %get-tuple-element.58, ...), kind=kLoop, calls=%fused_computation.137 | loop fusion | flops 36864 | bytes 180224 | tf_op jit(solution)/shard_map/add | solution.py:131
  (71 shorter events, 3.6 us)
Async XLA Ops:
  0.0 10.5 %copy-start.4 = (s32[4,64]{1,0:T(4,128)S(1)}, s32[4,64]{1,0:T(4,128)}, u32[]{:S(2)}) copy-start(s32[4,64]{1,0:T(4,128)} %param.9) | copy-start | bytes 3076
  0.0 10.5 %copy-start.1 = (f32[2,4,64,128]{3,2,1,0:T(8,128)S(1)}, f32[2,4,64,128]{3,2,1,0:T(8,128)}, u32[]{:S(2)}) copy-start(f32[2,4,64,128]{3,2,1,0:T(8,128)} %param.8) | copy-start | bytes 786436
  2.4 16.1 %copy-start = (f32[1,6,4,64,128]{4,3,2,1,0:T(8,128)S(1)}, f32[1,6,4,64,128]{4,3,2,1,0:T(8,128)}, u32[]{:S(2)}) copy-start(f32[1,6,4,64,128]{4,3,2,1,0:T(8,128)} %param.6) | copy-start | bytes 2359300
  2.4 14.6 %collective-permute-start = (f32[1,8,3,64,128]{4,3,2,1,0:T(8,128)}, f32[1,8,3,64,128]{4,3,2,1,0:T(8,128)S(1)}, u32[]{:S(2)}, u32[]{:S(2)}) collective-permute-start(f32[1,8,3,64,128]{4,3,2,1,0:T(8,128)} %get-tuple-element.26), channel_id=1, source_target_pairs={{0,1},{1,2},{2,3},{3,4},{4,5},{5,6},{6,7},{7,8},{8,9},{9,10},{10,1... | collective-permute-start | bytes 2359304 | tf_op jit(solution)/shard_map/ppermute | solution.py:20
  4.5 14.1 %collective-permute-start.1 = (f32[1,8,3,64,128]{4,3,2,1,0:T(8,128)S(1)}, f32[1,8,3,64,128]{4,3,2,1,0:T(8,128)S(1)}, u32[]{:S(2)}, u32[]{:S(2)}) collective-permute-start(f32[1,8,3,64,128]{4,3,2,1,0:T(8,128)S(1)} %get-tuple-element.27), channel_id=1, source_target_pairs={{1,0},{2,1},{3,2},{4,3},{5,4},{6,5},{7,6},{8,7},{9,8},{10,9},{11,1... | collective-permute-start | bytes 2359304 | tf_op jit(solution)/shard_map/ppermute | solution.py:21
  27.0 13.3 %copy-start.3 = (s32[1,4,64]{2,1,0:T(4,128)S(1)}, s32[1,4,64]{2,1,0:T(4,128)}, u32[]{:S(2)}) copy-start(s32[1,4,64]{2,1,0:T(4,128)} %param.10) | copy-start | bytes 3076
  27.3 37.1 %copy-start.2 = (f32[9,1,32,128]{3,2,1,0:T(8,128)S(1)}, f32[9,1,32,128]{3,2,1,0:T(8,128)}, u32[]{:S(2)}) copy-start(f32[9,1,32,128]{3,2,1,0:T(8,128)} %param.11) | copy-start | bytes 442372
  27.3 11.6 %collective-permute-start.2 = (f32[1,1,64,128]{3,2,1,0:T(8,128)S(1)}, f32[1,1,64,128]{3,2,1,0:T(8,128)S(1)}, u32[]{:S(2)}, u32[]{:S(2)}) collective-permute-start(f32[1,1,64,128]{3,2,1,0:T(8,128)S(1)} %slice.711), channel_id=1, source_target_pairs={{1,0},{2,1},{3,2},{4,3},{5,4},{6,5},{7,6},{8,7},{9,8},{10,9},{11,1... | collective-permute-start | bytes 98312 | tf_op jit(solution)/shard_map/ppermute | solution.py:29
  32.2 8.1 %collective-permute-start.3 = (f32[1,1,64,128]{3,2,1,0:T(8,128)S(1)}, f32[1,1,64,128]{3,2,1,0:T(8,128)S(1)}, u32[]{:S(2)}, u32[]{:S(2)}) collective-permute-start(f32[1,1,64,128]{3,2,1,0:T(8,128)S(1)} %slice.715), channel_id=1, source_target_pairs={{1,0},{2,1},{3,2},{4,3},{5,4},{6,5},{7,6},{8,7},{9,8},{10,9},{11,1... | collective-permute-start | bytes 98312 | tf_op jit(solution)/shard_map/ppermute | solution.py:29
  41.1 12.1 %collective-permute-start.4 = (f32[32,128]{1,0:T(8,128)S(1)}, f32[32,128]{1,0:T(8,128)S(1)}, u32[]{:S(2)}, u32[]{:S(2)}) collective-permute-start(f32[32,128]{1,0:T(8,128)S(1)} %bitcast.195), channel_id=1, source_target_pairs={{2,0},{3,1},{4,2},{5,3},{6,4},{7,5},{8,6},{9,7},{10,8},{11,9},{12,... | collective-permute-start | bytes 49160 | tf_op jit(solution)/shard_map/ppermute | solution.py:29
  43.0 10.1 %collective-permute-start.5 = (f32[32,128]{1,0:T(8,128)S(1)}, f32[32,128]{1,0:T(8,128)S(1)}, u32[]{:S(2)}, u32[]{:S(2)}) collective-permute-start(f32[32,128]{1,0:T(8,128)S(1)} %bitcast.194), channel_id=1, source_target_pairs={{1,0},{2,1},{3,2},{4,3},{5,4},{6,5},{7,6},{8,7},{9,8},{10,9},{11,1... | collective-permute-start | bytes 49160 | tf_op jit(solution)/shard_map/ppermute | solution.py:29
  47.6 6.0 %collective-permute-start.6 = (f32[32,128]{1,0:T(8,128)S(1)}, f32[32,128]{1,0:T(8,128)S(1)}, u32[]{:S(2)}, u32[]{:S(2)}) collective-permute-start(f32[32,128]{1,0:T(8,128)S(1)} %bitcast.193), channel_id=1, source_target_pairs={{0,1},{1,2},{2,3},{3,4},{4,5},{5,6},{6,7},{7,8},{8,9},{9,10},{10,1... | collective-permute-start | bytes 49160 | tf_op jit(solution)/shard_map/ppermute | solution.py:29
  49.6 6.5 %collective-permute-start.7 = (f32[32,128]{1,0:T(8,128)S(1)}, f32[32,128]{1,0:T(8,128)S(1)}, u32[]{:S(2)}, u32[]{:S(2)}) collective-permute-start(f32[32,128]{1,0:T(8,128)S(1)} %bitcast.192), channel_id=1, source_target_pairs={{0,2},{1,3},{2,4},{3,5},{4,6},{5,7},{6,8},{7,9},{8,10},{9,11},{10,... | collective-permute-start | bytes 49160 | tf_op jit(solution)/shard_map/ppermute | solution.py:29
where the time goes:
time: 65.4 us; the launch traced here: 65 us
  starting transfers between devices  30 us (46%)
  waiting for transfers between devices  12.4 us (19%)
  other arithmetic  10.4 us (16%)
  blocking collectives  8.15 us (12%)
  local copies, waits for them, and re-layouts  2.83 us (4%)
    ppermute x6, starting transfers between devices, shifted(): lax.ppermute(value, axis, [(source, source + steps) for source in range(f...  23.4 us
    psum x1, blocking collectives, shards(): total = lax.psum(owned, 'src')  8.15 us
    ppermute x1, waiting for transfers between devices, padded_2(): before = lax.ppermute(last, axis, up)  6.52 us
    ppermute x1, starting transfers between devices, padded_2(): after = lax.ppermute(first, axis, down)  4.54 us
    ppermute x6, waiting for transfers between devices, shifted(): lax.ppermute(value, axis, [(source, source + steps) for source in range(f...  4.38 us
    concatenate x1, other arithmetic, shards(): joined = jnp.concatenate([adjoint_source, medium[None]], axis=1)  2.41 us
    ppermute x1, starting transfers between devices, padded_2(): before = lax.ppermute(last, axis, up)  2.04 us
    another operation x6, other arithmetic, curl_curl(): stacked = jnp.stack([out_x, out_y, out_z], axis=-4)  1.56 us
  transfers between devices with their start and end apart: 8, of which 5 were waited for; matrix products, arithmetic and copies ran while one was open for 2% of the time, Pallas kernels for 0%

commit v1 on v0

v1 whole, which is shorter than its diff:
```python
import functools

import jax
import jax.numpy as jnp
from jax import lax
from jax.experimental import pallas as pl
from jax.experimental.pallas import tpu as pltpu
from jax.sharding import PartitionSpec as P

SWEEPS = 4
REACH = 2

sweep_steps = (0.323, 1.658, 0.422, 0.752)

PAD = 8
ROWS = 16


def lane_of(width):
    return lax.broadcasted_iota(jnp.int32, (ROWS, width), 1)


def ahead(value, lane):
    width = value.shape[-1]
    return jnp.where(lane == width - 1, 0.0, pltpu.roll(value, width - 1, 1))


def behind(value, lane):
    return jnp.where(lane == 0, 0.0, pltpu.roll(value, 1, 1))


def rows_at(ref, index, row, shift=0):
    return ref[index + (pl.ds(PAD + row + shift, ROWS), slice(None))]


def put(ref, index, row, value):
    ref[index + (pl.ds(PAD + row, ROWS), slice(None))] = value


def clear_pads(ref):
    rows = ref.shape[-2]
    lead = ref.shape[:-2]
    zero = jnp.zeros((PAD, ref.shape[-1]), jnp.float32)
    for flat in range(functools.reduce(lambda a, b: a * b, lead, 1)):
        index = []
        rest = flat
        for size in reversed(lead):
            index.insert(0, rest % size)
            rest //= size
        ref[tuple(index) + (pl.ds(0, PAD), slice(None))] = zero
        ref[tuple(index) + (pl.ds(rows - PAD, PAD), slice(None))] = zero


def chunks(total):
    return range(0, total, ROWS)


def curl(field, ahead_of, row, lane):
    out = []
    for part in (0, 3):
        ex, ey, ez = field(part, 0), field(part + 1, 0), field(part + 2, 0)
        hx = (field(part + 2, 1) - ez) - (ahead(ey, lane) - ey)
        hy = (ahead(ex, lane) - ex) - (ahead_of(part + 2) - ez)
        hz = (ahead_of(part + 1) - ey) - (field(part, 1) - ex)
        out += [hx, hy, hz]
    return out


def curl_back(held, before, lane):
    out = []
    for part in (0, 3):
        hx, hy, hz = held(part, 0), held(part + 1, 0), held(part + 2, 0)
        ox = (behind(hy, lane) - hy) - (held(part + 2, -1) - hz)
        oy = (before(part + 2) - hz) - (behind(hx, lane) - hx)
        oz = (held(part, -1) - hx) - (before(part + 1) - hy)
        out += [ox, oy, oz]
    return out


def updated(center, image, source, real, imag, scale):
    out = []
    for c in range(3):
        applied = image[c] + real * center[c] - imag * center[c + 3]
        out.append(center[c] + scale * (source[c] - applied))
    for c in range(3):
        applied = image[c + 3] + real * center[c + 3] + imag * center[c]
        out.append(center[c + 3] + scale * (source[c + 3] - applied))
    return out


def edge_sums(field, lane):
    out = []
    for part in (0, 3):
        ex = field(part, 0)
        out.append(field(part + 1, 0) + (field(part, 1) - ex))
        out.append(field(part + 2, 0) + (ahead(ex, lane) - ex))
    return out


def sweep_slab(state, held, result, source_ref, medium_ref, scale_ref, weight, low, high, first_scale, planes, rows, lane, wanted=None):
    wanted = range(planes) if wanted is None else wanted
    needed = sorted({i for w in wanted for i in (w - 1, w)})
    for i in needed:
        for row in chunks(rows):
            if i < 0:
                for part in (0, 3):
                    gy, gz = low(part, row)
                    ey, ez = rows_at(state, (part + 1, 0), row), rows_at(state, (part + 2, 0), row)
                    put(held, (part + 1, 0), row, first_scale * (gz - ez))
                    put(held, (part + 2, 0), row, first_scale * (ey - gy))
                continue

            def ahead_of(c, i=i, row=row):
                if i + 1 < planes:
                    return rows_at(state, (c, i + 1), row)
                return high(c, row)

            values = curl(lambda c, s: rows_at(state, (c, i), row, s), ahead_of, row, lane)
            for c in range(6):
                put(held, (c, i + 1), row, values[c])
    for i in wanted:
        for row in chunks(rows):
            image = curl_back(
                lambda c, s: rows_at(held, (c, i + 1), row, s), lambda c: rows_at(held, (c, i), row), lane
            )
            here = pl.ds(row, ROWS)
            new = updated(
                [rows_at(state, (c, i), row) for c in range(6)],
                image,
                [source_ref[0, c, i, here, :] for c in range(6)],
                medium_ref[0, i, here, :],
                medium_ref[1, i, here, :],
                weight * scale_ref[i, here, :],
            )
            for c in range(6):
                put(result, (c, i), row, new[c])


def first_sweep(source_ref, medium_ref, scale_ref, state, planes, rows):
    for i in range(planes):
        for row in chunks(rows):
            here = pl.ds(row, ROWS)
            scale = 1.0 / (4.0 + medium_ref[0, i, here, :])
            scale_ref[i, here, :] = scale
            for c in range(6):
                put(state, (c, i), row, sweep_steps[0] * source_ref[0, c, i, here, :] * scale)


def send_kernel(source_ref, medium_ref, meta_ref, pair_ref, chip_ref, scale_ref, one, two, held):
    planes, rows, width = medium_ref.shape[1:]
    lane = lane_of(width)
    index = lax.axis_index("space")
    odd = lax.rem(index, 2) == 1
    first_scale = jnp.where(index == 0, 0.0, 1.0)
    for ref in (one, two, held):
        clear_pads(ref)
    first_sweep(source_ref, medium_ref, scale_ref, one, planes, rows)

    def emit(slot, row, below, above):
        here = pl.ds(slot * rows + row, ROWS)
        pair_ref[here, :] = jnp.where(odd, below, above)
        chip_ref[here, :] = jnp.where(odd, above, below)

    def emit_level(level, state):
        for row in chunks(rows):
            sums = edge_sums(lambda c, s: rows_at(state, (c, planes - 1), row, s), lane)
            bottom = [rows_at(state, (c, 0), row) for c in (1, 2, 4, 5)]
            for k in range(4):
                emit(4 * level + k, row, bottom[k], sums[k])

    def zero(c, row):
        return 0.0

    def zeros(part, row):
        return 0.0, 0.0

    emit_level(0, one)
    for row in chunks(rows):
        here = pl.ds(row, ROWS)
        for k in range(2):
            emit(12 + k, row, medium_ref[k, 0, here, :], medium_ref[k, planes - 1, here, :])
    meta = pl.ds(14 * rows, 8)
    pair_ref[meta, :] = meta_ref[...]
    chip_ref[meta, :] = meta_ref[...]
    sweep_slab(one, held, two, source_ref, medium_ref, scale_ref, sweep_steps[1], zeros, zero, first_scale, planes, rows, lane)
    emit_level(1, two)
    sweep_slab(
        two, held, one, source_ref, medium_ref, scale_ref, sweep_steps[2], zeros, zero, first_scale, planes, rows, lane,
        wanted=sorted({0, planes - 1}),
    )
    emit_level(2, one)


def window_kernel(
    source_ref, medium_ref, saved_ref, keep_ref, offset_ref, edge_ref, pair_ref, chip_ref,
    send_ref, stay_ref, scale_ref, one, two, held, delta_low, delta_high, delta_two, window, moment,
):
    planes, rows, width = medium_ref.shape[1:]
    lane = lane_of(width)
    index = lax.axis_index("space")
    odd = lax.rem(index, 2) == 1
    first_scale = jnp.where(index == 0, 0.0, 1.0)
    last_scale = jnp.where(index == lax.axis_size("space") - 1, 0.0, 1.0)
    for ref in (one, two, held, delta_low, delta_high, moment):
        clear_pads(ref)
    first_sweep(source_ref, medium_ref, scale_ref, one, planes, rows)

    def from_below(slot, row):
        here = pl.ds(slot * rows + row, ROWS)
        return jnp.where(odd, pair_ref[here, :], chip_ref[here, :])

    def from_above(slot, row):
        here = pl.ds(slot * rows + row, ROWS)
        return jnp.where(odd, chip_ref[here, :], pair_ref[here, :])

    for row in chunks(rows):
        sums = edge_sums(lambda c, s: rows_at(one, (c, planes - 1), row, s), lane)
        scale = (sweep_steps[1] * last_scale) / (4.0 + from_above(12, row))
        for k, c in enumerate((1, 2, 4, 5)):
            put(delta_high, (c,), row, scale * sums[k])
        scale = sweep_steps[1] / (4.0 + from_below(12, row))
        for part in (0, 3):
            ey, ez = rows_at(one, (part + 1, 0), row), rows_at(one, (part + 2, 0), row)
            put(delta_low, (part + 1,), row, scale * ey)
            put(delta_low, (part + 2,), row, scale * ez)
            put(delta_low, (part,), row, scale * ((behind(ez, lane) - ez) + (rows_at(one, (part + 1, 0), row, -1) - ey)))

    where_yz = {1: 0, 2: 1, 4: 2, 5: 3}
    sweep_slab(
        one, held, two, source_ref, medium_ref, scale_ref, sweep_steps[1],
        lambda part, row: (from_below(2 * (part // 3), row), from_below(2 * (part // 3) + 1, row)),
        lambda c, row: from_above(where_yz[c], row),
        first_scale, planes, rows, lane,
    )

    none = [0.0] * 6
    for row in chunks(rows):
        values = curl(
            lambda c, s: rows_at(delta_low, (c,), row, s), lambda c: rows_at(two, (c, 0), row), row, lane
        )
        for c in range(6):
            put(held, (c, 0), row, values[c])
    for row in chunks(rows):
        before = {1: -rows_at(delta_low, (2,), row), 2: rows_at(delta_low, (1,), row),
                  4: -rows_at(delta_low, (5,), row), 5: rows_at(delta_low, (4,), row)}
        image = curl_back(lambda c, s: rows_at(held, (c, 0), row, s), lambda c: before[c], lane)
        real, imag = from_below(12, row), from_below(13, row)
        new = updated(
            [rows_at(delta_low, (c,), row) for c in range(6)], image, none, real, imag, sweep_steps[2] / (4.0 + real)
        )
        for c in range(6):
            put(delta_two, (c,), row, new[c])
    for row in chunks(rows):
        for part in (0, 3):
            ey, ez = rows_at(delta_high, (part + 1,), row), rows_at(delta_high, (part + 2,), row)
            put(held, (part, 1), row, (rows_at(delta_high, (part + 2,), row, 1) - ez) - (ahead(ey, lane) - ey))
    for row in chunks(rows):
        sums = edge_sums(lambda c, s: rows_at(two, (c, planes - 1), row, s), lane)
        real, imag = from_above(12, row), from_above(13, row)
        scale = (sweep_steps[2] * last_scale) / (4.0 + real)
        center, image = {}, {}
        for part in (0, 3):
            ey, ez = rows_at(delta_high, (part + 1,), row), rows_at(delta_high, (part + 2,), row)
            hx = rows_at(held, (part, 1), row)
            k = 2 * (part // 3)
            center[part + 1], center[part + 2] = ey, ez
            image[part + 1] = 2.0 * ey - sums[k] - (behind(hx, lane) - hx)
            image[part + 2] = (rows_at(held, (part, 1), row, -1) - hx) - sums[k + 1] + 2.0 * ez
        for k, c in enumerate((1, 2)):
            value = center[c] - scale * (image[c] + real * center[c] - imag * center[c + 3])
            delta_two[6 + k, pl.ds(PAD + row, ROWS), :] = value
            value = center[c + 3] - scale * (image[c + 3] + real * center[c + 3] + imag * center[c])
            delta_two[8 + k, pl.ds(PAD + row, ROWS), :] = value

    def low_of(level, deltas):
        def low(part, row):
            k = 4 * level + 2 * (part // 3)
            ex = rows_at(deltas, (part,), row)
            gy = from_below(k, row) + rows_at(deltas, (part + 1,), row) + (rows_at(deltas, (part,), row, 1) - ex)
            gz = from_below(k + 1, row) + rows_at(deltas, (part + 2,), row) + (ahead(ex, lane) - ex)
            return gy, gz
        return low

    sweep_slab(
        two, held, one, source_ref, medium_ref, scale_ref, sweep_steps[2],
        low_of(1, delta_low),
        lambda c, row: from_above(4 + where_yz[c], row) + rows_at(delta_high, (c,), row),
        first_scale, planes, rows, lane,
    )
    for c in range(6):
        delta_two[c, pl.ds(PAD + rows, PAD), :] = jnp.zeros((PAD, width), jnp.float32)
    sweep_slab(
        one, held, two, source_ref, medium_ref, scale_ref, sweep_steps[3],
        low_of(2, delta_two),
        lambda c, row: from_above(8 + where_yz[c], row) + rows_at(delta_two, (6 + where_yz[c],), row),
        first_scale, planes, rows, lane,
    )

    for i in range(planes):
        for row in chunks(rows):
            here = pl.ds(row, ROWS)
            for c in range(3):
                real = saved_ref[0, c, i, here, :].astype(jnp.float32)
                imag = saved_ref[0, c + 3, i, here, :].astype(jnp.float32)
                value = real * rows_at(two, (c + 3, i), row) + imag * rows_at(two, (c, i), row)
                if c < 2:
                    value = value + ahead(value, lane)
                put(moment, (c, i), row, value)
    for row in chunks(rows):
        here = pl.ds(row, ROWS)
        sums = [0.0] * (2 * REACH + 2)

        def add(value, offset, low):
            for k in range(2 * REACH + 1):
                slot = k + low
                sums[slot] = sums[slot] + jnp.where(offset == float(slot - REACH - 1), value, 0.0)

        def side(i):
            return rows_at(moment, (1, i), row) + (rows_at(moment, (2, i), row) + rows_at(moment, (2, i), row, 1))

        lower = side(0)
        add(edge_ref[0, here, :] * lower, edge_ref[1, here, :], 0)
        for i in range(planes):
            cell = rows_at(moment, (0, i), row) + rows_at(moment, (0, i), row, 1) + lower
            if i + 1 < planes:
                lower = side(i + 1)
                cell = cell + lower
            add(keep_ref[i, here, :] * cell, offset_ref[i, here, :], 1)
        for k in range(2 * REACH + 2):
            window[k, here, :] = sums[k]
    for k in range(2 * REACH + 2):
        both = window[k, pl.ds(0, rows // 2, stride=2), :] + window[k, pl.ds(1, rows // 2, stride=2), :]
        if k % 2 == 0:
            send_ref[k // 2] = both
        else:
            stay_ref[k // 2] = both


def vmem():
    return pl.BlockSpec(memory_space=pltpu.VMEM)


def call(kernel, out_shape, scratch, arguments, name):
    return pl.pallas_call(
        kernel,
        out_shape=[jax.ShapeDtypeStruct(s, jnp.float32) for s in out_shape],
        in_specs=[vmem()] * len(arguments),
        out_specs=[vmem()] * len(out_shape),
        scratch_shapes=[pltpu.VMEM(s, jnp.float32) for s in scratch],
        compiler_params=pltpu.CompilerParams(vmem_limit_bytes=24 << 20),
        name=name,
    )(*arguments)


def core_swap(value):
    size = lax.axis_size("space")
    return lax.ppermute(value, "space", [(i, i ^ 1) for i in range(size)])


def chip_swap(value):
    size = lax.axis_size("space")
    pairs = []
    for i in range(1, size - 1, 2):
        pairs += [(i, i + 1), (i + 1, i)]
    return lax.ppermute(value, "space", pairs)


def sum_over_groups(value):
    size = lax.axis_size("src")
    if size & (size - 1):
        return lax.psum(value, "src")
    step = 1
    while step < size:
        value = value + lax.ppermute(value, "src", [(i, i ^ step) for i in range(size)])
        step *= 2
    return value


def gather_owned(send, stay):
    size = lax.axis_size("space")
    index = lax.axis_index("space")
    odd = lax.rem(index, 2) == 1
    other = core_swap(send)
    far = jnp.where(odd, other[0], 0.0)
    below = stay[0] + jnp.where(odd, other[1], other[0])
    here = stay[1] + jnp.where(odd, other[2], other[1])
    above = stay[2] + jnp.where(odd, 0.0, other[2])
    chip = index // 2
    upward = lax.rem(chip, 2) == 0
    chips = size // 2
    inner, outer = [], []
    for c in range(chips):
        for core in range(2):
            if c ^ 1 < chips:
                inner.append((2 * c + core, 2 * (c ^ 1) + core))
            partner = ((c + 1) ^ 1) - 1
            if 0 <= partner < chips:
                outer.append((2 * c + core, 2 * partner + core))
    from_outer = lax.ppermute(jnp.where(upward, below, above), "space", outer)
    from_inner = lax.ppermute(jnp.where(upward, above, below), "space", inner)
    from_far = lax.ppermute(far, "space", [(i, i - 4) for i in range(5, size, 2)])
    return here + from_outer + from_inner + from_far


def transposed_smooth(summed, rough):
    rows_in = summed.shape[-2]
    depth_in = summed.shape[-1]
    total = jnp.zeros_like(summed)
    for vertical in range(3):
        for lateral in range(3):
            product = rough[vertical * 3 + lateral] * summed
            padded = jnp.pad(product, ((0, 0), (1, 1), (1, 1)))
            total = (
                total
                + padded[
                    :, 2 - vertical : 2 - vertical + rows_in, 2 - lateral : 2 - lateral + depth_in
                ]
            )
    return total


def shards(adjoint_source, forward_field, medium, plane_map, depth, rough):
    planes, rows, width = medium.shape[1:]
    index = lax.axis_index("space")
    levels = depth[0].astype(jnp.float32)
    owners = plane_map.astype(jnp.float32)
    meta = jnp.zeros((8, width), jnp.float32)
    meta = meta.at[0, :rows].set(levels[planes - 1]).at[1, :rows].set(owners[planes - 1])
    state = (6, planes, rows + 2 * PAD, width)
    held = (6, planes + 1, rows + 2 * PAD, width)
    message = (14 * rows + 8, width)
    pair, chip = call(
        send_kernel,
        [message, message],
        [(planes, rows, width), state, state, held],
        (adjoint_source, medium, meta),
        "send",
    )
    chip = chip_swap(chip)
    pair = core_swap(pair)
    here = index.astype(jnp.float32)
    position = lax.broadcasted_iota(jnp.int32, (planes, rows, width), 2).astype(jnp.float32)
    keep = jnp.where(position < levels[:, :, None], 0.25, 0.0)
    offset = jnp.broadcast_to((owners - here)[:, :, None], (planes, rows, width))
    below = jnp.where(lax.rem(index, 2) == 1, pair[14 * rows :], chip[14 * rows :])
    edge = jnp.stack(
        [
            jnp.where(position[0] < below[0, :rows, None], 0.25, 0.0),
            jnp.broadcast_to((below[1, :rows] - here)[:, None], (rows, width)),
        ]
    )
    plane = (rows + 2 * PAD, width)
    send, stay = call(
        window_kernel,
        [(REACH + 1, rows // 2, width), (REACH + 1, rows // 2, width)],
        [
            (planes, rows, width), state, state, held, (6,) + plane, (6,) + plane, (10,) + plane,
            (2 * REACH + 2, rows, width), (3, planes) + plane,
        ],
        (adjoint_source, medium, forward_field, keep, offset, edge, pair, chip),
        "window",
    )
    total = sum_over_groups(gather_owned(send, stay))
    return transposed_smooth(total[None], rough)


def solution(mesh):
    in_specs = (
        P("src", None, "space", None, None),
        P("src", None, "space", None, None),
        P(None, "space", None, None),
        P("space", None),
        P("src", "space", None),
        P(None, "space", None, None),
    )
    out_specs = P("space", None, None)
    return jax.shard_map(shards, mesh=mesh, in_specs=in_specs, out_specs=out_specs, check_vma=False)
```

time: 65.4 us -> 37 us (0.57)
  starting transfers between devices: 30 us -> 13.6 us
  other arithmetic: 10.4 us -> 1.64 us
  blocking collectives: 8.15 us -> 0 us
  Pallas kernels: 0 us -> 3.16 us
  waiting for transfers between devices: 12.4 us -> 15 us
    ppermute x8 -> x7, starting transfers between devices: 30 us -> 13.6 us  [the longest x2 4.58 us: core_swap(): return lax.ppermute(value, 'space', [(i, i ^ 1) for i in range(size)])]
    psum x1 -> x0, blocking collectives: 8.15 us -> none  [shards(): total = lax.psum(owned, 'src')]
    pallas_call x0 -> x2, Pallas kernels: none -> 3.16 us  [call(): pl.pallas_call(kernel, out_shape=[jax.ShapeDtypeStruct(s, jnp.float32) fo...]
    mul x6 -> x0, other arithmetic: 2.77 us -> none  [the longest x3 1.41 us: curl_curl(): curl_z = curl_z * front]
    unnamed x10 -> x14, local copies, waits for them, and re-layouts: 0.02 us -> 2.77 us
    ppermute x8 -> x7, waiting for transfers between devices: 12.4 us -> 15 us  [the longest x1 7.28 us: chip_swap(): return lax.ppermute(value, 'space', pairs)]
    concatenate x2 -> x0, other arithmetic: 2.59 us -> none  [the longest x1 2.41 us: shards(): joined = jnp.concatenate([adjoint_source, medium[None]], axis=1)]
    slice x38 -> x2, local copies, waits for them, and re-layouts: 2.35 us -> 0.01 us  [the longest x1 0.01 us: shards(): owners[planes - 1]]
  transfers between devices with their start and end apart: 8 -> 7, of which waited for: 5 -> 4; matrix products, arithmetic and copies ran while one was open for 2% -> 0% of each run, Pallas kernels for 0% -> 0%
where the time goes in v1:
time: 37 us; the launch traced here: 36.7 us
  waiting for transfers between devices  15 us (41%)
  starting transfers between devices  13.6 us (37%)
  Pallas kernels  3.16 us (9%)
  local copies, waits for them, and re-layouts  3.13 us (8%)
  other arithmetic  1.64 us (4%)
    ppermute x1, waiting for transfers between devices, chip_swap(): return lax.ppermute(value, 'space', pairs)  7.28 us
    ppermute x1, waiting for transfers between devices, gather_owned(): from_outer = lax.ppermute(jnp.where(upward, below, above), 'space', outer)  4.58 us
    ppermute x2, starting transfers between devices, core_swap(): return lax.ppermute(value, 'space', [(i, i ^ 1) for i in range(size)])  4.58 us
    ppermute x1, starting transfers between devices, chip_swap(): return lax.ppermute(value, 'space', pairs)  3.4 us
    pallas_call x2, Pallas kernels, call(): pl.pallas_call(kernel, out_shape=[jax.ShapeDtypeStruct(s, jnp.float32) fo...  3.16 us
    unnamed x14, local copies, waits for them, and re-layouts  2.77 us
    ppermute x1, waiting for transfers between devices, sum_over_groups(): lax.ppermute(value, 'src', [(i, i ^ step) for i in range(size)])  2.25 us
    ppermute x1, starting transfers between devices, gather_owned(): from_outer = lax.ppermute(jnp.where(upward, below, above), 'space', outer)  1.92 us
  transfers between devices with their start and end apart: 7, of which 4 were waited for; matrix products, arithmetic and copies ran while one was open for 0% of the time, Pallas kernels for 0%

profile of v1, /device:TPU:8, one launch (start us, length us, event | category | flops | bytes accessed | tf_op | source)
XLA Modules:
  0.0 36.7 jit_solution(4776772397982333682)
XLA Ops:
  0.0 0.7 %fusion.18 = (f32[1,4,64]{2,1,0:T(4,128)S(1)}, f32[4,64]{1,0:T(4,128)S(1)}) fusion(s32[1,4,64]{2,1,0:T(4,128)} %param.14), kind=kLoop, calls=%fused_computation.51 | loop fusion | flops 256 | bytes 3072 | tf_op jit(solution)/shard_map/convert_element_type | solution.py:425
  0.7 0.7 %copy-done.6 = s32[4,64]{1,0:T(4,128)S(1)} copy-done((s32[4,64]{1,0:T(4,128)S(1)}, s32[4,64]{1,0:T(4,128)}, u32[]{:S(2)}) %copy-start.6) | copy-done | bytes 1048
  1.4 0.2 scatter.9.meta_ref
  1.6 0.0 copy-start
  1.6 1.1 %copy-done = f32[1,6,4,64,128]{4,3,2,1,0:T(8,128)S(1)} copy-done((f32[1,6,4,64,128]{4,3,2,1,0:T(8,128)S(1)}, f32[1,6,4,64,128]{4,3,2,1,0:T(8,128)}, u32[]{:S(2)}) %copy-start) | copy-done | bytes 786456
  2.7 0.9 %copy-done.2 = f32[2,4,64,128]{3,2,1,0:T(8,128)S(1)} copy-done((f32[2,4,64,128]{3,2,1,0:T(8,128)S(1)}, f32[2,4,64,128]{3,2,1,0:T(8,128)}, u32[]{:S(2)}) %copy-start.2) | copy-done | bytes 262168
  3.7 0.9 %send.1 = (f32[904,128]{1,0:T(8,128)S(1)}, f32[904,128]{1,0:T(8,128)S(1)}) custom-call(f32[1,6,4,64,128]{4,3,2,1,0:T(8,128)S(1)} %copy-done, f32[2,4,64,128]{3,2,1,0:T(8,128)S(1)} %copy-done.2, f32[8,128]{1,0:T(8,128)S(1)} %scatter.9.meta_ref), custom_call_target="tpu_custom_call" | custom-call | tf_op jit(solution)/shard_map/send/pallas_call | solution.py:344
  4.6 0.0 copy-start.3
  4.6 0.1 collective-permute-start
  4.7 3.4 %collective-permute-start.1 = (f32[904,128]{1,0:T(8,128)S(1)}, f32[904,128]{1,0:T(8,128)S(1)}, u32[]{:S(2)}, u32[]{:S(2)}) collective-permute-start(f32[904,128]{1,0:T(8,128)S(1)} %get-tuple-element.34), channel_id=1, source_target_pairs={{1,2},{2,1},{3,4},{4,3},{5,6},{6,5},{7,8},{8,7},{9,10},{10,9},{11,... | collective-permute-start | bytes 1388552 | tf_op jit(solution)/shard_map/ppermute | solution.py:365
  8.1 0.1 compare_select_fusion.keep_ref
  8.3 0.0 collective-permute-done.pair_ref
  8.3 7.3 %collective-permute-done.1.chip_ref = f32[904,128]{1,0:T(8,128)S(1)} collective-permute-done((f32[904,128]{1,0:T(8,128)S(1)}, f32[904,128]{1,0:T(8,128)S(1)}, u32[]{:S(2)}, u32[]{:S(2)}) %collective-permute-start.1) | collective-permute-done | bytes 462880 | tf_op jit(solution)/shard_map/ppermute | solution.py:365
  15.6 0.1 compare_select_fusion.1
  15.6 0.1 stack_broadcast_in_dim.2
  15.7 0.1 broadcast_in_dim.34.offset_ref
  15.8 0.0 copy-done.1
  15.8 0.0 copy-done.4
  15.8 0.0 copy-done.3
  15.8 2.2 %window.1 = (f32[3,32,128]{2,1,0:T(8,128)S(1)}, f32[3,32,128]{2,1,0:T(8,128)S(1)}) custom-call(f32[1,6,4,64,128]{4,3,2,1,0:T(8,128)S(1)} %copy-done.1, f32[2,4,64,128]{3,2,1,0:T(8,128)S(1)} %copy-done.3, bf16[1,6,4,64,128]{4,3,2,1,0:T(8,128)(2,1)S(1)} %copy-done.4, f32[4,64,128]{2,1,0:T(8,128)S(1)} %compare_select_fusion.keep_ref, ...), custom_call_target="tpu_custom_call" | custom-call | tf_op jit(solution)/shard_map/window/pallas_call | solution.py:344
  18.1 4.5 %collective-permute-start.2 = (f32[3,32,128]{2,1,0:T(8,128)S(1)}, f32[3,32,128]{2,1,0:T(8,128)S(1)}, u32[]{:S(2)}, u32[]{:S(2)}) collective-permute-start(f32[3,32,128]{2,1,0:T(8,128)S(1)} %get-tuple-element.36), channel_id=1, source_target_pairs={{0,1},{1,0},{2,3},{3,2},{4,5},{5,4},{6,7},{7,6},{8,9},{9,8},{10,11... | collective-permute-start | bytes 147464 | tf_op jit(solution)/shard_map/ppermute | solution.py:357
  22.6 0.9 %collective-permute-done.2 = f32[3,32,128]{2,1,0:T(8,128)S(1)} collective-permute-done((f32[3,32,128]{2,1,0:T(8,128)S(1)}, f32[3,32,128]{2,1,0:T(8,128)S(1)}, u32[]{:S(2)}, u32[]{:S(2)}) %collective-permute-start.2) | collective-permute-done | bytes 49184 | tf_op jit(solution)/shard_map/ppermute | solution.py:357
  23.5 1.4 %collective-permute-start.4 = (f32[32,128]{1,0:T(8,128)S(1)}, f32[32,128]{1,0:T(8,128)S(1)}, u32[]{:S(2)}, u32[]{:S(2)}) collective-permute-start(f32[32,128]{1,0:T(8,128)S(1)} %get-tuple-element.48), channel_id=1, source_target_pairs={{0,2},{1,3},{2,0},{3,1},{4,6},{5,7},{6,4},{7,5},{8,10},{9,11},{10,... | collective-permute-start | bytes 49160 | tf_op jit(solution)/shard_map/ppermute | solution.py:400
  24.9 0.7 %collective-permute-start.5 = (f32[32,128]{1,0:T(8,128)S(1)}, f32[32,128]{1,0:T(8,128)S(1)}, u32[]{:S(2)}, u32[]{:S(2)}) collective-permute-start(f32[32,128]{1,0:T(8,128)S(1)} %get-tuple-element.49), channel_id=1, source_target_pairs={{5,1},{7,3},{9,5},{11,7},{13,9},{15,11},{21,17},{23,19},{25,21},{2... | collective-permute-start | bytes 49160 | tf_op jit(solution)/shard_map/ppermute | solution.py:401
  25.6 1.9 %collective-permute-start.3 = (f32[32,128]{1,0:T(8,128)S(1)}, f32[32,128]{1,0:T(8,128)S(1)}, u32[]{:S(2)}, u32[]{:S(2)}) collective-permute-start(f32[32,128]{1,0:T(8,128)S(1)} %get-tuple-element.39), channel_id=1, source_target_pairs={{2,4},{3,5},{4,2},{5,3},{6,8},{7,9},{8,6},{9,7},{10,12},{11,13},{1... | collective-permute-start | bytes 49160 | tf_op jit(solution)/shard_map/ppermute | solution.py:399
  27.5 0.0 collective-permute-done.4
  27.5 0.0 collective-permute-done.5
  27.6 4.6 %collective-permute-done.3 = f32[32,128]{1,0:T(8,128)S(1)} collective-permute-done((f32[32,128]{1,0:T(8,128)S(1)}, f32[32,128]{1,0:T(8,128)S(1)}, u32[]{:S(2)}, u32[]{:S(2)}) %collective-permute-start.3) | collective-permute-done | bytes 16416 | tf_op jit(solution)/shard_map/ppermute | solution.py:399
  32.1 1.6 %collective-permute-start.6 = (f32[32,128]{1,0:T(8,128)S(1)}, f32[32,128]{1,0:T(8,128)S(1)}, u32[]{:S(2)}, u32[]{:S(2)}) collective-permute-start(f32[32,128]{1,0:T(8,128)S(1)} %fusion.16), channel_id=1, source_target_pairs={{0,16},{16,0},{1,17},{17,1},{2,18},{18,2},{3,19},{19,3},{4,20},{20... | collective-permute-start | bytes 49160 | tf_op jit(solution)/shard_map/ppermute | solution.py:374
  33.7 2.2 %collective-permute-done.6 = f32[32,128]{1,0:T(8,128)S(1)} collective-permute-done((f32[32,128]{1,0:T(8,128)S(1)}, f32[32,128]{1,0:T(8,128)S(1)}, u32[]{:S(2)}, u32[]{:S(2)}) %collective-permute-start.6) | collective-permute-done | bytes 16416 | tf_op jit(solution)/shard_map/ppermute | solution.py:374
  36.0 0.0 copy-done.5
  36.0 0.7 %fusion.7 = f32[1,32,128]{2,1,0:T(8,128)} fusion(f32[1,32,128]{2,1,0:T(8,128)S(1)} %get-tuple-element.47, f32[1,32,128]{2,1,0:T(8,128)S(1)} %get-tuple-element.46, f32[1,32,128]{2,1,0:T(8,128)S(1)} %get-tuple-element.45, f32[1,32,128]{2,1,0:T(8,128)S(1)} %get-tuple-element.44, f32[1,32,128]{2,1,0:T(8,128)S(1)} %get-tuple-element.43, ...), kind=kLoop, calls=%fused_computation.18 | loop fusion | flops 36864 | bytes 180224 | tf_op jit(solution)/shard_map/add | solution.py:414
  (19 shorter events, 0.1 us)
Async XLA Ops:
  0.7 0.7 %copy-start.6 = (s32[4,64]{1,0:T(4,128)S(1)}, s32[4,64]{1,0:T(4,128)}, u32[]{:S(2)}) copy-start(s32[4,64]{1,0:T(4,128)} %param.13) | copy-start | bytes 3076
  1.6 1.1 %copy-start = (f32[1,6,4,64,128]{4,3,2,1,0:T(8,128)S(1)}, f32[1,6,4,64,128]{4,3,2,1,0:T(8,128)}, u32[]{:S(2)}) copy-start(f32[1,6,4,64,128]{4,3,2,1,0:T(8,128)} %source_ref.3) | copy-start | bytes 2359300
  2.7 0.9 %copy-start.2 = (f32[2,4,64,128]{3,2,1,0:T(8,128)S(1)}, f32[2,4,64,128]{3,2,1,0:T(8,128)}, u32[]{:S(2)}) copy-start(f32[2,4,64,128]{3,2,1,0:T(8,128)} %medium_ref.3) | copy-start | bytes 786436
  3.7 12.2 %copy-start.1 = (f32[1,6,4,64,128]{4,3,2,1,0:T(8,128)S(1)}, f32[1,6,4,64,128]{4,3,2,1,0:T(8,128)}, u32[]{:S(2)}) copy-start(f32[1,6,4,64,128]{4,3,2,1,0:T(8,128)} %source_ref.3) | copy-start | bytes 2359300
  3.7 12.2 %copy-start.4 = (bf16[1,6,4,64,128]{4,3,2,1,0:T(8,128)(2,1)S(1)}, bf16[1,6,4,64,128]{4,3,2,1,0:T(8,128)(2,1)}, u32[]{:S(2)}) copy-start(bf16[1,6,4,64,128]{4,3,2,1,0:T(8,128)(2,1)} %saved_ref.1) | copy-start | bytes 1179652
  4.6 11.2 %copy-start.3 = (f32[2,4,64,128]{3,2,1,0:T(8,128)S(1)}, f32[2,4,64,128]{3,2,1,0:T(8,128)}, u32[]{:S(2)}) copy-start(f32[2,4,64,128]{3,2,1,0:T(8,128)} %medium_ref.3) | copy-start | bytes 786436
  4.6 3.6 %collective-permute-start = (f32[904,128]{1,0:T(8,128)S(1)}, f32[904,128]{1,0:T(8,128)S(1)}, u32[]{:S(2)}, u32[]{:S(2)}) collective-permute-start(f32[904,128]{1,0:T(8,128)S(1)} %get-tuple-element.33), channel_id=1, source_target_pairs={{0,1},{1,0},{2,3},{3,2},{4,5},{5,4},{6,7},{7,6},{8,9},{9,8},{10,11... | collective-permute-start | bytes 1388552 | tf_op jit(solution)/shard_map/ppermute | solution.py:357
  4.7 10.8 %collective-permute-start.1 = (f32[904,128]{1,0:T(8,128)S(1)}, f32[904,128]{1,0:T(8,128)S(1)}, u32[]{:S(2)}, u32[]{:S(2)}) collective-permute-start(f32[904,128]{1,0:T(8,128)S(1)} %get-tuple-element.34), channel_id=1, source_target_pairs={{1,2},{2,1},{3,4},{4,3},{5,6},{6,5},{7,8},{8,7},{9,10},{10,9},{11,... | collective-permute-start | bytes 1388552 | tf_op jit(solution)/shard_map/ppermute | solution.py:365
  18.1 5.4 %collective-permute-start.2 = (f32[3,32,128]{2,1,0:T(8,128)S(1)}, f32[3,32,128]{2,1,0:T(8,128)S(1)}, u32[]{:S(2)}, u32[]{:S(2)}) collective-permute-start(f32[3,32,128]{2,1,0:T(8,128)S(1)} %get-tuple-element.36), channel_id=1, source_target_pairs={{0,1},{1,0},{2,3},{3,2},{4,5},{5,4},{6,7},{7,6},{8,9},{9,8},{10,11... | collective-permute-start | bytes 147464 | tf_op jit(solution)/shard_map/ppermute | solution.py:357
  23.5 12.5 %copy-start.5 = (f32[9,1,32,128]{3,2,1,0:T(8,128)S(1)}, f32[9,1,32,128]{3,2,1,0:T(8,128)}, u32[]{:S(2)}) copy-start(f32[9,1,32,128]{3,2,1,0:T(8,128)} %param.15) | copy-start | bytes 442372
  23.5 4.0 %collective-permute-start.4 = (f32[32,128]{1,0:T(8,128)S(1)}, f32[32,128]{1,0:T(8,128)S(1)}, u32[]{:S(2)}, u32[]{:S(2)}) collective-permute-start(f32[32,128]{1,0:T(8,128)S(1)} %get-tuple-element.48), channel_id=1, source_target_pairs={{0,2},{1,3},{2,0},{3,1},{4,6},{5,7},{6,4},{7,5},{8,10},{9,11},{10,... | collective-permute-start | bytes 49160 | tf_op jit(solution)/shard_map/ppermute | solution.py:400
  24.9 2.6 %collective-permute-start.5 = (f32[32,128]{1,0:T(8,128)S(1)}, f32[32,128]{1,0:T(8,128)S(1)}, u32[]{:S(2)}, u32[]{:S(2)}) collective-permute-start(f32[32,128]{1,0:T(8,128)S(1)} %get-tuple-element.49), channel_id=1, source_target_pairs={{5,1},{7,3},{9,5},{11,7},{13,9},{15,11},{21,17},{23,19},{25,21},{2... | collective-permute-start | bytes 49160 | tf_op jit(solution)/shard_map/ppermute | solution.py:401
  25.6 6.5 %collective-permute-start.3 = (f32[32,128]{1,0:T(8,128)S(1)}, f32[32,128]{1,0:T(8,128)S(1)}, u32[]{:S(2)}, u32[]{:S(2)}) collective-permute-start(f32[32,128]{1,0:T(8,128)S(1)} %get-tuple-element.39), channel_id=1, source_target_pairs={{2,4},{3,5},{4,2},{5,3},{6,8},{7,9},{8,6},{9,7},{10,12},{11,13},{1... | collective-permute-start | bytes 49160 | tf_op jit(solution)/shard_map/ppermute | solution.py:399
  32.1 3.8 %collective-permute-start.6 = (f32[32,128]{1,0:T(8,128)S(1)}, f32[32,128]{1,0:T(8,128)S(1)}, u32[]{:S(2)}, u32[]{:S(2)}) collective-permute-start(f32[32,128]{1,0:T(8,128)S(1)} %fusion.16), channel_id=1, source_target_pairs={{0,16},{16,0},{1,17},{17,1},{2,18},{18,2},{3,19},{19,3},{4,20},{20... | collective-permute-start | bytes 49160 | tf_op jit(solution)/shard_map/ppermute | solution.py:374

commit v2 on v1

v2 whole, which is shorter than its diff:
```python
import functools

import jax
import jax.numpy as jnp
from jax import lax
from jax.experimental import pallas as pl
from jax.experimental.pallas import tpu as pltpu
from jax.sharding import PartitionSpec as P


REACH = 2

sweep_steps = (0.323, 1.658, 0.422, 0.752)

PAD = 8
ROWS = 16


def lane_of(width):
    return lax.broadcasted_iota(jnp.int32, (ROWS, width), 1)


def ahead(value, lane):
    width = value.shape[-1]
    return jnp.where(lane == width - 1, 0.0, pltpu.roll(value, width - 1, 1))


def behind(value, lane):
    return jnp.where(lane == 0, 0.0, pltpu.roll(value, 1, 1))


def rows_at(ref, index, row, shift=0):
    return ref[index + (pl.ds(PAD + row + shift, ROWS), slice(None))]


def put(ref, index, row, value):
    ref[index + (pl.ds(PAD + row, ROWS), slice(None))] = value


def clear_pads(ref):
    rows = ref.shape[-2]
    lead = ref.shape[:-2]
    zero = jnp.zeros((PAD, ref.shape[-1]), jnp.float32)
    for flat in range(functools.reduce(lambda a, b: a * b, lead, 1)):
        index = []
        rest = flat
        for size in reversed(lead):
            index.insert(0, rest % size)
            rest //= size
        ref[tuple(index) + (pl.ds(0, PAD), slice(None))] = zero
        ref[tuple(index) + (pl.ds(rows - PAD, PAD), slice(None))] = zero


def chunks(total):
    return range(0, total, ROWS)


def curl(field, ahead_of, lane):
    out = []
    for part in (0, 3):
        ex, ey, ez = field(part, 0), field(part + 1, 0), field(part + 2, 0)
        hx = (field(part + 2, 1) - ez) - (ahead(ey, lane) - ey)
        hy = (ahead(ex, lane) - ex) - (ahead_of(part + 2) - ez)
        hz = (ahead_of(part + 1) - ey) - (field(part, 1) - ex)
        out += [hx, hy, hz]
    return out


def curl_back(held, before, lane):
    out = []
    for part in (0, 3):
        hx, hy, hz = held(part, 0), held(part + 1, 0), held(part + 2, 0)
        ox = (behind(hy, lane) - hy) - (held(part + 2, -1) - hz)
        oy = (before(part + 2) - hz) - (behind(hx, lane) - hx)
        oz = (held(part, -1) - hx) - (before(part + 1) - hy)
        out += [ox, oy, oz]
    return out


def updated(center, image, source, real, imag, scale):
    out = []
    for c in range(3):
        applied = image[c] + real * center[c] - imag * center[c + 3]
        out.append(center[c] + scale * (source[c] - applied))
    for c in range(3):
        applied = image[c + 3] + real * center[c + 3] + imag * center[c]
        out.append(center[c + 3] + scale * (source[c + 3] - applied))
    return out


def edge_sums(field, lane):
    out = []
    for part in (0, 3):
        ex = field(part, 0)
        out.append(field(part + 1, 0) + (field(part, 1) - ex))
        out.append(field(part + 2, 0) + (ahead(ex, lane) - ex))
    return out


def sweep_slab(state, held, result, source_ref, medium_ref, scale_ref, weight, low, high, first_scale, planes, rows, lane, wanted=None):
    wanted = range(planes) if wanted is None else wanted
    needed = sorted({i for w in wanted for i in (w - 1, w)})
    for i in needed:
        for row in chunks(rows):
            if i < 0:
                for part in (0, 3):
                    gy, gz = low(part, row)
                    ey, ez = rows_at(state, (part + 1, 0), row), rows_at(state, (part + 2, 0), row)
                    put(held, (part + 1, 0), row, first_scale * (gz - ez))
                    put(held, (part + 2, 0), row, first_scale * (ey - gy))
                continue

            def ahead_of(c, i=i, row=row):
                if i + 1 < planes:
                    return rows_at(state, (c, i + 1), row)
                return high(c, row)

            values = curl(lambda c, s: rows_at(state, (c, i), row, s), ahead_of, lane)
            for c in range(6):
                put(held, (c, i + 1), row, values[c])
    for i in wanted:
        for row in chunks(rows):
            image = curl_back(
                lambda c, s: rows_at(held, (c, i + 1), row, s), lambda c: rows_at(held, (c, i), row), lane
            )
            here = pl.ds(row, ROWS)
            new = updated(
                [rows_at(state, (c, i), row) for c in range(6)],
                image,
                [source_ref[0, c, i, here, :] for c in range(6)],
                medium_ref[0, i, here, :],
                medium_ref[1, i, here, :],
                weight * scale_ref[i, here, :],
            )
            for c in range(6):
                put(result, (c, i), row, new[c])


def first_sweep(source_ref, medium_ref, scale_ref, state, planes, rows):
    for i in range(planes):
        for row in chunks(rows):
            here = pl.ds(row, ROWS)
            scale = 1.0 / (4.0 + medium_ref[0, i, here, :])
            scale_ref[i, here, :] = scale
            for c in range(6):
                put(state, (c, i), row, sweep_steps[0] * source_ref[0, c, i, here, :] * scale)


def parity_and_ends():
    index = lax.axis_index("space")
    odd = lax.rem(index, 2) == 1
    first_scale = jnp.where(index == 0, 0.0, 1.0)
    last_scale = jnp.where(index == lax.axis_size("space") - 1, 0.0, 1.0)
    return odd, first_scale, last_scale


def emitter(odd, pair_ref, chip_ref, rows):
    def emit(slot, row, below, above):
        here = pl.ds(slot * rows + row, ROWS)
        pair_ref[here, :] = jnp.where(odd, below, above)
        chip_ref[here, :] = jnp.where(odd, above, below)

    return emit


def emit_level(emit, state, planes, rows, lane):
    for row in chunks(rows):
        sums = edge_sums(lambda c, s: rows_at(state, (c, planes - 1), row, s), lane)
        bottom = [rows_at(state, (c, 0), row) for c in (1, 2, 4, 5)]
        for k in range(4):
            emit(k, row, bottom[k], sums[k])


def start_kernel(
    source_hbm, medium_hbm, depth_hbm, map_hbm, pair_ref, chip_ref, source_ref, medium_ref, meta_ref, top, levels, owners, sems
):
    planes, rows, width = medium_ref.shape[1:]
    lane = lane_of(width)
    odd = parity_and_ends()[0]
    order = [planes - 1, 0] + list(range(1, planes - 1))
    copies = []
    for i in order:
        copies.append(pltpu.make_async_copy(medium_hbm.at[:, i], medium_ref.at[:, i], sems.at[2 * i]))
        copies.append(pltpu.make_async_copy(source_hbm.at[0, :, i], source_ref.at[0, :, i], sems.at[2 * i + 1]))
    copies.append(pltpu.make_async_copy(depth_hbm.at[0], levels, sems.at[2 * planes]))
    copies.append(pltpu.make_async_copy(map_hbm, owners, sems.at[2 * planes + 1]))
    for copy in copies:
        copy.start()
    clear_pads(top)
    emit = emitter(odd, pair_ref, chip_ref, rows)
    last = planes - 1
    for copy in copies[:2]:
        copy.wait()
    for row in chunks(rows):
        here = pl.ds(row, ROWS)
        scale = sweep_steps[0] / (4.0 + medium_ref[0, last, here, :])
        for c in range(6):
            put(top, (c,), row, scale * source_ref[0, c, last, here, :])
    for copy in copies[2:4]:
        copy.wait()
    for row in chunks(rows):
        here = pl.ds(row, ROWS)
        scale = sweep_steps[0] / (4.0 + medium_ref[0, 0, here, :])
        sums = edge_sums(lambda c, s: rows_at(top, (c,), row, s), lane)
        for k, c in enumerate((1, 2, 4, 5)):
            emit(k, row, scale * source_ref[0, c, 0, here, :], sums[k])
        for k in range(2):
            emit(4 + k, row, medium_ref[k, 0, here, :], medium_ref[k, last, here, :])
    for copy in copies[4:]:
        copy.wait()
    meta_ref[...] = jnp.zeros_like(meta_ref)
    meta_ref[pl.ds(0, 1), pl.ds(0, rows)] = levels[pl.ds(last, 1), :].astype(jnp.float32)
    meta_ref[pl.ds(1, 1), pl.ds(0, rows)] = owners[pl.ds(last, 1), :].astype(jnp.float32)


def no_plane(c, row):
    return 0.0


def no_sums(part, row):
    return 0.0, 0.0


def follow_kernel(
    source_ref, medium_ref, meta_ref, pair_ref, chip_ref, pair_two_ref, chip_two_ref, scale_ref, one, two, held
):
    planes, rows, width = medium_ref.shape[1:]
    lane = lane_of(width)
    odd, first_scale, _ = parity_and_ends()
    for ref in (one, two, held):
        clear_pads(ref)
    first_sweep(source_ref, medium_ref, scale_ref, one, planes, rows)
    sweep_slab(
        one, held, two, source_ref, medium_ref, scale_ref, sweep_steps[1], no_sums, no_plane, first_scale,
        planes, rows, lane,
    )
    emit_level(emitter(odd, pair_ref, chip_ref, rows), two, planes, rows, lane)
    for ref in (pair_ref, chip_ref):
        ref[pl.ds(4 * rows, PAD), :] = meta_ref[...]
    sweep_slab(
        two, held, one, source_ref, medium_ref, scale_ref, sweep_steps[2], no_sums, no_plane, first_scale,
        planes, rows, lane, wanted=sorted({0, planes - 1}),
    )
    emit_level(emitter(odd, pair_two_ref, chip_two_ref, rows), one, planes, rows, lane)


def readers(odd, pair_ref, chip_ref, rows):
    def from_below(slot, row):
        here = pl.ds(slot * rows + row, ROWS)
        return jnp.where(odd, pair_ref[here, :], chip_ref[here, :])

    def from_above(slot, row):
        here = pl.ds(slot * rows + row, ROWS)
        return jnp.where(odd, chip_ref[here, :], pair_ref[here, :])

    return from_below, from_above


WHERE_YZ = {1: 0, 2: 1, 4: 2, 5: 3}


def moments(saved_ref, state, moment_ref, i, rows, lane):
    for row in chunks(rows):
        here = pl.ds(row, ROWS)
        for c in range(3):
            real = saved_ref[0, c, i, here, :].astype(jnp.float32)
            imag = saved_ref[0, c + 3, i, here, :].astype(jnp.float32)
            value = real * rows_at(state, (c + 3, i), row) + imag * rows_at(state, (c, i), row)
            if c < 2:
                value = value + ahead(value, lane)
            put(moment_ref, (c, i), row, value)


def middle_kernel(
    source_ref, medium_ref, saved_ref, pair_ref, chip_ref, pair_one_ref, chip_one_ref,
    state_ref, held, extra_ref, moment_ref, one, two, scale_ref, delta_low, delta_high, delta_two,
):
    planes, rows, width = medium_ref.shape[1:]
    lane = lane_of(width)
    odd, first_scale, last_scale = parity_and_ends()
    for ref in (one, two, state_ref, held, delta_low, delta_high, delta_two, moment_ref):
        clear_pads(ref)
    first_sweep(source_ref, medium_ref, scale_ref, one, planes, rows)
    from_below, from_above = readers(odd, pair_ref, chip_ref, rows)

    for row in chunks(rows):
        sums = edge_sums(lambda c, s: rows_at(one, (c, planes - 1), row, s), lane)
        scale = (sweep_steps[1] * last_scale) / (4.0 + from_above(4, row))
        for k, c in enumerate((1, 2, 4, 5)):
            put(delta_high, (c,), row, scale * sums[k])
        scale = sweep_steps[1] / (4.0 + from_below(4, row))
        for part in (0, 3):
            ey, ez = rows_at(one, (part + 1, 0), row), rows_at(one, (part + 2, 0), row)
            put(delta_low, (part + 1,), row, scale * ey)
            put(delta_low, (part + 2,), row, scale * ez)
            put(delta_low, (part,), row, scale * ((behind(ez, lane) - ez) + (rows_at(one, (part + 1, 0), row, -1) - ey)))

    sweep_slab(
        one, held, two, source_ref, medium_ref, scale_ref, sweep_steps[1],
        lambda part, row: (from_below(2 * (part // 3), row), from_below(2 * (part // 3) + 1, row)),
        lambda c, row: from_above(WHERE_YZ[c], row),
        first_scale, planes, rows, lane,
    )

    none = [0.0] * 6
    for row in chunks(rows):
        values = curl(lambda c, s: rows_at(delta_low, (c,), row, s), lambda c: rows_at(two, (c, 0), row), lane)
        for c in range(6):
            put(held, (c, 0), row, values[c])
    for row in chunks(rows):
        before = {1: -rows_at(delta_low, (2,), row), 2: rows_at(delta_low, (1,), row),
                  4: -rows_at(delta_low, (5,), row), 5: rows_at(delta_low, (4,), row)}
        image = curl_back(lambda c, s: rows_at(held, (c, 0), row, s), lambda c: before[c], lane)
        real, imag = from_below(4, row), from_below(5, row)
        new = updated(
            [rows_at(delta_low, (c,), row) for c in range(6)], image, none, real, imag, sweep_steps[2] / (4.0 + real)
        )
        for c in range(6):
            put(delta_two, (c,), row, new[c])
    for row in chunks(rows):
        sums = edge_sums(lambda c, s: rows_at(delta_two, (c,), row, s), lane)
        for k in range(4):
            extra_ref[k, pl.ds(row, ROWS), :] = sums[k]
    for row in chunks(rows):
        for part in (0, 3):
            ey, ez = rows_at(delta_high, (part + 1,), row), rows_at(delta_high, (part + 2,), row)
            put(held, (part, 1), row, (rows_at(delta_high, (part + 2,), row, 1) - ez) - (ahead(ey, lane) - ey))
    for row in chunks(rows):
        here = pl.ds(row, ROWS)
        sums = edge_sums(lambda c, s: rows_at(two, (c, planes - 1), row, s), lane)
        real, imag = from_above(4, row), from_above(5, row)
        scale = (sweep_steps[2] * last_scale) / (4.0 + real)
        center, image = {}, {}
        for part in (0, 3):
            ey, ez = rows_at(delta_high, (part + 1,), row), rows_at(delta_high, (part + 2,), row)
            hx = rows_at(held, (part, 1), row)
            k = 2 * (part // 3)
            center[part + 1], center[part + 2] = ey, ez
            image[part + 1] = 2.0 * ey - sums[k] - (behind(hx, lane) - hx)
            image[part + 2] = (rows_at(held, (part, 1), row, -1) - hx) - sums[k + 1] + 2.0 * ez
        for k, c in enumerate((1, 2)):
            extra_ref[4 + k, here, :] = center[c] - scale * (image[c] + real * center[c] - imag * center[c + 3])
            extra_ref[6 + k, here, :] = center[c + 3] - scale * (
                image[c + 3] + real * center[c + 3] + imag * center[c]
            )

    below_one, above_one = readers(odd, pair_one_ref, chip_one_ref, rows)

    def low(part, row):
        k = 2 * (part // 3)
        ex = rows_at(delta_low, (part,), row)
        gy = below_one(k, row) + rows_at(delta_low, (part + 1,), row) + (rows_at(delta_low, (part,), row, 1) - ex)
        gz = below_one(k + 1, row) + rows_at(delta_low, (part + 2,), row) + (ahead(ex, lane) - ex)
        return gy, gz

    sweep_slab(
        two, held, state_ref, source_ref, medium_ref, scale_ref, sweep_steps[2],
        low, lambda c, row: above_one(WHERE_YZ[c], row) + rows_at(delta_high, (c,), row),
        first_scale, planes, rows, lane,
    )
    inner = range(1, planes - 1)
    sweep_slab(
        state_ref, held, one, source_ref, medium_ref, scale_ref, sweep_steps[3], None, None, first_scale,
        planes, rows, lane, wanted=inner,
    )
    for i in inner:
        moments(saved_ref, one, moment_ref, i, rows, lane)


def window_kernel(
    source_ref, medium_ref, saved_ref, keep_ref, offset_ref, edge_ref, pair_ref, chip_ref, state_ref, held_ref,
    extra_ref, moment_in_ref, send_ref, stay_ref, held, two, scale_ref, moment, window,
):
    planes, rows, width = medium_ref.shape[1:]
    lane = lane_of(width)
    odd, first_scale, _ = parity_and_ends()
    from_below, from_above = readers(odd, pair_ref, chip_ref, rows)
    clear_pads(held)
    clear_pads(moment)
    ends = sorted({0, planes - 1})

    for row in chunks(rows):
        here = pl.ds(row, ROWS)
        for part in (0, 3):
            k = 2 * (part // 3)
            ey, ez = rows_at(state_ref, (part + 1, 0), row), rows_at(state_ref, (part + 2, 0), row)
            gy = from_below(k, row) + extra_ref[k, here, :]
            gz = from_below(k + 1, row) + extra_ref[k + 1, here, :]
            put(held, (part + 1, 0), row, first_scale * (gz - ez))
            put(held, (part + 2, 0), row, first_scale * (ey - gy))
        values = curl(
            lambda c, s: rows_at(state_ref, (c, planes - 1), row, s),
            lambda c: from_above(WHERE_YZ[c], row) + extra_ref[4 + WHERE_YZ[c], here, :],
            lane,
        )
        for c in range(6):
            put(held, (c, 1), row, values[c])
    for i in ends:
        for row in chunks(rows):
            here = pl.ds(row, ROWS)
            if i == planes - 1:
                now = lambda c, s: rows_at(held, (c, 1), row, s)
            else:
                now = lambda c, s: rows_at(held_ref, (c, i + 1), row, s)
            if i == 0:
                before = lambda c: rows_at(held, (c, 0), row)
            else:
                before = lambda c: rows_at(held_ref, (c, i), row)
            image = curl_back(now, before, lane)
            real, imag = medium_ref[0, i, here, :], medium_ref[1, i, here, :]
            new = updated(
                [rows_at(state_ref, (c, i), row) for c in range(6)], image,
                [source_ref[0, c, i, here, :] for c in range(6)], real, imag, sweep_steps[3] / (4.0 + real),
            )
            for c in range(6):
                put(two, (c, i), row, new[c])
        moments(saved_ref, two, moment, i, rows, lane)

    def moment_rows(c, i, row, shift=0):
        return rows_at(moment if i in ends else moment_in_ref, (c, i), row, shift)

    for row in chunks(rows):
        here = pl.ds(row, ROWS)
        sums = [0.0] * (2 * REACH + 2)

        def add(value, offset, low):
            for k in range(2 * REACH + 1):
                slot = k + low
                sums[slot] = sums[slot] + jnp.where(offset == float(slot - REACH - 1), value, 0.0)

        def side(i):
            return moment_rows(1, i, row) + (moment_rows(2, i, row) + moment_rows(2, i, row, 1))

        lower = side(0)
        add(edge_ref[0, here, :] * lower, edge_ref[1, here, :], 0)
        for i in range(planes):
            cell = moment_rows(0, i, row) + moment_rows(0, i, row, 1) + lower
            if i + 1 < planes:
                lower = side(i + 1)
                cell = cell + lower
            add(keep_ref[i, here, :] * cell, offset_ref[i, here, :], 1)
        for k in range(2 * REACH + 2):
            window[k, here, :] = sums[k]
    for k in range(2 * REACH + 2):
        both = window[k, pl.ds(0, rows // 2, stride=2), :] + window[k, pl.ds(1, rows // 2, stride=2), :]
        if k % 2 == 0:
            send_ref[k // 2] = both
        else:
            stay_ref[k // 2] = both


def vmem():
    return pl.BlockSpec(memory_space=pltpu.VMEM)


def call(kernel, out_shape, scratch, arguments, in_specs=None, limit=24 << 20, flops=1 << 20):
    return pl.pallas_call(
        kernel,
        out_shape=[jax.ShapeDtypeStruct(s, jnp.float32) for s in out_shape],
        in_specs=in_specs or [vmem()] * len(arguments),
        out_specs=[vmem()] * len(out_shape),
        scratch_shapes=[s if not isinstance(s, tuple) else pltpu.VMEM(s, jnp.float32) for s in scratch],
        compiler_params=pltpu.CompilerParams(vmem_limit_bytes=limit),
        cost_estimate=pl.CostEstimate(flops=flops, bytes_accessed=1 << 20, transcendentals=0),
    )(*arguments)


def core_swap(value):
    size = lax.axis_size("space")
    return lax.ppermute(value, "space", [(i, i ^ 1) for i in range(size)])


def chip_swap(value):
    size = lax.axis_size("space")
    pairs = []
    for i in range(1, size - 1, 2):
        pairs += [(i, i + 1), (i + 1, i)]
    return lax.ppermute(value, "space", pairs)


def sum_over_groups(value):
    size = lax.axis_size("src")
    if size & (size - 1):
        return lax.psum(value, "src")
    step = 1
    while step < size:
        value = value + lax.ppermute(value, "src", [(i, i ^ step) for i in range(size)])
        step *= 2
    return value


def gather_owned(send, stay):
    size = lax.axis_size("space")
    index = lax.axis_index("space")
    odd = lax.rem(index, 2) == 1
    other = core_swap(send)
    from_far = lax.ppermute(send[0], "space", [(i, i - 3) for i in range(4, size, 2)])
    below = stay[0] + jnp.where(odd, other[1], other[0])
    here = stay[1] + jnp.where(odd, other[2], other[1])
    above = stay[2] + jnp.where(odd, 0.0, other[2])
    chip = index // 2
    upward = lax.rem(chip, 2) == 0
    chips = size // 2
    inner, outer = [], []
    for c in range(chips):
        for core in range(2):
            if c ^ 1 < chips:
                inner.append((2 * c + core, 2 * (c ^ 1) + core))
            partner = ((c + 1) ^ 1) - 1
            if 0 <= partner < chips:
                outer.append((2 * c + core, 2 * partner + core))
    from_outer = lax.ppermute(jnp.where(upward, below, above), "space", outer)
    from_inner = lax.ppermute(jnp.where(upward, above, below), "space", inner)
    return here + from_far + from_outer + from_inner


def transposed_smooth(summed, rough):
    rows_in = summed.shape[-2]
    depth_in = summed.shape[-1]
    total = jnp.zeros_like(summed)
    for vertical in range(3):
        for lateral in range(3):
            product = rough[vertical * 3 + lateral] * summed
            padded = jnp.pad(product, ((0, 0), (1, 1), (1, 1)))
            total = (
                total
                + padded[
                    :, 2 - vertical : 2 - vertical + rows_in, 2 - lateral : 2 - lateral + depth_in
                ]
            )
    return total


def slab(adjoint_source, forward_field, medium, plane_map, depth, rough):
    planes, rows, width = medium.shape[1:]
    index = lax.axis_index("space")
    plane = (rows + 2 * PAD, width)
    state = (6, planes) + plane
    held = (6, planes + 1) + plane
    scale = (planes, rows, width)
    hbm = pl.BlockSpec(memory_space=pltpu.HBM)
    columns = pltpu.VMEM((planes, rows), jnp.int32)
    given = (adjoint_source, medium, depth, plane_map)
    pair, chip, adjoint_source, medium, meta = call(
        start_kernel,
        [(6 * rows, width)] * 2 + [adjoint_source.shape, medium.shape, (PAD, width)],
        [(6,) + plane, columns, columns, pltpu.SemaphoreType.DMA((2 * planes + 2,))],
        tuple(pltpu.with_memory_space_constraint(a, pltpu.HBM) for a in given),
        in_specs=[hbm] * 4,
    )
    chip = chip_swap(chip)
    pair = core_swap(pair)
    pair_one, chip_one, pair_two, chip_two = call(
        follow_kernel,
        [(4 * rows + PAD, width)] * 2 + [(4 * rows, width)] * 2,
        [scale, state, state, held],
        (adjoint_source, medium, meta),
    )
    chip_one = chip_swap(chip_one)
    pair_one = core_swap(pair_one)
    chip_two = chip_swap(chip_two)
    pair_two = core_swap(pair_two)

    here = index.astype(jnp.float32)
    levels = depth[0].astype(jnp.float32)
    owners = plane_map.astype(jnp.float32)
    position = lax.broadcasted_iota(jnp.int32, (planes, rows, width), 2).astype(jnp.float32)
    keep = jnp.where(position < levels[:, :, None], 0.25, 0.0)
    offset = jnp.broadcast_to((owners - here)[:, :, None], (planes, rows, width))
    below = jnp.where(lax.rem(index, 2) == 1, pair_one[4 * rows :], chip_one[4 * rows :])
    edge = jnp.stack(
        [
            jnp.where(position[0] < below[0, :rows, None], 0.25, 0.0),
            jnp.broadcast_to((below[1, :rows] - here)[:, None], (rows, width)),
        ]
    )
    middle, curls, extra, moment = call(
        middle_kernel,
        [state, held, (8, rows, width), (3, planes) + plane],
        [state, state, scale, (6,) + plane, (6,) + plane, (6,) + plane],
        (adjoint_source, medium, forward_field, pair, chip, pair_one, chip_one),
    )
    send, stay = call(
        window_kernel,
        [(REACH + 1, rows // 2, width), (REACH + 1, rows // 2, width)],
        [(6, 2) + plane, state, scale, (3, planes) + plane, (2 * REACH + 2, rows, width)],
        (adjoint_source, medium, forward_field, keep, offset, edge, pair_two, chip_two, middle, curls, extra, moment),
    )
    total = sum_over_groups(gather_owned(send, stay))
    return transposed_smooth(total[None], rough)


def solution(mesh):
    in_specs = (
        P("src", None, "space", None, None),
        P("src", None, "space", None, None),
        P(None, "space", None, None),
        P("space", None),
        P("src", "space", None),
        P(None, "space", None, None),
    )
    out_specs = P("space", None, None)
    return jax.shard_map(slab, mesh=mesh, in_specs=in_specs, out_specs=out_specs, check_vma=False)
```

time: 37 us -> 34 us (0.919)
  waiting for transfers between devices: 15 us -> 8.99 us
  starting transfers between devices: 13.6 us -> 18.7 us
  local copies, waits for them, and re-layouts: 3.13 us -> 0.18 us
  Pallas kernels: 3.16 us -> 4.73 us
  other arithmetic: 1.64 us -> 0.96 us
    ppermute x1 -> x3, starting transfers between devices: 3.4 us -> 9.31 us  [chip_swap(): return lax.ppermute(value, 'space', pairs)]
    ppermute x1 -> x3, waiting for transfers between devices: 7.28 us -> 2.14 us  [chip_swap(): return lax.ppermute(value, 'space', pairs)]
    unnamed x14 -> x8, local copies, waits for them, and re-layouts: 2.77 us -> 0.02 us
    ppermute x2 -> x4, starting transfers between devices: 4.58 us -> 2.22 us  [core_swap(): return lax.ppermute(value, 'space', [(i, i ^ 1) for i in range(size)])]
    pallas_call x2 -> x4, Pallas kernels: 3.16 us -> 4.73 us  [call(): pl.pallas_call(kernel, out_shape=[jax.ShapeDtypeStruct(s, jnp.float32) fo...]
    ppermute x1, starting transfers between devices: 1.45 us -> 2.39 us  [gather_owned(): from_inner = lax.ppermute(jnp.where(upward, above, below), 'space', inner)]
    ppermute x2 -> x4, waiting for transfers between devices: 0.88 us -> 0.01 us  [core_swap(): return lax.ppermute(value, 'space', [(i, i ^ 1) for i in range(size)])]
    convert_element_type x3 -> x2, other arithmetic: 0.69 us -> 0.01 us  [the longest x1 0.01 us: slab(): lax.broadcasted_iota(jnp.int32, (planes, rows, width), 2)]
  transfers between devices with their start and end apart: 7 -> 11, of which waited for: 4 -> 4; matrix products, arithmetic and copies ran while one was open for 0% -> 1% of each run, Pallas kernels for 0% -> 6%
where the time goes in v2:
time: 34 us; the launch traced here: 33.8 us
  starting transfers between devices  18.7 us (55%)
  waiting for transfers between devices  8.99 us (26%)
  Pallas kernels  4.73 us (14%)
  other arithmetic  0.96 us (3%)
    ppermute x3, starting transfers between devices, chip_swap(): return lax.ppermute(value, 'space', pairs)  9.31 us
    pallas_call x4, Pallas kernels, call(): pl.pallas_call(kernel, out_shape=[jax.ShapeDtypeStruct(s, jnp.float32) fo...  4.73 us
    ppermute x1, waiting for transfers between devices, gather_owned(): from_outer = lax.ppermute(jnp.where(upward, below, above), 'space', outer)  4.58 us
    ppermute x1, starting transfers between devices, gather_owned(): from_inner = lax.ppermute(jnp.where(upward, above, below), 'space', inner)  2.39 us
    ppermute x1, waiting for transfers between devices, sum_over_groups(): lax.ppermute(value, 'src', [(i, i ^ step) for i in range(size)])  2.25 us
    ppermute x4, starting transfers between devices, core_swap(): return lax.ppermute(value, 'space', [(i, i ^ 1) for i in range(size)])  2.22 us
    ppermute x3, waiting for transfers between devices, chip_swap(): return lax.ppermute(value, 'space', pairs)  2.14 us
    ppermute x1, starting transfers between devices, gather_owned(): from_outer = lax.ppermute(jnp.where(upward, below, above), 'space', outer)  1.91 us
  transfers between devices with their start and end apart: 11, of which 4 were waited for; matrix products, arithmetic and copies ran while one was open for 1% of the time, Pallas kernels for 6%

profile of v2, /device:TPU:8, one launch (start us, length us, event | category | flops | bytes accessed | tf_op | source)
XLA Modules:
  0.0 33.8 jit_solution(17677217010515123568)
XLA Ops:
  0.0 1.4 %shard_map.64 = (f32[384,128]{1,0:T(8,128)S(1)}, f32[384,128]{1,0:T(8,128)S(1)}, f32[1,6,4,64,128]{4,3,2,1,0:T(8,128)S(1)}, f32[2,4,64,128]{3,2,1,0:T(8,128)S(1)}, f32[8,128]{1,0:T(8,128)S(1)}) custom-call(f32[1,6,4,64,128]{4,3,2,1,0:T(8,128)} %source_hbm.1, f32[2,4,64,128]{3,2,1,0:T(8,128)} %medium_hbm.1, s32[1,4,64]{2,1,0:T(4,128)} %depth_hbm.1, ...), custom_call_target="tpu_custom_call" | custom-call | flops 1048576 | bytes 1048576 | tf_op jit(solution)/shard_map/pallas_call | solution.py:457
  1.4 0.9 %shard_map.65 = (f32[264,128]{1,0:T(8,128)S(1)}, f32[264,128]{1,0:T(8,128)S(1)}, f32[256,128]{1,0:T(8,128)S(1)}, f32[256,128]{1,0:T(8,128)S(1)}) custom-call(f32[1,6,4,64,128]{4,3,2,1,0:T(8,128)S(1)} %get-tuple-element.20.source_ref, f32[2,4,64,128]{3,2,1,0:T(8,128)S(1)} %get-tuple-element.21.medium_ref, f32[8,128]{1,0:T(8,128)S(1)} %get-tuple-element.22.meta_ref), custom_call_target="tpu_custom_call" | custom-call | flops 1048576 | bytes 1048576 | tf_op jit(solution)/shard_map/pallas_call | solution.py:457
  2.4 0.1 collective-permute-start
  2.5 3.4 %collective-permute-start.1 = (f32[264,128]{1,0:T(8,128)S(1)}, f32[264,128]{1,0:T(8,128)S(1)}, u32[]{:S(2)}, u32[]{:S(2)}) collective-permute-start(f32[264,128]{1,0:T(8,128)S(1)} %get-tuple-element.24), channel_id=1, source_target_pairs={{1,2},{2,1},{3,4},{4,3},{5,6},{6,5},{7,8},{8,7},{9,10},{10,9},{11,... | collective-permute-start | bytes 405512 | tf_op jit(solution)/shard_map/ppermute | solution.py:478
  5.9 0.2 collective-permute-start.4
  6.1 2.9 %collective-permute-start.5 = (f32[384,128]{1,0:T(8,128)S(1)}, f32[384,128]{1,0:T(8,128)S(1)}, u32[]{:S(2)}, u32[]{:S(2)}) collective-permute-start(f32[384,128]{1,0:T(8,128)S(1)} %get-tuple-element.28), channel_id=1, source_target_pairs={{1,2},{2,1},{3,4},{4,3},{5,6},{6,5},{7,8},{8,7},{9,10},{10,9},{11,... | collective-permute-start | bytes 589832 | tf_op jit(solution)/shard_map/ppermute | solution.py:478
  9.0 0.7 %collective-permute-start.2 = (f32[256,128]{1,0:T(8,128)S(1)}, f32[256,128]{1,0:T(8,128)S(1)}, u32[]{:S(2)}, u32[]{:S(2)}) collective-permute-start(f32[256,128]{1,0:T(8,128)S(1)} %get-tuple-element.25), channel_id=1, source_target_pairs={{0,1},{1,0},{2,3},{3,2},{4,5},{5,4},{6,7},{7,6},{8,9},{9,8},{10,11... | collective-permute-start | bytes 393224 | tf_op jit(solution)/shard_map/ppermute | solution.py:470
  9.7 0.1 compare_select_fusion.keep_ref
  9.8 0.0 collective-permute-done.pair_one_ref
  9.8 3.0 %collective-permute-start.3 = (f32[256,128]{1,0:T(8,128)S(1)}, f32[256,128]{1,0:T(8,128)S(1)}, u32[]{:S(2)}, u32[]{:S(2)}) collective-permute-start(f32[256,128]{1,0:T(8,128)S(1)} %get-tuple-element.26), channel_id=1, source_target_pairs={{1,2},{2,1},{3,4},{4,3},{5,6},{6,5},{7,8},{8,7},{9,10},{10,9},{11,... | collective-permute-start | bytes 393224 | tf_op jit(solution)/shard_map/ppermute | solution.py:478
  12.8 0.0 collective-permute-done.1.chip_one_ref
  12.9 0.1 compare_select_fusion.1
  12.9 0.1 stack_broadcast_in_dim.2
  13.0 0.0 collective-permute-done.4.pair_ref
  13.0 1.0 %collective-permute-done.5.chip_ref = f32[384,128]{1,0:T(8,128)S(1)} collective-permute-done((f32[384,128]{1,0:T(8,128)S(1)}, f32[384,128]{1,0:T(8,128)S(1)}, u32[]{:S(2)}, u32[]{:S(2)}) %collective-permute-start.5) | collective-permute-done | bytes 196640 | tf_op jit(solution)/shard_map/ppermute | solution.py:478
  14.0 1.9 %shard_map.66 = (f32[6,4,80,128]{3,2,1,0:T(8,128)S(1)}, f32[6,5,80,128]{3,2,1,0:T(8,128)S(1)}, f32[8,64,128]{2,1,0:T(8,128)S(1)}, f32[3,4,80,128]{3,2,1,0:T(8,128)S(1)}) custom-call(f32[1,6,4,64,128]{4,3,2,1,0:T(8,128)S(1)} %get-tuple-element.20.source_ref, f32[2,4,64,128]{3,2,1,0:T(8,128)S(1)} %get-tuple-element.21.medium_ref, ...), custom_call_target="tpu_custom_call" | custom-call | flops 1048576 | bytes 1048576 | tf_op jit(solution)/shard_map/pallas_call | solution.py:457
  16.0 0.0 collective-permute-done.2.pair_ref
  16.0 1.1 %collective-permute-done.3.chip_ref = f32[256,128]{1,0:T(8,128)S(1)} collective-permute-done((f32[256,128]{1,0:T(8,128)S(1)}, f32[256,128]{1,0:T(8,128)S(1)}, u32[]{:S(2)}, u32[]{:S(2)}) %collective-permute-start.3) | collective-permute-done | bytes 131104 | tf_op jit(solution)/shard_map/ppermute | solution.py:478
  17.1 0.1 broadcast_in_dim.31.offset_ref
  17.2 0.0 copy-start.1
  17.2 0.5 %shard_map.67 = (f32[3,32,128]{2,1,0:T(8,128)S(1)}, f32[3,32,128]{2,1,0:T(8,128)S(1)}) custom-call(f32[1,6,4,64,128]{4,3,2,1,0:T(8,128)S(1)} %get-tuple-element.20.source_ref, f32[2,4,64,128]{3,2,1,0:T(8,128)S(1)} %get-tuple-element.21.medium_ref, bf16[1,6,4,64,128]{4,3,2,1,0:T(8,128)(2,1)S(1)} %copy-done, f32[4,64,128]{2,1,0:T(8,128)S(1)} %compare_select_fusion.keep_ref, ...), custom_call_target="tpu_custom_call" | custom-call | flops 1048576 | bytes 1048576 | tf_op jit(solution)/shard_map/pallas_call | solution.py:457
  17.7 1.3 %collective-permute-start.6 = (f32[3,32,128]{2,1,0:T(8,128)S(1)}, f32[3,32,128]{2,1,0:T(8,128)S(1)}, u32[]{:S(2)}, u32[]{:S(2)}) collective-permute-start(f32[3,32,128]{2,1,0:T(8,128)S(1)} %get-tuple-element.34), channel_id=1, source_target_pairs={{0,1},{1,0},{2,3},{3,2},{4,5},{5,4},{6,7},{7,6},{8,9},{9,8},{10,11... | collective-permute-start | bytes 147464 | tf_op jit(solution)/shard_map/ppermute | solution.py:470
  19.0 1.3 %collective-permute-start.7 = (f32[32,128]{1,0:T(8,128)S(1)}, f32[32,128]{1,0:T(8,128)S(1)}, u32[]{:S(2)}, u32[]{:S(2)}) collective-permute-start(f32[32,128]{1,0:T(8,128)S(1)} %slice_bitcast_fusion), channel_id=1, source_target_pairs={{4,1},{6,3},{8,5},{10,7},{12,9},{14,11},{20,17},{22,19},{24,21},{2... | collective-permute-start | bytes 49160 | tf_op jit(solution)/shard_map/ppermute | solution.py:497
  20.3 0.0 collective-permute-done.6
  20.3 2.4 %collective-permute-start.9 = (f32[32,128]{1,0:T(8,128)S(1)}, f32[32,128]{1,0:T(8,128)S(1)}, u32[]{:S(2)}, u32[]{:S(2)}) collective-permute-start(f32[32,128]{1,0:T(8,128)S(1)} %select_bitcast_fusion), channel_id=1, source_target_pairs={{0,2},{1,3},{2,0},{3,1},{4,6},{5,7},{6,4},{7,5},{8,10},{9,11},{10,... | collective-permute-start | bytes 49160 | tf_op jit(solution)/shard_map/ppermute | solution.py:513
  22.7 1.9 %collective-permute-start.8 = (f32[32,128]{1,0:T(8,128)S(1)}, f32[32,128]{1,0:T(8,128)S(1)}, u32[]{:S(2)}, u32[]{:S(2)}) collective-permute-start(f32[32,128]{1,0:T(8,128)S(1)} %get-tuple-element.37), channel_id=1, source_target_pairs={{2,4},{3,5},{4,2},{5,3},{6,8},{7,9},{8,6},{9,7},{10,12},{11,13},{1... | collective-permute-start | bytes 49160 | tf_op jit(solution)/shard_map/ppermute | solution.py:512
  24.6 0.0 collective-permute-done.7
  24.6 0.0 collective-permute-done.9
  24.6 4.6 %collective-permute-done.8 = f32[32,128]{1,0:T(8,128)S(1)} collective-permute-done((f32[32,128]{1,0:T(8,128)S(1)}, f32[32,128]{1,0:T(8,128)S(1)}, u32[]{:S(2)}, u32[]{:S(2)}) %collective-permute-start.8) | collective-permute-done | bytes 16416 | tf_op jit(solution)/shard_map/ppermute | solution.py:512
  29.2 1.6 %collective-permute-start.10 = (f32[32,128]{1,0:T(8,128)S(1)}, f32[32,128]{1,0:T(8,128)S(1)}, u32[]{:S(2)}, u32[]{:S(2)}) collective-permute-start(f32[32,128]{1,0:T(8,128)S(1)} %fusion.17), channel_id=1, source_target_pairs={{0,16},{16,0},{1,17},{17,1},{2,18},{18,2},{3,19},{19,3},{4,20},{20... | collective-permute-start | bytes 49160 | tf_op jit(solution)/shard_map/ppermute | solution.py:487
  30.8 2.2 %collective-permute-done.10 = f32[32,128]{1,0:T(8,128)S(1)} collective-permute-done((f32[32,128]{1,0:T(8,128)S(1)}, f32[32,128]{1,0:T(8,128)S(1)}, u32[]{:S(2)}, u32[]{:S(2)}) %collective-permute-start.10) | collective-permute-done | bytes 16416 | tf_op jit(solution)/shard_map/ppermute | solution.py:487
  33.1 0.7 %fusion.7 = f32[1,32,128]{2,1,0:T(8,128)} fusion(f32[1,32,128]{2,1,0:T(8,128)S(1)} %get-tuple-element.45, f32[1,32,128]{2,1,0:T(8,128)S(1)} %get-tuple-element.44, f32[1,32,128]{2,1,0:T(8,128)S(1)} %get-tuple-element.43, f32[1,32,128]{2,1,0:T(8,128)S(1)} %get-tuple-element.42, f32[1,32,128]{2,1,0:T(8,128)S(1)} %get-tuple-element.41, ...), kind=kLoop, calls=%fused_computation.18 | loop fusion | flops 36864 | bytes 180224 | tf_op jit(solution)/shard_map/add | solution.py:526
  (19 shorter events, 0.1 us)
Async XLA Ops:
  0.0 9.7 %copy-start.2 = (s32[1,4,64]{2,1,0:T(4,128)S(1)}, s32[1,4,64]{2,1,0:T(4,128)}, u32[]{:S(2)}) copy-start(s32[1,4,64]{2,1,0:T(4,128)} %depth_hbm.1) | copy-start | bytes 3076
  0.0 9.8 %copy-start.3 = (s32[4,64]{1,0:T(4,128)S(1)}, s32[4,64]{1,0:T(4,128)}, u32[]{:S(2)}) copy-start(s32[4,64]{1,0:T(4,128)} %map_hbm.1) | copy-start | bytes 3076
  0.0 14.0 %copy-start = (bf16[1,6,4,64,128]{4,3,2,1,0:T(8,128)(2,1)S(1)}, bf16[1,6,4,64,128]{4,3,2,1,0:T(8,128)(2,1)}, u32[]{:S(2)}) copy-start(bf16[1,6,4,64,128]{4,3,2,1,0:T(8,128)(2,1)} %saved_ref.3) | copy-start | bytes 1179652
  2.4 7.4 %collective-permute-start = (f32[264,128]{1,0:T(8,128)S(1)}, f32[264,128]{1,0:T(8,128)S(1)}, u32[]{:S(2)}, u32[]{:S(2)}) collective-permute-start(f32[264,128]{1,0:T(8,128)S(1)} %get-tuple-element.23), channel_id=1, source_target_pairs={{0,1},{1,0},{2,3},{3,2},{4,5},{5,4},{6,7},{7,6},{8,9},{9,8},{10,11... | collective-permute-start | bytes 405512 | tf_op jit(solution)/shard_map/ppermute | solution.py:470
  2.5 10.4 %collective-permute-start.1 = (f32[264,128]{1,0:T(8,128)S(1)}, f32[264,128]{1,0:T(8,128)S(1)}, u32[]{:S(2)}, u32[]{:S(2)}) collective-permute-start(f32[264,128]{1,0:T(8,128)S(1)} %get-tuple-element.24), channel_id=1, source_target_pairs={{1,2},{2,1},{3,4},{4,3},{5,6},{6,5},{7,8},{8,7},{9,10},{10,9},{11,... | collective-permute-start | bytes 405512 | tf_op jit(solution)/shard_map/ppermute | solution.py:478
  5.9 7.2 %collective-permute-start.4 = (f32[384,128]{1,0:T(8,128)S(1)}, f32[384,128]{1,0:T(8,128)S(1)}, u32[]{:S(2)}, u32[]{:S(2)}) collective-permute-start(f32[384,128]{1,0:T(8,128)S(1)} %get-tuple-element.27), channel_id=1, source_target_pairs={{0,1},{1,0},{2,3},{3,2},{4,5},{5,4},{6,7},{7,6},{8,9},{9,8},{10,11... | collective-permute-start | bytes 589832 | tf_op jit(solution)/shard_map/ppermute | solution.py:470
  6.1 8.0 %collective-permute-start.5 = (f32[384,128]{1,0:T(8,128)S(1)}, f32[384,128]{1,0:T(8,128)S(1)}, u32[]{:S(2)}, u32[]{:S(2)}) collective-permute-start(f32[384,128]{1,0:T(8,128)S(1)} %get-tuple-element.28), channel_id=1, source_target_pairs={{1,2},{2,1},{3,4},{4,3},{5,6},{6,5},{7,8},{8,7},{9,10},{10,9},{11,... | collective-permute-start | bytes 589832 | tf_op jit(solution)/shard_map/ppermute | solution.py:478
  9.0 7.0 %collective-permute-start.2 = (f32[256,128]{1,0:T(8,128)S(1)}, f32[256,128]{1,0:T(8,128)S(1)}, u32[]{:S(2)}, u32[]{:S(2)}) collective-permute-start(f32[256,128]{1,0:T(8,128)S(1)} %get-tuple-element.25), channel_id=1, source_target_pairs={{0,1},{1,0},{2,3},{3,2},{4,5},{5,4},{6,7},{7,6},{8,9},{9,8},{10,11... | collective-permute-start | bytes 393224 | tf_op jit(solution)/shard_map/ppermute | solution.py:470
  9.8 7.3 %collective-permute-start.3 = (f32[256,128]{1,0:T(8,128)S(1)}, f32[256,128]{1,0:T(8,128)S(1)}, u32[]{:S(2)}, u32[]{:S(2)}) collective-permute-start(f32[256,128]{1,0:T(8,128)S(1)} %get-tuple-element.26), channel_id=1, source_target_pairs={{1,2},{2,1},{3,4},{4,3},{5,6},{6,5},{7,8},{8,7},{9,10},{10,9},{11,... | collective-permute-start | bytes 393224 | tf_op jit(solution)/shard_map/ppermute | solution.py:478
  17.2 15.8 %copy-start.1 = (f32[9,1,32,128]{3,2,1,0:T(8,128)S(1)}, f32[9,1,32,128]{3,2,1,0:T(8,128)}, u32[]{:S(2)}) copy-start(f32[9,1,32,128]{3,2,1,0:T(8,128)} %param.11) | copy-start | bytes 442372
  17.7 2.6 %collective-permute-start.6 = (f32[3,32,128]{2,1,0:T(8,128)S(1)}, f32[3,32,128]{2,1,0:T(8,128)S(1)}, u32[]{:S(2)}, u32[]{:S(2)}) collective-permute-start(f32[3,32,128]{2,1,0:T(8,128)S(1)} %get-tuple-element.34), channel_id=1, source_target_pairs={{0,1},{1,0},{2,3},{3,2},{4,5},{5,4},{6,7},{7,6},{8,9},{9,8},{10,11... | collective-permute-start | bytes 147464 | tf_op jit(solution)/shard_map/ppermute | solution.py:470
  19.0 5.6 %collective-permute-start.7 = (f32[32,128]{1,0:T(8,128)S(1)}, f32[32,128]{1,0:T(8,128)S(1)}, u32[]{:S(2)}, u32[]{:S(2)}) collective-permute-start(f32[32,128]{1,0:T(8,128)S(1)} %slice_bitcast_fusion), channel_id=1, source_target_pairs={{4,1},{6,3},{8,5},{10,7},{12,9},{14,11},{20,17},{22,19},{24,21},{2... | collective-permute-start | bytes 49160 | tf_op jit(solution)/shard_map/ppermute | solution.py:497
  20.3 4.3 %collective-permute-start.9 = (f32[32,128]{1,0:T(8,128)S(1)}, f32[32,128]{1,0:T(8,128)S(1)}, u32[]{:S(2)}, u32[]{:S(2)}) collective-permute-start(f32[32,128]{1,0:T(8,128)S(1)} %select_bitcast_fusion), channel_id=1, source_target_pairs={{0,2},{1,3},{2,0},{3,1},{4,6},{5,7},{6,4},{7,5},{8,10},{9,11},{10,... | collective-permute-start | bytes 49160 | tf_op jit(solution)/shard_map/ppermute | solution.py:513
  22.7 6.5 %collective-permute-start.8 = (f32[32,128]{1,0:T(8,128)S(1)}, f32[32,128]{1,0:T(8,128)S(1)}, u32[]{:S(2)}, u32[]{:S(2)}) collective-permute-start(f32[32,128]{1,0:T(8,128)S(1)} %get-tuple-element.37), channel_id=1, source_target_pairs={{2,4},{3,5},{4,2},{5,3},{6,8},{7,9},{8,6},{9,7},{10,12},{11,13},{1... | collective-permute-start | bytes 49160 | tf_op jit(solution)/shard_map/ppermute | solution.py:512
  29.2 3.8 %collective-permute-start.10 = (f32[32,128]{1,0:T(8,128)S(1)}, f32[32,128]{1,0:T(8,128)S(1)}, u32[]{:S(2)}, u32[]{:S(2)}) collective-permute-start(f32[32,128]{1,0:T(8,128)S(1)} %fusion.17), channel_id=1, source_target_pairs={{0,16},{16,0},{1,17},{17,1},{2,18},{18,2},{3,19},{19,3},{4,20},{20... | collective-permute-start | bytes 49160 | tf_op jit(solution)/shard_map/ppermute | solution.py:487

commit v3 on v2

--- a/solution.py
+++ b/solution.py
@@ -154,15 +154,6 @@
     return odd, first_scale, last_scale
 
 
-def emitter(odd, pair_ref, chip_ref, rows):
-    def emit(slot, row, below, above):
-        here = pl.ds(slot * rows + row, ROWS)
-        pair_ref[here, :] = jnp.where(odd, below, above)
-        chip_ref[here, :] = jnp.where(odd, above, below)
-
-    return emit
-
-
 def emit_level(emit, state, planes, rows, lane):
     for row in chunks(rows):
         sums = edge_sums(lambda c, s: rows_at(state, (c, planes - 1), row, s), lane)
@@ -171,8 +162,12 @@
             emit(k, row, bottom[k], sums[k])
 
 
+def message_rows(slot, row, rows):
+    return pl.ds(slot * rows + row, ROWS)
+
+
 def start_kernel(
-    source_hbm, medium_hbm, depth_hbm, map_hbm, pair_ref, chip_ref, source_ref, medium_ref, meta_ref, top, levels, owners, sems
+    source_hbm, medium_hbm, depth_hbm, map_hbm, chip_ref, source_ref, medium_ref, meta_ref, top, levels, owners, sems
 ):
     planes, rows, width = medium_ref.shape[1:]
     lane = lane_of(width)
@@ -187,8 +182,11 @@
     for copy in copies:
         copy.start()
     clear_pads(top)
-    emit = emitter(odd, pair_ref, chip_ref, rows)
     last = planes - 1
+
+    def emit(slot, row, below, above):
+        chip_ref[message_rows(slot, row, rows), :] = jnp.where(odd, above, below)
+
     for copy in copies[:2]:
         copy.wait()
     for row in chunks(rows):
@@ -221,37 +219,50 @@
     return 0.0, 0.0
 
 
-def follow_kernel(
-    source_ref, medium_ref, meta_ref, pair_ref, chip_ref, pair_two_ref, chip_two_ref, scale_ref, one, two, held
-):
+def follow_kernel(source_ref, medium_ref, meta_ref, pair_ref, chip_ref, chip_two_ref, scale_ref, one, two, held):
     planes, rows, width = medium_ref.shape[1:]
     lane = lane_of(width)
     odd, first_scale, _ = parity_and_ends()
     for ref in (one, two, held):
         clear_pads(ref)
+
+    def emitter(slots, to_chip):
+        def emit(slot, row, below, above):
+            pair_ref[message_rows(slots + slot, row, rows), :] = jnp.where(odd, below, above)
+            if to_chip is not None:
+                to_chip[message_rows(slot, row, rows), :] = jnp.where(odd, above, below)
+
+        return emit
+
     first_sweep(source_ref, medium_ref, scale_ref, one, planes, rows)
     sweep_slab(
         one, held, two, source_ref, medium_ref, scale_ref, sweep_steps[1], no_sums, no_plane, first_scale,
         planes, rows, lane,
     )
-    emit_level(emitter(odd, pair_ref, chip_ref, rows), two, planes, rows, lane)
-    for ref in (pair_ref, chip_ref):
-        ref[pl.ds(4 * rows, PAD), :] = meta_ref[...]
+    emit_level(emitter(6, chip_ref), two, planes, rows, lane)
+    emit_level(emitter(0, None), one, planes, rows, lane)
+    emit = emitter(4, None)
+    for row in chunks(rows):
+        for k in range(2):
+            here = pl.ds(row, ROWS)
+            emit(k, row, medium_ref[k, 0, here, :], medium_ref[k, planes - 1, here, :])
+    chip_ref[pl.ds(4 * rows, PAD), :] = meta_ref[...]
+    pair_ref[pl.ds(14 * rows, PAD), :] = meta_ref[...]
     sweep_slab(
         two, held, one, source_ref, medium_ref, scale_ref, sweep_steps[2], no_sums, no_plane, first_scale,
         planes, rows, lane, wanted=sorted({0, planes - 1}),
     )
-    emit_level(emitter(odd, pair_two_ref, chip_two_ref, rows), one, planes, rows, lane)
-
-
-def readers(odd, pair_ref, chip_ref, rows):
+    emit_level(emitter(10, chip_two_ref), one, planes, rows, lane)
+
+
+def readers(odd, pair_ref, chip_ref, rows, first):
     def from_below(slot, row):
-        here = pl.ds(slot * rows + row, ROWS)
-        return jnp.where(odd, pair_ref[here, :], chip_ref[here, :])
+        pair, chip = pair_ref[message_rows(first + slot, row, rows), :], chip_ref[message_rows(slot, row, rows), :]
+        return jnp.where(odd, pair, chip)
 
     def from_above(slot, row):
-        here = pl.ds(slot * rows + row, ROWS)
-        return jnp.where(odd, chip_ref[here, :], pair_ref[here, :])
+        pair, chip = pair_ref[message_rows(first + slot, row, rows), :], chip_ref[message_rows(slot, row, rows), :]
+        return jnp.where(odd, chip, pair)
 
     return from_below, from_above
 
@@ -271,17 +282,16 @@
             put(moment_ref, (c, i), row, value)
 
 
-def middle_kernel(
-    source_ref, medium_ref, saved_ref, pair_ref, chip_ref, pair_one_ref, chip_one_ref,
-    state_ref, held, extra_ref, moment_ref, one, two, scale_ref, delta_low, delta_high, delta_two,
+def early_kernel(
+    source_ref, medium_ref, pair_ref, chip_ref, two, scale_ref, extra_ref, one, held, delta_low, delta_high, delta_two,
 ):
     planes, rows, width = medium_ref.shape[1:]
     lane = lane_of(width)
     odd, first_scale, last_scale = parity_and_ends()
-    for ref in (one, two, state_ref, held, delta_low, delta_high, delta_two, moment_ref):
+    for ref in (one, two, held, delta_low, delta_high, delta_two):
         clear_pads(ref)
     first_sweep(source_ref, medium_ref, scale_ref, one, planes, rows)
-    from_below, from_above = readers(odd, pair_ref, chip_ref, rows)
+    from_below, from_above = readers(odd, pair_ref, chip_ref, rows, 0)
 
     for row in chunks(rows):
         sums = edge_sums(lambda c, s: rows_at(one, (c, planes - 1), row, s), lane)
@@ -318,9 +328,12 @@
         for c in range(6):
             put(delta_two, (c,), row, new[c])
     for row in chunks(rows):
-        sums = edge_sums(lambda c, s: rows_at(delta_two, (c,), row, s), lane)
-        for k in range(4):
-            extra_ref[k, pl.ds(row, ROWS), :] = sums[k]
+        for level, deltas in enumerate((delta_low, delta_two)):
+            sums = edge_sums(lambda c, s: rows_at(deltas, (c,), row, s), lane)
+            for k in range(4):
+                extra_ref[8 * level + k, pl.ds(row, ROWS), :] = sums[k]
+        for k, c in enumerate((1, 2, 4, 5)):
+            extra_ref[4 + k, pl.ds(row, ROWS), :] = rows_at(delta_high, (c,), row)
     for row in chunks(rows):
         for part in (0, 3):
             ey, ez = rows_at(delta_high, (part + 1,), row), rows_at(delta_high, (part + 2,), row)
@@ -339,24 +352,34 @@
             image[part + 1] = 2.0 * ey - sums[k] - (behind(hx, lane) - hx)
             image[part + 2] = (rows_at(held, (part, 1), row, -1) - hx) - sums[k + 1] + 2.0 * ez
         for k, c in enumerate((1, 2)):
-            extra_ref[4 + k, here, :] = center[c] - scale * (image[c] + real * center[c] - imag * center[c + 3])
-            extra_ref[6 + k, here, :] = center[c + 3] - scale * (
+            extra_ref[12 + k, here, :] = center[c] - scale * (image[c] + real * center[c] - imag * center[c + 3])
+            extra_ref[14 + k, here, :] = center[c + 3] - scale * (
                 image[c + 3] + real * center[c + 3] + imag * center[c]
             )
 
-    below_one, above_one = readers(odd, pair_one_ref, chip_one_ref, rows)
+
+def middle_kernel(
+    source_ref, medium_ref, saved_ref, pair_ref, chip_ref, state_in_ref, scale_ref, extra_ref,
+    state_ref, held, moment_ref, one,
+):
+    planes, rows, width = medium_ref.shape[1:]
+    lane = lane_of(width)
+    odd, first_scale, _ = parity_and_ends()
+    for ref in (one, state_ref, held, moment_ref):
+        clear_pads(ref)
+    from_below, from_above = readers(odd, pair_ref, chip_ref, rows, 6)
 
     def low(part, row):
         k = 2 * (part // 3)
-        ex = rows_at(delta_low, (part,), row)
-        gy = below_one(k, row) + rows_at(delta_low, (part + 1,), row) + (rows_at(delta_low, (part,), row, 1) - ex)
-        gz = below_one(k + 1, row) + rows_at(delta_low, (part + 2,), row) + (ahead(ex, lane) - ex)
-        return gy, gz
+        here = pl.ds(row, ROWS)
+        return from_below(k, row) + extra_ref[k, here, :], from_below(k + 1, row) + extra_ref[k + 1, here, :]
+
+    def high(c, row):
+        return from_above(WHERE_YZ[c], row) + extra_ref[4 + WHERE_YZ[c], pl.ds(row, ROWS), :]
 
     sweep_slab(
-        two, held, state_ref, source_ref, medium_ref, scale_ref, sweep_steps[2],
-        low, lambda c, row: above_one(WHERE_YZ[c], row) + rows_at(delta_high, (c,), row),
-        first_scale, planes, rows, lane,
+        state_in_ref, held, state_ref, source_ref, medium_ref, scale_ref, sweep_steps[2], low, high, first_scale,
+        planes, rows, lane,
     )
     inner = range(1, planes - 1)
     sweep_slab(
@@ -368,13 +391,13 @@
 
 
 def window_kernel(
-    source_ref, medium_ref, saved_ref, keep_ref, offset_ref, edge_ref, pair_ref, chip_ref, state_ref, held_ref,
-    extra_ref, moment_in_ref, send_ref, stay_ref, held, two, scale_ref, moment, window,
+    source_ref, medium_ref, saved_ref, owner_ref, edge_ref, pair_ref, chip_ref, state_ref, held_ref, scale_ref,
+    extra_ref, moment_in_ref, send_ref, stay_ref, held, two, moment, window,
 ):
     planes, rows, width = medium_ref.shape[1:]
     lane = lane_of(width)
     odd, first_scale, _ = parity_and_ends()
-    from_below, from_above = readers(odd, pair_ref, chip_ref, rows)
+    from_below, from_above = readers(odd, pair_ref, chip_ref, rows, 10)
     clear_pads(held)
     clear_pads(moment)
     ends = sorted({0, planes - 1})
@@ -384,13 +407,13 @@
         for part in (0, 3):
             k = 2 * (part // 3)
             ey, ez = rows_at(state_ref, (part + 1, 0), row), rows_at(state_ref, (part + 2, 0), row)
-            gy = from_below(k, row) + extra_ref[k, here, :]
-            gz = from_below(k + 1, row) + extra_ref[k + 1, here, :]
+            gy = from_below(k, row) + extra_ref[8 + k, here, :]
+            gz = from_below(k + 1, row) + extra_ref[9 + k, here, :]
             put(held, (part + 1, 0), row, first_scale * (gz - ez))
             put(held, (part + 2, 0), row, first_scale * (ey - gy))
         values = curl(
             lambda c, s: rows_at(state_ref, (c, planes - 1), row, s),
-            lambda c: from_above(WHERE_YZ[c], row) + extra_ref[4 + WHERE_YZ[c], here, :],
+            lambda c: from_above(WHERE_YZ[c], row) + extra_ref[12 + WHERE_YZ[c], here, :],
             lane,
         )
         for c in range(6):
@@ -410,7 +433,7 @@
             real, imag = medium_ref[0, i, here, :], medium_ref[1, i, here, :]
             new = updated(
                 [rows_at(state_ref, (c, i), row) for c in range(6)], image,
-                [source_ref[0, c, i, here, :] for c in range(6)], real, imag, sweep_steps[3] / (4.0 + real),
+                [source_ref[0, c, i, here, :] for c in range(6)], real, imag, sweep_steps[3] * scale_ref[i, here, :],
             )
             for c in range(6):
                 put(two, (c, i), row, new[c])
@@ -432,17 +455,17 @@
             return moment_rows(1, i, row) + (moment_rows(2, i, row) + moment_rows(2, i, row, 1))
 
         lower = side(0)
-        add(edge_ref[0, here, :] * lower, edge_ref[1, here, :], 0)
+        add(lower, edge_ref[here, :], 0)
         for i in range(planes):
             cell = moment_rows(0, i, row) + moment_rows(0, i, row, 1) + lower
             if i + 1 < planes:
                 lower = side(i + 1)
                 cell = cell + lower
-            add(keep_ref[i, here, :] * cell, offset_ref[i, here, :], 1)
+            add(cell, owner_ref[i, here, :], 1)
         for k in range(2 * REACH + 2):
             window[k, here, :] = sums[k]
     for k in range(2 * REACH + 2):
-        both = window[k, pl.ds(0, rows // 2, stride=2), :] + window[k, pl.ds(1, rows // 2, stride=2), :]
+        both = 0.25 * (window[k, pl.ds(0, rows // 2, stride=2), :] + window[k, pl.ds(1, rows // 2, stride=2), :])
         if k % 2 == 0:
             send_ref[k // 2] = both
         else:
@@ -494,7 +517,6 @@
     index = lax.axis_index("space")
     odd = lax.rem(index, 2) == 1
     other = core_swap(send)
-    from_far = lax.ppermute(send[0], "space", [(i, i - 3) for i in range(4, size, 2)])
     below = stay[0] + jnp.where(odd, other[1], other[0])
     here = stay[1] + jnp.where(odd, other[2], other[1])
     above = stay[2] + jnp.where(odd, 0.0, other[2])
@@ -509,9 +531,10 @@
             partner = ((c + 1) ^ 1) - 1
             if 0 <= partner < chips:
                 outer.append((2 * c + core, 2 * partner + core))
+    from_inner = lax.ppermute(jnp.where(upward, above, below), "space", inner)
     from_outer = lax.ppermute(jnp.where(upward, below, above), "space", outer)
-    from_inner = lax.ppermute(jnp.where(upward, above, below), "space", inner)
-    return here + from_far + from_outer + from_inner
+    from_far = lax.ppermute(other[0], "space", [(i, i - 4) for i in range(5, size, 2)])
+    return here + from_inner + from_outer + from_far
 
 
 def transposed_smooth(summed, rough):
@@ -534,6 +557,7 @@
 def slab(adjoint_source, forward_field, medium, plane_map, depth, rough):
     planes, rows, width = medium.shape[1:]
     index = lax.axis_index("space")
+    size = lax.axis_size("space") + REACH
     plane = (rows + 2 * PAD, width)
     state = (6, planes) + plane
     held = (6, planes + 1) + plane
@@ -541,50 +565,49 @@
     hbm = pl.BlockSpec(memory_space=pltpu.HBM)
     columns = pltpu.VMEM((planes, rows), jnp.int32)
     given = (adjoint_source, medium, depth, plane_map)
-    pair, chip, adjoint_source, medium, meta = call(
+    chip, adjoint_source, medium, meta = call(
         start_kernel,
-        [(6 * rows, width)] * 2 + [adjoint_source.shape, medium.shape, (PAD, width)],
+        [(6 * rows, width), adjoint_source.shape, medium.shape, (PAD, width)],
         [(6,) + plane, columns, columns, pltpu.SemaphoreType.DMA((2 * planes + 2,))],
         tuple(pltpu.with_memory_space_constraint(a, pltpu.HBM) for a in given),
         in_specs=[hbm] * 4,
     )
     chip = chip_swap(chip)
-    pair = core_swap(pair)
-    pair_one, chip_one, pair_two, chip_two = call(
+    pair, chip_one, chip_two = call(
         follow_kernel,
-        [(4 * rows + PAD, width)] * 2 + [(4 * rows, width)] * 2,
+        [(14 * rows + PAD, width), (4 * rows + PAD, width), (4 * rows, width)],
         [scale, state, state, held],
         (adjoint_source, medium, meta),
     )
     chip_one = chip_swap(chip_one)
-    pair_one = core_swap(pair_one)
     chip_two = chip_swap(chip_two)
-    pair_two = core_swap(pair_two)
+    pair = core_swap(pair)
 
     here = index.astype(jnp.float32)
     levels = depth[0].astype(jnp.float32)
     owners = plane_map.astype(jnp.float32)
     position = lax.broadcasted_iota(jnp.int32, (planes, rows, width), 2).astype(jnp.float32)
-    keep = jnp.where(position < levels[:, :, None], 0.25, 0.0)
-    offset = jnp.broadcast_to((owners - here)[:, :, None], (planes, rows, width))
-    below = jnp.where(lax.rem(index, 2) == 1, pair_one[4 * rows :], chip_one[4 * rows :])
-    edge = jnp.stack(
-        [
-            jnp.where(position[0] < below[0, :rows, None], 0.25, 0.0),
-            jnp.broadcast_to((below[1, :rows] - here)[:, None], (rows, width)),
-        ]
-    )
-    middle, curls, extra, moment = call(
+    outside = float(size)
+    owner = jnp.where(position < levels[:, :, None], (owners - here)[:, :, None], outside)
+    below = jnp.where(lax.rem(index, 2) == 1, pair[14 * rows :], chip_one[4 * rows :])
+    edge = jnp.where(position[0] < below[0, :rows, None], (below[1, :rows] - here)[:, None], outside)
+    first, scales, extra = call(
+        early_kernel,
+        [state, scale, (16, rows, width)],
+        [state, held, (6,) + plane, (6,) + plane, (6,) + plane],
+        (adjoint_source, medium, pair, chip),
+    )
+    middle, curls, moment = call(
         middle_kernel,
-        [state, held, (8, rows, width), (3, planes) + plane],
-        [state, state, scale, (6,) + plane, (6,) + plane, (6,) + plane],
-        (adjoint_source, medium, forward_field, pair, chip, pair_one, chip_one),
+        [state, held, (3, planes) + plane],
+        [state],
+        (adjoint_source, medium, forward_field, pair, chip_one, first, scales, extra),
     )
     send, stay = call(
         window_kernel,
         [(REACH + 1, rows // 2, width), (REACH + 1, rows // 2, width)],
-        [(6, 2) + plane, state, scale, (3, planes) + plane, (2 * REACH + 2, rows, width)],
-        (adjoint_source, medium, forward_field, keep, offset, edge, pair_two, chip_two, middle, curls, extra, moment),
+        [(6, 2) + plane, state, (3, planes) + plane, (2 * REACH + 2, rows, width)],
+        (adjoint_source, medium, forward_field, owner, edge, pair, chip_two, middle, curls, scales, extra, moment),
     )
     total = sum_over_groups(gather_owned(send, stay))
     return transposed_smooth(total[None], rough)

time: 34 us -> 32.4 us (0.953)
  the two profiles are of different devices: /device:TPU:8 before, /device:TPU:17 now
where the time goes in v3:
time: 32.4 us; the launch traced here: 32.1 us
  starting transfers between devices  15.9 us (49%)
  waiting for transfers between devices  10.1 us (31%)
  Pallas kernels  4.84 us (15%)
  other arithmetic  0.97 us (3%)
    ppermute x3, starting transfers between devices, chip_swap(): return lax.ppermute(value, 'space', pairs)  8.61 us
    pallas_call x5, Pallas kernels, call(): pl.pallas_call(kernel, out_shape=[jax.ShapeDtypeStruct(s, jnp.float32) fo...  4.84 us
    ppermute x3, waiting for transfers between devices, chip_swap(): return lax.ppermute(value, 'space', pairs)  4.56 us
    ppermute x1, starting transfers between devices, gather_owned(): from_outer = lax.ppermute(jnp.where(upward, below, above), 'space', outer)  3.12 us
    ppermute x1, waiting for transfers between devices, gather_owned(): lax.ppermute(other[0], 'space', [(i, i - 4) for i in range(5, size, 2)])  2.25 us
    ppermute x1, starting transfers between devices, gather_owned(): lax.ppermute(other[0], 'space', [(i, i - 4) for i in range(5, size, 2)])  1.92 us
    ppermute x1, waiting for transfers between devices, sum_over_groups(): lax.ppermute(value, 'src', [(i, i ^ step) for i in range(size)])  1.84 us
    ppermute x1, starting transfers between devices, sum_over_groups(): lax.ppermute(value, 'src', [(i, i ^ step) for i in range(size)])  1.28 us
  transfers between devices with their start and end apart: 9, of which 5 were waited for; matrix products, arithmetic and copies ran while one was open for 1% of the time, Pallas kernels for 6%

profile of v3, /device:TPU:17, one launch (start us, length us, event | category | flops | bytes accessed | tf_op | source)
XLA Modules:
  0.0 32.1 jit_solution(8469150064085133882)
XLA Ops:
  0.0 1.4 %shard_map.64 = (f32[384,128]{1,0:T(8,128)S(1)}, f32[1,6,4,64,128]{4,3,2,1,0:T(8,128)S(1)}, f32[2,4,64,128]{3,2,1,0:T(8,128)S(1)}, f32[8,128]{1,0:T(8,128)S(1)}) custom-call(f32[1,6,4,64,128]{4,3,2,1,0:T(8,128)} %source_hbm.1, f32[2,4,64,128]{3,2,1,0:T(8,128)} %medium_hbm.1, s32[1,4,64]{2,1,0:T(4,128)} %depth_hbm.1, s32[4,64]{1,0:T(4,128)} %map_hbm.1), custom_call_target="tpu_custom_call" | custom-call | flops 1048576 | bytes 1048576 | tf_op jit(solution)/shard_map/pallas_call | solution.py:480
  1.4 0.0 copy-start
  1.4 0.9 %shard_map.65 = (f32[904,128]{1,0:T(8,128)S(1)}, f32[264,128]{1,0:T(8,128)S(1)}, f32[256,128]{1,0:T(8,128)S(1)}) custom-call(f32[1,6,4,64,128]{4,3,2,1,0:T(8,128)S(1)} %get-tuple-element.20.source_ref, f32[2,4,64,128]{3,2,1,0:T(8,128)S(1)} %get-tuple-element.21.medium_ref, f32[8,128]{1,0:T(8,128)S(1)} %get-tuple-element.22.meta_ref), custom_call_target="tpu_custom_call" | custom-call | flops 1048576 | bytes 1048576 | tf_op jit(solution)/shard_map/pallas_call | solution.py:480
  2.4 0.7 %collective-permute-start = (f32[904,128]{1,0:T(8,128)S(1)}, f32[904,128]{1,0:T(8,128)S(1)}, u32[]{:S(2)}, u32[]{:S(2)}) collective-permute-start(f32[904,128]{1,0:T(8,128)S(1)} %get-tuple-element.23), channel_id=1, source_target_pairs={{0,1},{1,0},{2,3},{3,2},{4,5},{5,4},{6,7},{7,6},{8,9},{9,8},{10,11... | collective-permute-start | bytes 1388552 | tf_op jit(solution)/shard_map/ppermute | solution.py:493
  3.1 3.0 %collective-permute-start.3 = (f32[384,128]{1,0:T(8,128)S(1)}, f32[384,128]{1,0:T(8,128)S(1)}, u32[]{:S(2)}, u32[]{:S(2)}) collective-permute-start(f32[384,128]{1,0:T(8,128)S(1)} %get-tuple-element.26), channel_id=1, source_target_pairs={{1,2},{2,1},{3,4},{4,3},{5,6},{6,5},{7,8},{8,7},{9,10},{10,9},{11,... | collective-permute-start | bytes 589832 | tf_op jit(solution)/shard_map/ppermute | solution.py:501
  6.2 2.5 %collective-permute-start.1 = (f32[264,128]{1,0:T(8,128)S(1)}, f32[264,128]{1,0:T(8,128)S(1)}, u32[]{:S(2)}, u32[]{:S(2)}) collective-permute-start(f32[264,128]{1,0:T(8,128)S(1)} %get-tuple-element.24), channel_id=1, source_target_pairs={{1,2},{2,1},{3,4},{4,3},{5,6},{6,5},{7,8},{8,7},{9,10},{10,9},{11,... | collective-permute-start | bytes 405512 | tf_op jit(solution)/shard_map/ppermute | solution.py:501
  8.7 3.1 %collective-permute-start.2 = (f32[256,128]{1,0:T(8,128)S(1)}, f32[256,128]{1,0:T(8,128)S(1)}, u32[]{:S(2)}, u32[]{:S(2)}) collective-permute-start(f32[256,128]{1,0:T(8,128)S(1)} %get-tuple-element.25), channel_id=1, source_target_pairs={{1,2},{2,1},{3,4},{4,3},{5,6},{6,5},{7,8},{8,7},{9,10},{10,9},{11,... | collective-permute-start | bytes 393224 | tf_op jit(solution)/shard_map/ppermute | solution.py:501
  11.7 0.0 copy-done.2
  11.8 0.0 copy-done.3
  11.8 0.1 compare_select_fusion.owner_ref
  11.9 4.6 %collective-permute-done.1.chip_ref = f32[264,128]{1,0:T(8,128)S(1)} collective-permute-done((f32[264,128]{1,0:T(8,128)S(1)}, f32[264,128]{1,0:T(8,128)S(1)}, u32[]{:S(2)}, u32[]{:S(2)}) %collective-permute-start.1) | collective-permute-done | bytes 135200 | tf_op jit(solution)/shard_map/ppermute | solution.py:501
  16.5 0.0 collective-permute-done.pair_ref
  16.5 0.0 collective-permute-done.3.chip_ref
  16.5 0.9 %shard_map.66 = (f32[6,4,80,128]{3,2,1,0:T(8,128)S(1)}, f32[4,64,128]{2,1,0:T(8,128)S(1)}, f32[16,64,128]{2,1,0:T(8,128)S(1)}) custom-call(f32[1,6,4,64,128]{4,3,2,1,0:T(8,128)S(1)} %get-tuple-element.20.source_ref, f32[2,4,64,128]{3,2,1,0:T(8,128)S(1)} %get-tuple-element.21.medium_ref, f32[904,128]{1,0:T(8,128)S(1)} %collective-permute-done.pair_ref, ...), custom_call_target="tpu_custom_call" | custom-call | flops 1048576 | bytes 1048576 | tf_op jit(solution)/shard_map/pallas_call | solution.py:480
  17.5 0.0 copy-done
  17.5 1.1 %shard_map.67 = (f32[6,4,80,128]{3,2,1,0:T(8,128)S(1)}, f32[6,5,80,128]{3,2,1,0:T(8,128)S(1)}, f32[3,4,80,128]{3,2,1,0:T(8,128)S(1)}) custom-call(f32[1,6,4,64,128]{4,3,2,1,0:T(8,128)S(1)} %get-tuple-element.20.source_ref, f32[2,4,64,128]{3,2,1,0:T(8,128)S(1)} %get-tuple-element.21.medium_ref, bf16[1,6,4,64,128]{4,3,2,1,0:T(8,128)(2,1)S(1)} %copy-done, ...), custom_call_target="tpu_custom_call" | custom-call | flops 1048576 | bytes 1048576 | tf_op jit(solution)/shard_map/pallas_call | solution.py:480
  18.6 0.1 compare_select_fusion.1.edge_ref
  18.7 0.0 collective-permute-done.2.chip_ref
  18.7 0.0 copy-start.1
  18.7 0.5 %shard_map.68 = (f32[3,32,128]{2,1,0:T(8,128)S(1)}, f32[3,32,128]{2,1,0:T(8,128)S(1)}) custom-call(f32[1,6,4,64,128]{4,3,2,1,0:T(8,128)S(1)} %get-tuple-element.20.source_ref, f32[2,4,64,128]{3,2,1,0:T(8,128)S(1)} %get-tuple-element.21.medium_ref, bf16[1,6,4,64,128]{4,3,2,1,0:T(8,128)(2,1)S(1)} %copy-done, f32[4,64,128]{2,1,0:T(8,128)S(1)} %compare_select_fusion.owner_ref, ...), custom_call_target="tpu_custom_call" | custom-call | flops 1048576 | bytes 1048576 | tf_op jit(solution)/shard_map/pallas_call | solution.py:480
  19.2 0.1 collective-permute-start.4
  19.3 1.2 %collective-permute-done.4 = f32[3,32,128]{2,1,0:T(8,128)S(1)} collective-permute-done((f32[3,32,128]{2,1,0:T(8,128)S(1)}, f32[3,32,128]{2,1,0:T(8,128)S(1)}, u32[]{:S(2)}, u32[]{:S(2)}) %collective-permute-start.4) | collective-permute-done | bytes 49184 | tf_op jit(solution)/shard_map/ppermute | solution.py:493
  20.5 0.2 collective-permute-start.5
  20.7 3.1 %collective-permute-start.6 = (f32[32,128]{1,0:T(8,128)S(1)}, f32[32,128]{1,0:T(8,128)S(1)}, u32[]{:S(2)}, u32[]{:S(2)}) collective-permute-start(f32[32,128]{1,0:T(8,128)S(1)} %get-tuple-element.45), channel_id=1, source_target_pairs={{2,4},{3,5},{4,2},{5,3},{6,8},{7,9},{8,6},{9,7},{10,12},{11,13},{1... | collective-permute-start | bytes 49160 | tf_op jit(solution)/shard_map/ppermute | solution.py:535
  23.8 1.9 %collective-permute-start.7 = (f32[32,128]{1,0:T(8,128)S(1)}, f32[32,128]{1,0:T(8,128)S(1)}, u32[]{:S(2)}, u32[]{:S(2)}) collective-permute-start(f32[32,128]{1,0:T(8,128)S(1)} %slice_bitcast_fusion), channel_id=1, source_target_pairs={{5,1},{7,3},{9,5},{11,7},{13,9},{15,11},{21,17},{23,19},{25,21},{2... | collective-permute-start | bytes 49160 | tf_op jit(solution)/shard_map/ppermute | solution.py:536
  25.7 0.0 collective-permute-done.5
  25.7 0.3 collective-permute-done.6
  26.0 2.3 %collective-permute-done.7 = f32[32,128]{1,0:T(8,128)S(1)} collective-permute-done((f32[32,128]{1,0:T(8,128)S(1)}, f32[32,128]{1,0:T(8,128)S(1)}, u32[]{:S(2)}, u32[]{:S(2)}) %collective-permute-start.7) | collective-permute-done | bytes 16416 | tf_op jit(solution)/shard_map/ppermute | solution.py:536
  28.3 1.3 %collective-permute-start.8 = (f32[32,128]{1,0:T(8,128)S(1)}, f32[32,128]{1,0:T(8,128)S(1)}, u32[]{:S(2)}, u32[]{:S(2)}) collective-permute-start(f32[32,128]{1,0:T(8,128)S(1)} %fusion.17), channel_id=1, source_target_pairs={{0,16},{16,0},{1,17},{17,1},{2,18},{18,2},{3,19},{19,3},{4,20},{20... | collective-permute-start | bytes 49160 | tf_op jit(solution)/shard_map/ppermute | solution.py:510
  29.6 1.8 %collective-permute-done.8 = f32[32,128]{1,0:T(8,128)S(1)} collective-permute-done((f32[32,128]{1,0:T(8,128)S(1)}, f32[32,128]{1,0:T(8,128)S(1)}, u32[]{:S(2)}, u32[]{:S(2)}) %collective-permute-start.8) | collective-permute-done | bytes 16416 | tf_op jit(solution)/shard_map/ppermute | solution.py:510
  31.4 0.0 copy-done.1
  31.4 0.7 %fusion.7 = f32[1,32,128]{2,1,0:T(8,128)} fusion(f32[1,32,128]{2,1,0:T(8,128)S(1)} %get-tuple-element.43, f32[1,32,128]{2,1,0:T(8,128)S(1)} %get-tuple-element.42, f32[1,32,128]{2,1,0:T(8,128)S(1)} %get-tuple-element.41, f32[1,32,128]{2,1,0:T(8,128)S(1)} %get-tuple-element.40, f32[1,32,128]{2,1,0:T(8,128)S(1)} %get-tuple-element.39, ...), kind=kLoop, calls=%fused_computation.17 | loop fusion | flops 36864 | bytes 180224 | tf_op jit(solution)/shard_map/add | solution.py:549
  (12 shorter events, 0.1 us)
Async XLA Ops:
  0.0 11.8 %copy-start.2 = (s32[1,4,64]{2,1,0:T(4,128)S(1)}, s32[1,4,64]{2,1,0:T(4,128)}, u32[]{:S(2)}) copy-start(s32[1,4,64]{2,1,0:T(4,128)} %depth_hbm.1) | copy-start | bytes 3076
  0.0 11.8 %copy-start.3 = (s32[4,64]{1,0:T(4,128)S(1)}, s32[4,64]{1,0:T(4,128)}, u32[]{:S(2)}) copy-start(s32[4,64]{1,0:T(4,128)} %map_hbm.1) | copy-start | bytes 3076
  1.4 16.0 %copy-start = (bf16[1,6,4,64,128]{4,3,2,1,0:T(8,128)(2,1)S(1)}, bf16[1,6,4,64,128]{4,3,2,1,0:T(8,128)(2,1)}, u32[]{:S(2)}) copy-start(bf16[1,6,4,64,128]{4,3,2,1,0:T(8,128)(2,1)} %saved_ref.3) | copy-start | bytes 1179652
  2.4 14.1 %collective-permute-start = (f32[904,128]{1,0:T(8,128)S(1)}, f32[904,128]{1,0:T(8,128)S(1)}, u32[]{:S(2)}, u32[]{:S(2)}) collective-permute-start(f32[904,128]{1,0:T(8,128)S(1)} %get-tuple-element.23), channel_id=1, source_target_pairs={{0,1},{1,0},{2,3},{3,2},{4,5},{5,4},{6,7},{7,6},{8,9},{9,8},{10,11... | collective-permute-start | bytes 1388552 | tf_op jit(solution)/shard_map/ppermute | solution.py:493
  3.1 13.4 %collective-permute-start.3 = (f32[384,128]{1,0:T(8,128)S(1)}, f32[384,128]{1,0:T(8,128)S(1)}, u32[]{:S(2)}, u32[]{:S(2)}) collective-permute-start(f32[384,128]{1,0:T(8,128)S(1)} %get-tuple-element.26), channel_id=1, source_target_pairs={{1,2},{2,1},{3,4},{4,3},{5,6},{6,5},{7,8},{8,7},{9,10},{10,9},{11,... | collective-permute-start | bytes 589832 | tf_op jit(solution)/shard_map/ppermute | solution.py:501
  6.2 10.3 %collective-permute-start.1 = (f32[264,128]{1,0:T(8,128)S(1)}, f32[264,128]{1,0:T(8,128)S(1)}, u32[]{:S(2)}, u32[]{:S(2)}) collective-permute-start(f32[264,128]{1,0:T(8,128)S(1)} %get-tuple-element.24), channel_id=1, source_target_pairs={{1,2},{2,1},{3,4},{4,3},{5,6},{6,5},{7,8},{8,7},{9,10},{10,9},{11,... | collective-permute-start | bytes 405512 | tf_op jit(solution)/shard_map/ppermute | solution.py:501
  8.7 10.0 %collective-permute-start.2 = (f32[256,128]{1,0:T(8,128)S(1)}, f32[256,128]{1,0:T(8,128)S(1)}, u32[]{:S(2)}, u32[]{:S(2)}) collective-permute-start(f32[256,128]{1,0:T(8,128)S(1)} %get-tuple-element.25), channel_id=1, source_target_pairs={{1,2},{2,1},{3,4},{4,3},{5,6},{6,5},{7,8},{8,7},{9,10},{10,9},{11,... | collective-permute-start | bytes 393224 | tf_op jit(solution)/shard_map/ppermute | solution.py:501
  18.7 12.7 %copy-start.1 = (f32[9,1,32,128]{3,2,1,0:T(8,128)S(1)}, f32[9,1,32,128]{3,2,1,0:T(8,128)}, u32[]{:S(2)}) copy-start(f32[9,1,32,128]{3,2,1,0:T(8,128)} %param.11) | copy-start | bytes 442372
  19.2 1.3 %collective-permute-start.4 = (f32[3,32,128]{2,1,0:T(8,128)S(1)}, f32[3,32,128]{2,1,0:T(8,128)S(1)}, u32[]{:S(2)}, u32[]{:S(2)}) collective-permute-start(f32[3,32,128]{2,1,0:T(8,128)S(1)} %get-tuple-element.34), channel_id=1, source_target_pairs={{0,1},{1,0},{2,3},{3,2},{4,5},{5,4},{6,7},{7,6},{8,9},{9,8},{10,11... | collective-permute-start | bytes 147464 | tf_op jit(solution)/shard_map/ppermute | solution.py:493
  20.5 5.3 %collective-permute-start.5 = (f32[32,128]{1,0:T(8,128)S(1)}, f32[32,128]{1,0:T(8,128)S(1)}, u32[]{:S(2)}, u32[]{:S(2)}) collective-permute-start(f32[32,128]{1,0:T(8,128)S(1)} %get-tuple-element.44), channel_id=1, source_target_pairs={{0,2},{1,3},{2,0},{3,1},{4,6},{5,7},{6,4},{7,5},{8,10},{9,11},{10,... | collective-permute-start | bytes 49160 | tf_op jit(solution)/shard_map/ppermute | solution.py:534
  20.7 5.4 %collective-permute-start.6 = (f32[32,128]{1,0:T(8,128)S(1)}, f32[32,128]{1,0:T(8,128)S(1)}, u32[]{:S(2)}, u32[]{:S(2)}) collective-permute-start(f32[32,128]{1,0:T(8,128)S(1)} %get-tuple-element.45), channel_id=1, source_target_pairs={{2,4},{3,5},{4,2},{5,3},{6,8},{7,9},{8,6},{9,7},{10,12},{11,13},{1... | collective-permute-start | bytes 49160 | tf_op jit(solution)/shard_map/ppermute | solution.py:535
  23.8 4.5 %collective-permute-start.7 = (f32[32,128]{1,0:T(8,128)S(1)}, f32[32,128]{1,0:T(8,128)S(1)}, u32[]{:S(2)}, u32[]{:S(2)}) collective-permute-start(f32[32,128]{1,0:T(8,128)S(1)} %slice_bitcast_fusion), channel_id=1, source_target_pairs={{5,1},{7,3},{9,5},{11,7},{13,9},{15,11},{21,17},{23,19},{25,21},{2... | collective-permute-start | bytes 49160 | tf_op jit(solution)/shard_map/ppermute | solution.py:536
  28.3 3.1 %collective-permute-start.8 = (f32[32,128]{1,0:T(8,128)S(1)}, f32[32,128]{1,0:T(8,128)S(1)}, u32[]{:S(2)}, u32[]{:S(2)}) collective-permute-start(f32[32,128]{1,0:T(8,128)S(1)} %fusion.17), channel_id=1, source_target_pairs={{0,16},{16,0},{1,17},{17,1},{2,18},{18,2},{3,19},{19,3},{4,20},{20... | collective-permute-start | bytes 49160 | tf_op jit(solution)/shard_map/ppermute | solution.py:510

commit v4 on v3

--- a/solution.py
+++ b/solution.py
@@ -136,14 +136,13 @@
                 put(result, (c, i), row, new[c])
 
 
-def first_sweep(source_ref, medium_ref, scale_ref, state, planes, rows):
-    for i in range(planes):
-        for row in chunks(rows):
-            here = pl.ds(row, ROWS)
-            scale = 1.0 / (4.0 + medium_ref[0, i, here, :])
-            scale_ref[i, here, :] = scale
-            for c in range(6):
-                put(state, (c, i), row, sweep_steps[0] * source_ref[0, c, i, here, :] * scale)
+def first_sweep(source_ref, medium_ref, scale_ref, state, i, rows):
+    for row in chunks(rows):
+        here = pl.ds(row, ROWS)
+        scale = 1.0 / (4.0 + medium_ref[0, i, here, :])
+        scale_ref[i, here, :] = scale
+        for c in range(6):
+            put(state, (c, i), row, sweep_steps[0] * scale * source_ref[0, c, i, here, :])
 
 
 def parity_and_ends():
@@ -154,114 +153,106 @@
     return odd, first_scale, last_scale
 
 
-def emit_level(emit, state, planes, rows, lane):
+def emit_level(emit, first, state, planes, rows, lane):
     for row in chunks(rows):
         sums = edge_sums(lambda c, s: rows_at(state, (c, planes - 1), row, s), lane)
         bottom = [rows_at(state, (c, 0), row) for c in (1, 2, 4, 5)]
         for k in range(4):
-            emit(k, row, bottom[k], sums[k])
+            emit(first + k, row, bottom[k], sums[k])
 
 
 def message_rows(slot, row, rows):
     return pl.ds(slot * rows + row, ROWS)
 
 
+def no_plane(c, row):
+    return 0.0
+
+
+def no_sums(part, row):
+    return 0.0, 0.0
+
+
 def start_kernel(
-    source_hbm, medium_hbm, depth_hbm, map_hbm, chip_ref, source_ref, medium_ref, meta_ref, top, levels, owners, sems
+    source_hbm, medium_hbm, depth_hbm, map_hbm, chip_ref, source_ref, medium_ref, scale_ref, two, pair_ref,
+    one, held, levels, owners, sems,
 ):
     planes, rows, width = medium_ref.shape[1:]
     lane = lane_of(width)
-    odd = parity_and_ends()[0]
-    order = [planes - 1, 0] + list(range(1, planes - 1))
+    odd, first_scale, _ = parity_and_ends()
     copies = []
-    for i in order:
+    for i in range(planes):
         copies.append(pltpu.make_async_copy(medium_hbm.at[:, i], medium_ref.at[:, i], sems.at[2 * i]))
         copies.append(pltpu.make_async_copy(source_hbm.at[0, :, i], source_ref.at[0, :, i], sems.at[2 * i + 1]))
-    copies.append(pltpu.make_async_copy(depth_hbm.at[0], levels, sems.at[2 * planes]))
-    copies.append(pltpu.make_async_copy(map_hbm, owners, sems.at[2 * planes + 1]))
-    for copy in copies:
+    columns = [
+        pltpu.make_async_copy(depth_hbm.at[0], levels, sems.at[2 * planes]),
+        pltpu.make_async_copy(map_hbm, owners, sems.at[2 * planes + 1]),
+    ]
+    for copy in copies + columns:
         copy.start()
-    clear_pads(top)
+    for ref in (one, two, held):
+        clear_pads(ref)
+
+    def emit(slot, row, below, above):
+        here = message_rows(slot, row, rows)
+        pair_ref[here, :] = jnp.where(odd, below, above)
+        chip_ref[here, :] = jnp.where(odd, above, below)
+
     last = planes - 1
-
-    def emit(slot, row, below, above):
-        chip_ref[message_rows(slot, row, rows), :] = jnp.where(odd, above, below)
-
-    for copy in copies[:2]:
-        copy.wait()
+    for i in range(planes):
+        copies[2 * i].wait()
+        copies[2 * i + 1].wait()
+        first_sweep(source_ref, medium_ref, scale_ref, one, i, rows)
     for row in chunks(rows):
         here = pl.ds(row, ROWS)
-        scale = sweep_steps[0] / (4.0 + medium_ref[0, last, here, :])
-        for c in range(6):
-            put(top, (c,), row, scale * source_ref[0, c, last, here, :])
-    for copy in copies[2:4]:
-        copy.wait()
-    for row in chunks(rows):
-        here = pl.ds(row, ROWS)
-        scale = sweep_steps[0] / (4.0 + medium_ref[0, 0, here, :])
-        sums = edge_sums(lambda c, s: rows_at(top, (c,), row, s), lane)
-        for k, c in enumerate((1, 2, 4, 5)):
-            emit(k, row, scale * source_ref[0, c, 0, here, :], sums[k])
         for k in range(2):
             emit(4 + k, row, medium_ref[k, 0, here, :], medium_ref[k, last, here, :])
-    for copy in copies[4:]:
+    emit_level(emit, 0, one, planes, rows, lane)
+    sweep_slab(
+        one, held, two, source_ref, medium_ref, scale_ref, sweep_steps[1], no_sums, no_plane, first_scale,
+        planes, rows, lane,
+    )
+    emit_level(emit, 6, two, planes, rows, lane)
+    for copy in columns:
         copy.wait()
-    meta_ref[...] = jnp.zeros_like(meta_ref)
-    meta_ref[pl.ds(0, 1), pl.ds(0, rows)] = levels[pl.ds(last, 1), :].astype(jnp.float32)
-    meta_ref[pl.ds(1, 1), pl.ds(0, rows)] = owners[pl.ds(last, 1), :].astype(jnp.float32)
-
-
-def no_plane(c, row):
-    return 0.0
-
-
-def no_sums(part, row):
-    return 0.0, 0.0
-
-
-def follow_kernel(source_ref, medium_ref, meta_ref, pair_ref, chip_ref, chip_two_ref, scale_ref, one, two, held):
+    for ref in (pair_ref, chip_ref):
+        ref[pl.ds(10 * rows, PAD), :] = jnp.zeros((PAD, width), jnp.float32)
+        ref[pl.ds(10 * rows, 1), pl.ds(0, rows)] = levels[pl.ds(last, 1), :].astype(jnp.float32)
+        ref[pl.ds(10 * rows + 1, 1), pl.ds(0, rows)] = owners[pl.ds(last, 1), :].astype(jnp.float32)
+
+
+def follow_kernel(source_ref, medium_ref, scale_ref, two, pair_in_ref, chip_ref, pair_ref, one, held):
     planes, rows, width = medium_ref.shape[1:]
     lane = lane_of(width)
     odd, first_scale, _ = parity_and_ends()
-    for ref in (one, two, held):
-        clear_pads(ref)
-
-    def emitter(slots, to_chip):
-        def emit(slot, row, below, above):
-            pair_ref[message_rows(slots + slot, row, rows), :] = jnp.where(odd, below, above)
-            if to_chip is not None:
-                to_chip[message_rows(slot, row, rows), :] = jnp.where(odd, above, below)
-
-        return emit
-
-    first_sweep(source_ref, medium_ref, scale_ref, one, planes, rows)
-    sweep_slab(
-        one, held, two, source_ref, medium_ref, scale_ref, sweep_steps[1], no_sums, no_plane, first_scale,
-        planes, rows, lane,
-    )
-    emit_level(emitter(6, chip_ref), two, planes, rows, lane)
-    emit_level(emitter(0, None), one, planes, rows, lane)
-    emit = emitter(4, None)
-    for row in chunks(rows):
-        for k in range(2):
-            here = pl.ds(row, ROWS)
-            emit(k, row, medium_ref[k, 0, here, :], medium_ref[k, planes - 1, here, :])
-    chip_ref[pl.ds(4 * rows, PAD), :] = meta_ref[...]
-    pair_ref[pl.ds(14 * rows, PAD), :] = meta_ref[...]
+    clear_pads(one)
+    clear_pads(held)
     sweep_slab(
         two, held, one, source_ref, medium_ref, scale_ref, sweep_steps[2], no_sums, no_plane, first_scale,
         planes, rows, lane, wanted=sorted({0, planes - 1}),
     )
-    emit_level(emitter(10, chip_two_ref), one, planes, rows, lane)
-
-
-def readers(odd, pair_ref, chip_ref, rows, first):
+
+    def emit(slot, row, below, above):
+        here = message_rows(slot, row, rows)
+        pair_ref[here, :] = jnp.where(odd, below, above)
+        chip_ref[here, :] = jnp.where(odd, above, below)
+
+    emit_level(emit, 0, one, planes, rows, lane)
+    pair_ref[pl.ds(4 * rows, 10 * rows + PAD), :] = pair_in_ref[...]
+
+
+def readers(odd, pair_ref, pair_first, chip_ref, chip_first, rows):
+    def both(slot, row):
+        pair = pair_ref[message_rows(pair_first + slot, row, rows), :]
+        chip = chip_ref[message_rows(chip_first + slot, row, rows), :]
+        return pair, chip
+
     def from_below(slot, row):
-        pair, chip = pair_ref[message_rows(first + slot, row, rows), :], chip_ref[message_rows(slot, row, rows), :]
+        pair, chip = both(slot, row)
         return jnp.where(odd, pair, chip)
 
     def from_above(slot, row):
-        pair, chip = pair_ref[message_rows(first + slot, row, rows), :], chip_ref[message_rows(slot, row, rows), :]
+        pair, chip = both(slot, row)
         return jnp.where(odd, chip, pair)
 
     return from_below, from_above
@@ -282,16 +273,22 @@
             put(moment_ref, (c, i), row, value)
 
 
-def early_kernel(
-    source_ref, medium_ref, pair_ref, chip_ref, two, scale_ref, extra_ref, one, held, delta_low, delta_high, delta_two,
+def middle_kernel(
+    source_ref, medium_ref, saved_ref, scale_ref, pair_ref, chip_ref,
+    state_ref, held, extra_ref, moment_ref, one, two, delta_low, delta_high, delta_two,
 ):
     planes, rows, width = medium_ref.shape[1:]
     lane = lane_of(width)
     odd, first_scale, last_scale = parity_and_ends()
-    for ref in (one, two, held, delta_low, delta_high, delta_two):
+    for ref in (one, two, state_ref, held, delta_low, delta_high, delta_two, moment_ref):
         clear_pads(ref)
-    first_sweep(source_ref, medium_ref, scale_ref, one, planes, rows)
-    from_below, from_above = readers(odd, pair_ref, chip_ref, rows, 0)
+    for i in range(planes):
+        for row in chunks(rows):
+            here = pl.ds(row, ROWS)
+            scale = sweep_steps[0] * scale_ref[i, here, :]
+            for c in range(6):
+                put(one, (c, i), row, scale * source_ref[0, c, i, here, :])
+    from_below, from_above = readers(odd, pair_ref, 4, chip_ref, 0, rows)
 
     for row in chunks(rows):
         sums = edge_sums(lambda c, s: rows_at(one, (c, planes - 1), row, s), lane)
@@ -357,28 +354,18 @@
                 image[c + 3] + real * center[c + 3] + imag * center[c]
             )
 
-
-def middle_kernel(
-    source_ref, medium_ref, saved_ref, pair_ref, chip_ref, state_in_ref, scale_ref, extra_ref,
-    state_ref, held, moment_ref, one,
-):
-    planes, rows, width = medium_ref.shape[1:]
-    lane = lane_of(width)
-    odd, first_scale, _ = parity_and_ends()
-    for ref in (one, state_ref, held, moment_ref):
-        clear_pads(ref)
-    from_below, from_above = readers(odd, pair_ref, chip_ref, rows, 6)
+    below_one, above_one = readers(odd, pair_ref, 10, chip_ref, 6, rows)
 
     def low(part, row):
         k = 2 * (part // 3)
         here = pl.ds(row, ROWS)
-        return from_below(k, row) + extra_ref[k, here, :], from_below(k + 1, row) + extra_ref[k + 1, here, :]
+        return below_one(k, row) + extra_ref[k, here, :], below_one(k + 1, row) + extra_ref[k + 1, here, :]
 
     def high(c, row):
-        return from_above(WHERE_YZ[c], row) + extra_ref[4 + WHERE_YZ[c], pl.ds(row, ROWS), :]
+        return above_one(WHERE_YZ[c], row) + extra_ref[4 + WHERE_YZ[c], pl.ds(row, ROWS), :]
 
     sweep_slab(
-        state_in_ref, held, state_ref, source_ref, medium_ref, scale_ref, sweep_steps[2], low, high, first_scale,
+        two, held, state_ref, source_ref, medium_ref, scale_ref, sweep_steps[2], low, high, first_scale,
         planes, rows, lane,
     )
     inner = range(1, planes - 1)
@@ -397,7 +384,7 @@
     planes, rows, width = medium_ref.shape[1:]
     lane = lane_of(width)
     odd, first_scale, _ = parity_and_ends()
-    from_below, from_above = readers(odd, pair_ref, chip_ref, rows, 10)
+    from_below, from_above = readers(odd, pair_ref, 0, chip_ref, 0, rows)
     clear_pads(held)
     clear_pads(moment)
     ends = sorted({0, planes - 1})
@@ -565,23 +552,23 @@
     hbm = pl.BlockSpec(memory_space=pltpu.HBM)
     columns = pltpu.VMEM((planes, rows), jnp.int32)
     given = (adjoint_source, medium, depth, plane_map)
-    chip, adjoint_source, medium, meta = call(
+    first_message, last_message = (10 * rows + PAD, width), (4 * rows, width)
+    chip_one, adjoint_source, medium, scales, own, pair = call(
         start_kernel,
-        [(6 * rows, width), adjoint_source.shape, medium.shape, (PAD, width)],
-        [(6,) + plane, columns, columns, pltpu.SemaphoreType.DMA((2 * planes + 2,))],
+        [first_message, adjoint_source.shape, medium.shape, scale, state, first_message],
+        [state, held, columns, columns, pltpu.SemaphoreType.DMA((2 * planes + 2,))],
         tuple(pltpu.with_memory_space_constraint(a, pltpu.HBM) for a in given),
         in_specs=[hbm] * 4,
     )
-    chip = chip_swap(chip)
-    pair, chip_one, chip_two = call(
+    chip_one = chip_swap(chip_one)
+    chip_two, pair = call(
         follow_kernel,
-        [(14 * rows + PAD, width), (4 * rows + PAD, width), (4 * rows, width)],
-        [scale, state, state, held],
-        (adjoint_source, medium, meta),
-    )
-    chip_one = chip_swap(chip_one)
+        [last_message, (14 * rows + PAD, width)],
+        [state, held],
+        (adjoint_source, medium, scales, own, pair),
+    )
+    pair = core_swap(pair)
     chip_two = chip_swap(chip_two)
-    pair = core_swap(pair)
 
     here = index.astype(jnp.float32)
     levels = depth[0].astype(jnp.float32)
@@ -589,19 +576,13 @@
     position = lax.broadcasted_iota(jnp.int32, (planes, rows, width), 2).astype(jnp.float32)
     outside = float(size)
     owner = jnp.where(position < levels[:, :, None], (owners - here)[:, :, None], outside)
-    below = jnp.where(lax.rem(index, 2) == 1, pair[14 * rows :], chip_one[4 * rows :])
+    below = jnp.where(lax.rem(index, 2) == 1, pair[14 * rows :], chip_one[10 * rows :])
     edge = jnp.where(position[0] < below[0, :rows, None], (below[1, :rows] - here)[:, None], outside)
-    first, scales, extra = call(
-        early_kernel,
-        [state, scale, (16, rows, width)],
-        [state, held, (6,) + plane, (6,) + plane, (6,) + plane],
-        (adjoint_source, medium, pair, chip),
-    )
-    middle, curls, moment = call(
+    middle, curls, extra, moment = call(
         middle_kernel,
-        [state, held, (3, planes) + plane],
-        [state],
-        (adjoint_source, medium, forward_field, pair, chip_one, first, scales, extra),
+        [state, held, (16, rows, width), (3, planes) + plane],
+        [state, state, (6,) + plane, (6,) + plane, (6,) + plane],
+        (adjoint_source, medium, forward_field, scales, pair, chip_one),
     )
     send, stay = call(
         window_kernel,

time: 32.4 us -> 32.9 us (1.015)
  the two profiles are of different devices: /device:TPU:17 before, /device:TPU:8 now
where the time goes in v4:
time: 32.9 us; the launch traced here: 32.7 us
  starting transfers between devices  16.6 us (50%)
  waiting for transfers between devices  9.81 us (30%)
  Pallas kernels  5.08 us (15%)
  other arithmetic  0.98 us (3%)
    ppermute x2, starting transfers between devices, chip_swap(): return lax.ppermute(value, 'space', pairs)  6.46 us
    pallas_call x4, Pallas kernels, call(): pl.pallas_call(kernel, out_shape=[jax.ShapeDtypeStruct(s, jnp.float32) fo...  5.08 us
    ppermute x2, starting transfers between devices, core_swap(): return lax.ppermute(value, 'space', [(i, i ^ 1) for i in range(size)])  4.58 us
    ppermute x1, waiting for transfers between devices, gather_owned(): from_outer = lax.ppermute(jnp.where(upward, below, above), 'space', outer)  3.91 us
    ppermute x2, waiting for transfers between devices, chip_swap(): return lax.ppermute(value, 'space', pairs)  2.76 us
    ppermute x1, waiting for transfers between devices, sum_over_groups(): lax.ppermute(value, 'src', [(i, i ^ step) for i in range(size)])  2.25 us
    ppermute x1, starting transfers between devices, gather_owned(): from_outer = lax.ppermute(jnp.where(upward, below, above), 'space', outer)  1.91 us
    ppermute x1, starting transfers between devices, sum_over_groups(): lax.ppermute(value, 'src', [(i, i ^ step) for i in range(size)])  1.56 us
  transfers between devices with their start and end apart: 8, of which 4 were waited for; matrix products, arithmetic and copies ran while one was open for 1% of the time, Pallas kernels for 7%

profile of v4, /device:TPU:8, one launch (start us, length us, event | category | flops | bytes accessed | tf_op | source)
XLA Modules:
  0.0 32.7 jit_solution(1447750424531331865)
XLA Ops:
  0.0 2.0 %shard_map.64 = (f32[648,128]{1,0:T(8,128)S(1)}, f32[1,6,4,64,128]{4,3,2,1,0:T(8,128)S(1)}, f32[2,4,64,128]{3,2,1,0:T(8,128)S(1)}, f32[4,64,128]{2,1,0:T(8,128)S...) custom-call(f32[1,6,4,64,128]{4,3,2,1,0:T(8,128)} %source_hbm.1, f32[2,4,64,128]{3,2,1,0:T(8,128)} %medium_hbm.1, ...), custom_call_target="tpu_custom_call" | custom-call | flops 1048576 | bytes 1048576 | tf_op jit(solution)/shard_map/pallas_call | solution.py:467
  2.0 0.0 copy-start.2
  2.0 0.0 copy-start.3
  2.0 0.0 copy-start
  2.1 0.4 %shard_map.65 = (f32[256,128]{1,0:T(8,128)S(1)}, f32[904,128]{1,0:T(8,128)S(1)}) custom-call(f32[1,6,4,64,128]{4,3,2,1,0:T(8,128)S(1)} %get-tuple-element.19.source_ref, f32[2,4,64,128]{3,2,1,0:T(8,128)S(1)} %get-tuple-element.20.medium_ref, f32[4,64,128]{2,1,0:T(8,128)S(1)} %get-tuple-element.21.scale_ref, f32[6,4,80,128]{3,2,1,0:T(8,128)S(1)} %get-tuple-element.22.two, ...), custom_call_target="tpu_custom_call" | custom-call | flops 1048576 | bytes 1048576 | tf_op jit(solution)/shard_map/pallas_call | solution.py:467
  2.5 0.1 collective-permute-start
  2.5 3.4 %collective-permute-start.1 = (f32[648,128]{1,0:T(8,128)S(1)}, f32[648,128]{1,0:T(8,128)S(1)}, u32[]{:S(2)}, u32[]{:S(2)}) collective-permute-start(f32[648,128]{1,0:T(8,128)S(1)} %get-tuple-element.25), channel_id=1, source_target_pairs={{1,2},{2,1},{3,4},{4,3},{5,6},{6,5},{7,8},{8,7},{9,10},{10,9},{11,... | collective-permute-start | bytes 995336 | tf_op jit(solution)/shard_map/ppermute | solution.py:488
  5.9 3.1 %collective-permute-start.2 = (f32[256,128]{1,0:T(8,128)S(1)}, f32[256,128]{1,0:T(8,128)S(1)}, u32[]{:S(2)}, u32[]{:S(2)}) collective-permute-start(f32[256,128]{1,0:T(8,128)S(1)} %get-tuple-element.26), channel_id=1, source_target_pairs={{1,2},{2,1},{3,4},{4,3},{5,6},{6,5},{7,8},{8,7},{9,10},{10,9},{11,... | collective-permute-start | bytes 393224 | tf_op jit(solution)/shard_map/ppermute | solution.py:488
  9.0 0.0 copy-done.2
  9.0 0.0 copy-done.3
  9.1 0.1 compare_select_fusion.owner_ref
  9.2 2.8 %collective-permute-done.1.chip_ref = f32[648,128]{1,0:T(8,128)S(1)} collective-permute-done((f32[648,128]{1,0:T(8,128)S(1)}, f32[648,128]{1,0:T(8,128)S(1)}, u32[]{:S(2)}, u32[]{:S(2)}) %collective-permute-start.1) | collective-permute-done | bytes 331808 | tf_op jit(solution)/shard_map/ppermute | solution.py:488
  12.0 0.0 collective-permute-done.pair_ref
  12.0 0.0 copy-done
  12.0 2.2 %shard_map.66 = (f32[6,4,80,128]{3,2,1,0:T(8,128)S(1)}, f32[6,5,80,128]{3,2,1,0:T(8,128)S(1)}, f32[16,64,128]{2,1,0:T(8,128)S(1)}, f32[3,4,80,128]{3,2,1,0:T(8,128)S(1)}) custom-call(f32[1,6,4,64,128]{4,3,2,1,0:T(8,128)S(1)} %get-tuple-element.19.source_ref, f32[2,4,64,128]{3,2,1,0:T(8,128)S(1)} %get-tuple-element.20.medium_ref, ...), custom_call_target="tpu_custom_call" | custom-call | flops 1048576 | bytes 1048576 | tf_op jit(solution)/shard_map/pallas_call | solution.py:467
  14.2 0.1 compare_select_fusion.1.edge_ref
  14.3 0.0 collective-permute-done.2.chip_ref
  14.3 0.0 copy-start.1
  14.3 0.5 %shard_map.67 = (f32[3,32,128]{2,1,0:T(8,128)S(1)}, f32[3,32,128]{2,1,0:T(8,128)S(1)}) custom-call(f32[1,6,4,64,128]{4,3,2,1,0:T(8,128)S(1)} %get-tuple-element.19.source_ref, f32[2,4,64,128]{3,2,1,0:T(8,128)S(1)} %get-tuple-element.20.medium_ref, bf16[1,6,4,64,128]{4,3,2,1,0:T(8,128)(2,1)S(1)} %copy-done, f32[4,64,128]{2,1,0:T(8,128)S(1)} %compare_select_fusion.owner_ref, ...), custom_call_target="tpu_custom_call" | custom-call | flops 1048576 | bytes 1048576 | tf_op jit(solution)/shard_map/pallas_call | solution.py:467
  14.8 4.5 %collective-permute-start.3 = (f32[3,32,128]{2,1,0:T(8,128)S(1)}, f32[3,32,128]{2,1,0:T(8,128)S(1)}, u32[]{:S(2)}, u32[]{:S(2)}) collective-permute-start(f32[3,32,128]{2,1,0:T(8,128)S(1)} %get-tuple-element.32), channel_id=1, source_target_pairs={{0,1},{1,0},{2,3},{3,2},{4,5},{5,4},{6,7},{7,6},{8,9},{9,8},{10,11... | collective-permute-start | bytes 147464 | tf_op jit(solution)/shard_map/ppermute | solution.py:480
  19.3 0.9 %collective-permute-done.3 = f32[3,32,128]{2,1,0:T(8,128)S(1)} collective-permute-done((f32[3,32,128]{2,1,0:T(8,128)S(1)}, f32[3,32,128]{2,1,0:T(8,128)S(1)}, u32[]{:S(2)}, u32[]{:S(2)}) %collective-permute-start.3) | collective-permute-done | bytes 49184 | tf_op jit(solution)/shard_map/ppermute | solution.py:480
  20.2 1.5 %collective-permute-start.4 = (f32[32,128]{1,0:T(8,128)S(1)}, f32[32,128]{1,0:T(8,128)S(1)}, u32[]{:S(2)}, u32[]{:S(2)}) collective-permute-start(f32[32,128]{1,0:T(8,128)S(1)} %get-tuple-element.42), channel_id=1, source_target_pairs={{0,2},{1,3},{2,0},{3,1},{4,6},{5,7},{6,4},{7,5},{8,10},{9,11},{10,... | collective-permute-start | bytes 49160 | tf_op jit(solution)/shard_map/ppermute | solution.py:521
  21.6 1.9 %collective-permute-start.5 = (f32[32,128]{1,0:T(8,128)S(1)}, f32[32,128]{1,0:T(8,128)S(1)}, u32[]{:S(2)}, u32[]{:S(2)}) collective-permute-start(f32[32,128]{1,0:T(8,128)S(1)} %get-tuple-element.43), channel_id=1, source_target_pairs={{2,4},{3,5},{4,2},{5,3},{6,8},{7,9},{8,6},{9,7},{10,12},{11,13},{1... | collective-permute-start | bytes 49160 | tf_op jit(solution)/shard_map/ppermute | solution.py:522
  23.6 0.7 %collective-permute-start.6 = (f32[32,128]{1,0:T(8,128)S(1)}, f32[32,128]{1,0:T(8,128)S(1)}, u32[]{:S(2)}, u32[]{:S(2)}) collective-permute-start(f32[32,128]{1,0:T(8,128)S(1)} %slice_bitcast_fusion), channel_id=1, source_target_pairs={{5,1},{7,3},{9,5},{11,7},{13,9},{15,11},{21,17},{23,19},{25,21},{2... | collective-permute-start | bytes 49160 | tf_op jit(solution)/shard_map/ppermute | solution.py:523
  24.2 0.0 collective-permute-done.4
  24.3 3.9 %collective-permute-done.5 = f32[32,128]{1,0:T(8,128)S(1)} collective-permute-done((f32[32,128]{1,0:T(8,128)S(1)}, f32[32,128]{1,0:T(8,128)S(1)}, u32[]{:S(2)}, u32[]{:S(2)}) %collective-permute-start.5) | collective-permute-done | bytes 16416 | tf_op jit(solution)/shard_map/ppermute | solution.py:522
  28.2 0.0 collective-permute-done.6
  28.2 1.6 %collective-permute-start.7 = (f32[32,128]{1,0:T(8,128)S(1)}, f32[32,128]{1,0:T(8,128)S(1)}, u32[]{:S(2)}, u32[]{:S(2)}) collective-permute-start(f32[32,128]{1,0:T(8,128)S(1)} %fusion.17), channel_id=1, source_target_pairs={{0,16},{16,0},{1,17},{17,1},{2,18},{18,2},{3,19},{19,3},{4,20},{20... | collective-permute-start | bytes 49160 | tf_op jit(solution)/shard_map/ppermute | solution.py:497
  29.7 2.2 %collective-permute-done.7 = f32[32,128]{1,0:T(8,128)S(1)} collective-permute-done((f32[32,128]{1,0:T(8,128)S(1)}, f32[32,128]{1,0:T(8,128)S(1)}, u32[]{:S(2)}, u32[]{:S(2)}) %collective-permute-start.7) | collective-permute-done | bytes 16416 | tf_op jit(solution)/shard_map/ppermute | solution.py:497
  32.0 0.0 copy-done.1
  32.0 0.7 %fusion.7 = f32[1,32,128]{2,1,0:T(8,128)} fusion(f32[1,32,128]{2,1,0:T(8,128)S(1)} %get-tuple-element.41, f32[1,32,128]{2,1,0:T(8,128)S(1)} %get-tuple-element.40, f32[1,32,128]{2,1,0:T(8,128)S(1)} %get-tuple-element.39, f32[1,32,128]{2,1,0:T(8,128)S(1)} %get-tuple-element.38, f32[1,32,128]{2,1,0:T(8,128)S(1)} %get-tuple-element.37, ...), kind=kLoop, calls=%fused_computation.17 | loop fusion | flops 36864 | bytes 180224 | tf_op jit(solution)/shard_map/add | solution.py:536
  (10 shorter events, 0.1 us)
Async XLA Ops:
  2.0 7.0 %copy-start.2 = (s32[1,4,64]{2,1,0:T(4,128)S(1)}, s32[1,4,64]{2,1,0:T(4,128)}, u32[]{:S(2)}) copy-start(s32[1,4,64]{2,1,0:T(4,128)} %depth_hbm.1) | copy-start | bytes 3076
  2.0 7.0 %copy-start.3 = (s32[4,64]{1,0:T(4,128)S(1)}, s32[4,64]{1,0:T(4,128)}, u32[]{:S(2)}) copy-start(s32[4,64]{1,0:T(4,128)} %map_hbm.1) | copy-start | bytes 3076
  2.0 9.9 %copy-start = (bf16[1,6,4,64,128]{4,3,2,1,0:T(8,128)(2,1)S(1)}, bf16[1,6,4,64,128]{4,3,2,1,0:T(8,128)(2,1)}, u32[]{:S(2)}) copy-start(bf16[1,6,4,64,128]{4,3,2,1,0:T(8,128)(2,1)} %saved_ref.3) | copy-start | bytes 1179652
  2.5 9.5 %collective-permute-start = (f32[904,128]{1,0:T(8,128)S(1)}, f32[904,128]{1,0:T(8,128)S(1)}, u32[]{:S(2)}, u32[]{:S(2)}) collective-permute-start(f32[904,128]{1,0:T(8,128)S(1)} %get-tuple-element.24), channel_id=1, source_target_pairs={{0,1},{1,0},{2,3},{3,2},{4,5},{5,4},{6,7},{7,6},{8,9},{9,8},{10,11... | collective-permute-start | bytes 1388552 | tf_op jit(solution)/shard_map/ppermute | solution.py:480
  2.5 9.4 %collective-permute-start.1 = (f32[648,128]{1,0:T(8,128)S(1)}, f32[648,128]{1,0:T(8,128)S(1)}, u32[]{:S(2)}, u32[]{:S(2)}) collective-permute-start(f32[648,128]{1,0:T(8,128)S(1)} %get-tuple-element.25), channel_id=1, source_target_pairs={{1,2},{2,1},{3,4},{4,3},{5,6},{6,5},{7,8},{8,7},{9,10},{10,9},{11,... | collective-permute-start | bytes 995336 | tf_op jit(solution)/shard_map/ppermute | solution.py:488
  5.9 8.4 %collective-permute-start.2 = (f32[256,128]{1,0:T(8,128)S(1)}, f32[256,128]{1,0:T(8,128)S(1)}, u32[]{:S(2)}, u32[]{:S(2)}) collective-permute-start(f32[256,128]{1,0:T(8,128)S(1)} %get-tuple-element.26), channel_id=1, source_target_pairs={{1,2},{2,1},{3,4},{4,3},{5,6},{6,5},{7,8},{8,7},{9,10},{10,9},{11,... | collective-permute-start | bytes 393224 | tf_op jit(solution)/shard_map/ppermute | solution.py:488
  14.3 17.7 %copy-start.1 = (f32[9,1,32,128]{3,2,1,0:T(8,128)S(1)}, f32[9,1,32,128]{3,2,1,0:T(8,128)}, u32[]{:S(2)}) copy-start(f32[9,1,32,128]{3,2,1,0:T(8,128)} %param.11) | copy-start | bytes 442372
  14.8 5.4 %collective-permute-start.3 = (f32[3,32,128]{2,1,0:T(8,128)S(1)}, f32[3,32,128]{2,1,0:T(8,128)S(1)}, u32[]{:S(2)}, u32[]{:S(2)}) collective-permute-start(f32[3,32,128]{2,1,0:T(8,128)S(1)} %get-tuple-element.32), channel_id=1, source_target_pairs={{0,1},{1,0},{2,3},{3,2},{4,5},{5,4},{6,7},{7,6},{8,9},{9,8},{10,11... | collective-permute-start | bytes 147464 | tf_op jit(solution)/shard_map/ppermute | solution.py:480
  20.2 4.1 %collective-permute-start.4 = (f32[32,128]{1,0:T(8,128)S(1)}, f32[32,128]{1,0:T(8,128)S(1)}, u32[]{:S(2)}, u32[]{:S(2)}) collective-permute-start(f32[32,128]{1,0:T(8,128)S(1)} %get-tuple-element.42), channel_id=1, source_target_pairs={{0,2},{1,3},{2,0},{3,1},{4,6},{5,7},{6,4},{7,5},{8,10},{9,11},{10,... | collective-permute-start | bytes 49160 | tf_op jit(solution)/shard_map/ppermute | solution.py:521
  21.6 6.5 %collective-permute-start.5 = (f32[32,128]{1,0:T(8,128)S(1)}, f32[32,128]{1,0:T(8,128)S(1)}, u32[]{:S(2)}, u32[]{:S(2)}) collective-permute-start(f32[32,128]{1,0:T(8,128)S(1)} %get-tuple-element.43), channel_id=1, source_target_pairs={{2,4},{3,5},{4,2},{5,3},{6,8},{7,9},{8,6},{9,7},{10,12},{11,13},{1... | collective-permute-start | bytes 49160 | tf_op jit(solution)/shard_map/ppermute | solution.py:522
  23.6 4.6 %collective-permute-start.6 = (f32[32,128]{1,0:T(8,128)S(1)}, f32[32,128]{1,0:T(8,128)S(1)}, u32[]{:S(2)}, u32[]{:S(2)}) collective-permute-start(f32[32,128]{1,0:T(8,128)S(1)} %slice_bitcast_fusion), channel_id=1, source_target_pairs={{5,1},{7,3},{9,5},{11,7},{13,9},{15,11},{21,17},{23,19},{25,21},{2... | collective-permute-start | bytes 49160 | tf_op jit(solution)/shard_map/ppermute | solution.py:523
  28.2 3.8 %collective-permute-start.7 = (f32[32,128]{1,0:T(8,128)S(1)}, f32[32,128]{1,0:T(8,128)S(1)}, u32[]{:S(2)}, u32[]{:S(2)}) collective-permute-start(f32[32,128]{1,0:T(8,128)S(1)} %fusion.17), channel_id=1, source_target_pairs={{0,16},{16,0},{1,17},{17,1},{2,18},{18,2},{3,19},{19,3},{4,20},{20... | collective-permute-start | bytes 49160 | tf_op jit(solution)/shard_map/ppermute | solution.py:497

commit v5 on v3

--- a/solution.py
+++ b/solution.py
@@ -77,14 +77,14 @@
     return out
 
 
-def updated(center, image, source, real, imag, scale):
+def updated(center, image, base, ratio, real, imag, scale):
     out = []
     for c in range(3):
         applied = image[c] + real * center[c] - imag * center[c + 3]
-        out.append(center[c] + scale * (source[c] - applied))
+        out.append(center[c] + ratio * base[c] - scale * applied)
     for c in range(3):
         applied = image[c + 3] + real * center[c + 3] + imag * center[c]
-        out.append(center[c + 3] + scale * (source[c + 3] - applied))
+        out.append(center[c + 3] + ratio * base[c + 3] - scale * applied)
     return out
 
 
@@ -97,7 +97,7 @@
     return out
 
 
-def sweep_slab(state, held, result, source_ref, medium_ref, scale_ref, weight, low, high, first_scale, planes, rows, lane, wanted=None):
+def sweep_slab(state, held, result, base, medium_ref, scale_ref, weight, low, high, first_scale, planes, rows, lane, wanted=None):
     wanted = range(planes) if wanted is None else wanted
     needed = sorted({i for w in wanted for i in (w - 1, w)})
     for i in needed:
@@ -127,7 +127,8 @@
             new = updated(
                 [rows_at(state, (c, i), row) for c in range(6)],
                 image,
-                [source_ref[0, c, i, here, :] for c in range(6)],
+                [rows_at(base, (c, i), row) for c in range(6)],
+                weight / sweep_steps[0],
                 medium_ref[0, i, here, :],
                 medium_ref[1, i, here, :],
                 weight * scale_ref[i, here, :],
@@ -136,14 +137,13 @@
                 put(result, (c, i), row, new[c])
 
 
-def first_sweep(source_ref, medium_ref, scale_ref, state, planes, rows):
-    for i in range(planes):
-        for row in chunks(rows):
-            here = pl.ds(row, ROWS)
-            scale = 1.0 / (4.0 + medium_ref[0, i, here, :])
-            scale_ref[i, here, :] = scale
-            for c in range(6):
-                put(state, (c, i), row, sweep_steps[0] * source_ref[0, c, i, here, :] * scale)
+def first_sweep(fields, medium_ref, scale_ref, state, i, rows):
+    for row in chunks(rows):
+        here = pl.ds(row, ROWS)
+        scale = 1.0 / (4.0 + medium_ref[0, i, here, :])
+        scale_ref[i, here, :] = scale
+        for c in range(6):
+            put(state, (c, i), row, sweep_steps[0] * scale * fields[c, i, here, :])
 
 
 def parity_and_ends():
@@ -154,12 +154,12 @@
     return odd, first_scale, last_scale
 
 
-def emit_level(emit, state, planes, rows, lane):
+def emit_level(emit, first, state, planes, rows, lane):
     for row in chunks(rows):
         sums = edge_sums(lambda c, s: rows_at(state, (c, planes - 1), row, s), lane)
         bottom = [rows_at(state, (c, 0), row) for c in (1, 2, 4, 5)]
         for k in range(4):
-            emit(k, row, bottom[k], sums[k])
+            emit(first + k, row, bottom[k], sums[k])
 
 
 def message_rows(slot, row, rows):
@@ -167,48 +167,45 @@
 
 
 def start_kernel(
-    source_hbm, medium_hbm, depth_hbm, map_hbm, chip_ref, source_ref, medium_ref, meta_ref, top, levels, owners, sems
+    source_hbm, medium_hbm, depth_hbm, map_hbm, chip_ref, medium_ref, scale_ref, one, meta_ref,
+    fields, levels, owners, sems,
 ):
     planes, rows, width = medium_ref.shape[1:]
     lane = lane_of(width)
     odd = parity_and_ends()[0]
-    order = [planes - 1, 0] + list(range(1, planes - 1))
+    last = planes - 1
+    order = [last, 0] + list(range(1, last))
     copies = []
     for i in order:
         copies.append(pltpu.make_async_copy(medium_hbm.at[:, i], medium_ref.at[:, i], sems.at[2 * i]))
-        copies.append(pltpu.make_async_copy(source_hbm.at[0, :, i], source_ref.at[0, :, i], sems.at[2 * i + 1]))
-    copies.append(pltpu.make_async_copy(depth_hbm.at[0], levels, sems.at[2 * planes]))
-    copies.append(pltpu.make_async_copy(map_hbm, owners, sems.at[2 * planes + 1]))
-    for copy in copies:
+        copies.append(pltpu.make_async_copy(source_hbm.at[0, :, i], fields.at[:, i], sems.at[2 * i + 1]))
+    columns = [
+        pltpu.make_async_copy(depth_hbm.at[0], levels, sems.at[2 * planes]),
+        pltpu.make_async_copy(map_hbm, owners, sems.at[2 * planes + 1]),
+    ]
+    for copy in copies + columns:
         copy.start()
-    clear_pads(top)
-    last = planes - 1
+    clear_pads(one)
+    meta_ref[...] = jnp.zeros_like(meta_ref)
 
     def emit(slot, row, below, above):
         chip_ref[message_rows(slot, row, rows), :] = jnp.where(odd, above, below)
 
-    for copy in copies[:2]:
+    for k, i in enumerate(order):
+        copies[2 * k].wait()
+        copies[2 * k + 1].wait()
+        first_sweep(fields, medium_ref, scale_ref, one, i, rows)
+        if k == 1:
+            emit_level(emit, 0, one, planes, rows, lane)
+            for row in chunks(rows):
+                here = pl.ds(row, ROWS)
+                for part in range(2):
+                    emit(4 + part, row, medium_ref[part, 0, here, :], medium_ref[part, last, here, :])
+    for copy in columns:
         copy.wait()
-    for row in chunks(rows):
-        here = pl.ds(row, ROWS)
-        scale = sweep_steps[0] / (4.0 + medium_ref[0, last, here, :])
-        for c in range(6):
-            put(top, (c,), row, scale * source_ref[0, c, last, here, :])
-    for copy in copies[2:4]:
-        copy.wait()
-    for row in chunks(rows):
-        here = pl.ds(row, ROWS)
-        scale = sweep_steps[0] / (4.0 + medium_ref[0, 0, here, :])
-        sums = edge_sums(lambda c, s: rows_at(top, (c,), row, s), lane)
-        for k, c in enumerate((1, 2, 4, 5)):
-            emit(k, row, scale * source_ref[0, c, 0, here, :], sums[k])
-        for k in range(2):
-            emit(4 + k, row, medium_ref[k, 0, here, :], medium_ref[k, last, here, :])
-    for copy in copies[4:]:
-        copy.wait()
-    meta_ref[...] = jnp.zeros_like(meta_ref)
     meta_ref[pl.ds(0, 1), pl.ds(0, rows)] = levels[pl.ds(last, 1), :].astype(jnp.float32)
     meta_ref[pl.ds(1, 1), pl.ds(0, rows)] = owners[pl.ds(last, 1), :].astype(jnp.float32)
+    chip_ref[pl.ds(6 * rows, PAD), :] = meta_ref[...]
 
 
 def no_plane(c, row):
@@ -219,49 +216,53 @@
     return 0.0, 0.0
 
 
-def follow_kernel(source_ref, medium_ref, meta_ref, pair_ref, chip_ref, chip_two_ref, scale_ref, one, two, held):
+def follow_kernel(medium_ref, scale_ref, one, meta_ref, chip_ref, pair_ref, two, three, held):
     planes, rows, width = medium_ref.shape[1:]
     lane = lane_of(width)
     odd, first_scale, _ = parity_and_ends()
-    for ref in (one, two, held):
-        clear_pads(ref)
+    clear_pads(two)
+    clear_pads(three)
+    clear_pads(held)
 
     def emitter(slots, to_chip):
         def emit(slot, row, below, above):
             pair_ref[message_rows(slots + slot, row, rows), :] = jnp.where(odd, below, above)
             if to_chip is not None:
-                to_chip[message_rows(slot, row, rows), :] = jnp.where(odd, above, below)
+                chip_ref[message_rows(to_chip + slot, row, rows), :] = jnp.where(odd, above, below)
 
         return emit
 
-    first_sweep(source_ref, medium_ref, scale_ref, one, planes, rows)
     sweep_slab(
-        one, held, two, source_ref, medium_ref, scale_ref, sweep_steps[1], no_sums, no_plane, first_scale,
+        one, held, two, one, medium_ref, scale_ref, sweep_steps[1], no_sums, no_plane, first_scale,
         planes, rows, lane,
     )
-    emit_level(emitter(6, chip_ref), two, planes, rows, lane)
-    emit_level(emitter(0, None), one, planes, rows, lane)
+    emit_level(emitter(6, 0), 0, two, planes, rows, lane)
+    sweep_slab(
+        two, held, three, one, medium_ref, scale_ref, sweep_steps[2], no_sums, no_plane, first_scale,
+        planes, rows, lane, wanted=sorted({0, planes - 1}),
+    )
+    emit_level(emitter(10, 4), 0, three, planes, rows, lane)
+    emit_level(emitter(0, None), 0, one, planes, rows, lane)
     emit = emitter(4, None)
     for row in chunks(rows):
         for k in range(2):
             here = pl.ds(row, ROWS)
             emit(k, row, medium_ref[k, 0, here, :], medium_ref[k, planes - 1, here, :])
-    chip_ref[pl.ds(4 * rows, PAD), :] = meta_ref[...]
     pair_ref[pl.ds(14 * rows, PAD), :] = meta_ref[...]
-    sweep_slab(
-        two, held, one, source_ref, medium_ref, scale_ref, sweep_steps[2], no_sums, no_plane, first_scale,
-        planes, rows, lane, wanted=sorted({0, planes - 1}),
-    )
-    emit_level(emitter(10, chip_two_ref), one, planes, rows, lane)
-
-
-def readers(odd, pair_ref, chip_ref, rows, first):
+
+
+def readers(odd, pair_ref, pair_first, chip_ref, chip_first, rows):
+    def both(slot, row):
+        pair = pair_ref[message_rows(pair_first + slot, row, rows), :]
+        chip = chip_ref[message_rows(chip_first + slot, row, rows), :]
+        return pair, chip
+
     def from_below(slot, row):
-        pair, chip = pair_ref[message_rows(first + slot, row, rows), :], chip_ref[message_rows(slot, row, rows), :]
+        pair, chip = both(slot, row)
         return jnp.where(odd, pair, chip)
 
     def from_above(slot, row):
-        pair, chip = pair_ref[message_rows(first + slot, row, rows), :], chip_ref[message_rows(slot, row, rows), :]
+        pair, chip = both(slot, row)
         return jnp.where(odd, chip, pair)
 
     return from_below, from_above
@@ -283,15 +284,14 @@
 
 
 def early_kernel(
-    source_ref, medium_ref, pair_ref, chip_ref, two, scale_ref, extra_ref, one, held, delta_low, delta_high, delta_two,
+    medium_ref, scale_ref, one, pair_ref, chip_ref, two, extra_ref, held, delta_low, delta_high, delta_two,
 ):
     planes, rows, width = medium_ref.shape[1:]
     lane = lane_of(width)
     odd, first_scale, last_scale = parity_and_ends()
-    for ref in (one, two, held, delta_low, delta_high, delta_two):
+    for ref in (two, held, delta_low, delta_high, delta_two):
         clear_pads(ref)
-    first_sweep(source_ref, medium_ref, scale_ref, one, planes, rows)
-    from_below, from_above = readers(odd, pair_ref, chip_ref, rows, 0)
+    from_below, from_above = readers(odd, pair_ref, 0, chip_ref, 0, rows)
 
     for row in chunks(rows):
         sums = edge_sums(lambda c, s: rows_at(one, (c, planes - 1), row, s), lane)
@@ -306,7 +306,7 @@
             put(delta_low, (part,), row, scale * ((behind(ez, lane) - ez) + (rows_at(one, (part + 1, 0), row, -1) - ey)))
 
     sweep_slab(
-        one, held, two, source_ref, medium_ref, scale_ref, sweep_steps[1],
+        one, held, two, one, medium_ref, scale_ref, sweep_steps[1],
         lambda part, row: (from_below(2 * (part // 3), row), from_below(2 * (part // 3) + 1, row)),
         lambda c, row: from_above(WHERE_YZ[c], row),
         first_scale, planes, rows, lane,
@@ -323,7 +323,7 @@
         image = curl_back(lambda c, s: rows_at(held, (c, 0), row, s), lambda c: before[c], lane)
         real, imag = from_below(4, row), from_below(5, row)
         new = updated(
-            [rows_at(delta_low, (c,), row) for c in range(6)], image, none, real, imag, sweep_steps[2] / (4.0 + real)
+            [rows_at(delta_low, (c,), row) for c in range(6)], image, none, 0.0, real, imag, sweep_steps[2] / (4.0 + real)
         )
         for c in range(6):
             put(delta_two, (c,), row, new[c])
@@ -358,89 +358,41 @@
             )
 
 
-def middle_kernel(
-    source_ref, medium_ref, saved_ref, pair_ref, chip_ref, state_in_ref, scale_ref, extra_ref,
-    state_ref, held, moment_ref, one,
+def last_kernel(
+    base_ref, medium_ref, saved_ref, scale_ref, owner_ref, edge_ref, pair_ref, chip_ref, one, extra_ref,
+    send_ref, stay_ref, two, three, held, moment, window,
 ):
     planes, rows, width = medium_ref.shape[1:]
     lane = lane_of(width)
     odd, first_scale, _ = parity_and_ends()
-    for ref in (one, state_ref, held, moment_ref):
+    for ref in (two, held, moment):
         clear_pads(ref)
-    from_below, from_above = readers(odd, pair_ref, chip_ref, rows, 6)
-
-    def low(part, row):
-        k = 2 * (part // 3)
-        here = pl.ds(row, ROWS)
-        return from_below(k, row) + extra_ref[k, here, :], from_below(k + 1, row) + extra_ref[k + 1, here, :]
-
-    def high(c, row):
-        return from_above(WHERE_YZ[c], row) + extra_ref[4 + WHERE_YZ[c], pl.ds(row, ROWS), :]
-
-    sweep_slab(
-        state_in_ref, held, state_ref, source_ref, medium_ref, scale_ref, sweep_steps[2], low, high, first_scale,
-        planes, rows, lane,
-    )
-    inner = range(1, planes - 1)
-    sweep_slab(
-        state_ref, held, one, source_ref, medium_ref, scale_ref, sweep_steps[3], None, None, first_scale,
-        planes, rows, lane, wanted=inner,
-    )
-    for i in inner:
-        moments(saved_ref, one, moment_ref, i, rows, lane)
-
-
-def window_kernel(
-    source_ref, medium_ref, saved_ref, owner_ref, edge_ref, pair_ref, chip_ref, state_ref, held_ref, scale_ref,
-    extra_ref, moment_in_ref, send_ref, stay_ref, held, two, moment, window,
-):
-    planes, rows, width = medium_ref.shape[1:]
-    lane = lane_of(width)
-    odd, first_scale, _ = parity_and_ends()
-    from_below, from_above = readers(odd, pair_ref, chip_ref, rows, 10)
-    clear_pads(held)
-    clear_pads(moment)
-    ends = sorted({0, planes - 1})
-
-    for row in chunks(rows):
-        here = pl.ds(row, ROWS)
-        for part in (0, 3):
+
+    def sweep_with(level, state, result):
+        from_below, from_above = readers(odd, pair_ref, 2 + 4 * level, chip_ref, 4 * level - 4, rows)
+        first = 8 * level - 8
+
+        def low(part, row):
             k = 2 * (part // 3)
-            ey, ez = rows_at(state_ref, (part + 1, 0), row), rows_at(state_ref, (part + 2, 0), row)
-            gy = from_below(k, row) + extra_ref[8 + k, here, :]
-            gz = from_below(k + 1, row) + extra_ref[9 + k, here, :]
-            put(held, (part + 1, 0), row, first_scale * (gz - ez))
-            put(held, (part + 2, 0), row, first_scale * (ey - gy))
-        values = curl(
-            lambda c, s: rows_at(state_ref, (c, planes - 1), row, s),
-            lambda c: from_above(WHERE_YZ[c], row) + extra_ref[12 + WHERE_YZ[c], here, :],
-            lane,
+            here = pl.ds(row, ROWS)
+            below = from_below(k, row) + extra_ref[first + k, here, :]
+            return below, from_below(k + 1, row) + extra_ref[first + k + 1, here, :]
+
+        def high(c, row):
+            return from_above(WHERE_YZ[c], row) + extra_ref[first + 4 + WHERE_YZ[c], pl.ds(row, ROWS), :]
+
+        sweep_slab(
+            state, held, result, base_ref, medium_ref, scale_ref, sweep_steps[level + 1], low, high, first_scale,
+            planes, rows, lane,
         )
-        for c in range(6):
-            put(held, (c, 1), row, values[c])
-    for i in ends:
-        for row in chunks(rows):
-            here = pl.ds(row, ROWS)
-            if i == planes - 1:
-                now = lambda c, s: rows_at(held, (c, 1), row, s)
-            else:
-                now = lambda c, s: rows_at(held_ref, (c, i + 1), row, s)
-            if i == 0:
-                before = lambda c: rows_at(held, (c, 0), row)
-            else:
-                before = lambda c: rows_at(held_ref, (c, i), row)
-            image = curl_back(now, before, lane)
-            real, imag = medium_ref[0, i, here, :], medium_ref[1, i, here, :]
-            new = updated(
-                [rows_at(state_ref, (c, i), row) for c in range(6)], image,
-                [source_ref[0, c, i, here, :] for c in range(6)], real, imag, sweep_steps[3] * scale_ref[i, here, :],
-            )
-            for c in range(6):
-                put(two, (c, i), row, new[c])
-        moments(saved_ref, two, moment, i, rows, lane)
+
+    sweep_with(1, one, two)
+    sweep_with(2, two, three)
+    for i in range(planes):
+        moments(saved_ref, three, moment, i, rows, lane)
 
     def moment_rows(c, i, row, shift=0):
-        return rows_at(moment if i in ends else moment_in_ref, (c, i), row, shift)
+        return rows_at(moment, (c, i), row, shift)
 
     for row in chunks(rows):
         here = pl.ds(row, ROWS)
@@ -565,22 +517,18 @@
     hbm = pl.BlockSpec(memory_space=pltpu.HBM)
     columns = pltpu.VMEM((planes, rows), jnp.int32)
     given = (adjoint_source, medium, depth, plane_map)
-    chip, adjoint_source, medium, meta = call(
+    chip, medium, scales, own, meta = call(
         start_kernel,
-        [(6 * rows, width), adjoint_source.shape, medium.shape, (PAD, width)],
-        [(6,) + plane, columns, columns, pltpu.SemaphoreType.DMA((2 * planes + 2,))],
+        [(6 * rows + PAD, width), medium.shape, scale, state, (PAD, width)],
+        [(6, planes, rows, width), columns, columns, pltpu.SemaphoreType.DMA((2 * planes + 2,))],
         tuple(pltpu.with_memory_space_constraint(a, pltpu.HBM) for a in given),
         in_specs=[hbm] * 4,
     )
     chip = chip_swap(chip)
-    pair, chip_one, chip_two = call(
-        follow_kernel,
-        [(14 * rows + PAD, width), (4 * rows + PAD, width), (4 * rows, width)],
-        [scale, state, state, held],
-        (adjoint_source, medium, meta),
+    chip_one, pair = call(
+        follow_kernel, [(8 * rows, width), (14 * rows + PAD, width)], [state, state, held], (medium, scales, own, meta)
     )
     chip_one = chip_swap(chip_one)
-    chip_two = chip_swap(chip_two)
     pair = core_swap(pair)
 
     here = index.astype(jnp.float32)
@@ -589,25 +537,19 @@
     position = lax.broadcasted_iota(jnp.int32, (planes, rows, width), 2).astype(jnp.float32)
     outside = float(size)
     owner = jnp.where(position < levels[:, :, None], (owners - here)[:, :, None], outside)
-    below = jnp.where(lax.rem(index, 2) == 1, pair[14 * rows :], chip_one[4 * rows :])
+    below = jnp.where(lax.rem(index, 2) == 1, pair[14 * rows :], chip[6 * rows :])
     edge = jnp.where(position[0] < below[0, :rows, None], (below[1, :rows] - here)[:, None], outside)
-    first, scales, extra = call(
+    first, extra = call(
         early_kernel,
-        [state, scale, (16, rows, width)],
-        [state, held, (6,) + plane, (6,) + plane, (6,) + plane],
-        (adjoint_source, medium, pair, chip),
-    )
-    middle, curls, moment = call(
-        middle_kernel,
-        [state, held, (3, planes) + plane],
-        [state],
-        (adjoint_source, medium, forward_field, pair, chip_one, first, scales, extra),
+        [state, (16, rows, width)],
+        [held, (6,) + plane, (6,) + plane, (6,) + plane],
+        (medium, scales, own, pair, chip),
     )
     send, stay = call(
-        window_kernel,
+        last_kernel,
         [(REACH + 1, rows // 2, width), (REACH + 1, rows // 2, width)],
-        [(6, 2) + plane, state, (3, planes) + plane, (2 * REACH + 2, rows, width)],
-        (adjoint_source, medium, forward_field, owner, edge, pair, chip_two, middle, curls, scales, extra, moment),
+        [state, state, held, (3, planes) + plane, (2 * REACH + 2, rows, width)],
+        (own, medium, forward_field, scales, owner, edge, pair, chip_one, first, extra),
     )
     total = sum_over_groups(gather_owned(send, stay))
     return transposed_smooth(total[None], rough)

time: 32.4 us -> 32.8 us (1.012)
  the two profiles are of different devices: /device:TPU:17 before, /device:TPU:8 now
where the time goes in v5:
time: 32.8 us; the launch traced here: 32.6 us
  starting transfers between devices  15.4 us (47%)
  waiting for transfers between devices  10.8 us (33%)
  Pallas kernels  4.57 us (14%)
  other arithmetic  0.97 us (3%)
  local copies, waits for them, and re-layouts  0.7 us (2%)
    ppermute x2, starting transfers between devices, chip_swap(): return lax.ppermute(value, 'space', pairs)  6.46 us
    pallas_call x4, Pallas kernels, call(): pl.pallas_call(kernel, out_shape=[jax.ShapeDtypeStruct(s, jnp.float32) fo...  4.57 us
    ppermute x1, waiting for transfers between devices, gather_owned(): from_outer = lax.ppermute(jnp.where(upward, below, above), 'space', outer)  3.91 us
    ppermute x2, waiting for transfers between devices, chip_swap(): return lax.ppermute(value, 'space', pairs)  3.74 us
    ppermute x2, starting transfers between devices, core_swap(): return lax.ppermute(value, 'space', [(i, i ^ 1) for i in range(size)])  3.32 us
    ppermute x1, waiting for transfers between devices, sum_over_groups(): lax.ppermute(value, 'src', [(i, i ^ step) for i in range(size)])  2.25 us
    ppermute x1, starting transfers between devices, gather_owned(): from_outer = lax.ppermute(jnp.where(upward, below, above), 'space', outer)  1.91 us
    ppermute x1, starting transfers between devices, sum_over_groups(): lax.ppermute(value, 'src', [(i, i ^ step) for i in range(size)])  1.56 us
  transfers between devices with their start and end apart: 8, of which 5 were waited for; matrix products, arithmetic and copies ran while one was open for 1% of the time, Pallas kernels for 3%

profile of v5, /device:TPU:8, one launch (start us, length us, event | category | flops | bytes accessed | tf_op | source)
XLA Modules:
  0.0 32.6 jit_solution(1011595278160295440)
XLA Ops:
  0.0 1.4 %shard_map.64 = (f32[392,128]{1,0:T(8,128)S(1)}, f32[2,4,64,128]{3,2,1,0:T(8,128)S(1)}, f32[4,64,128]{2,1,0:T(8,128)S(1)}, f32[6,4,80,128]{3,2,1,0:T(8,128)S(1)}, f32[8,128]{1,0:T(8,128)S(1)}) custom-call(f32[1,6,4,64,128]{4,3,2,1,0:T(8,128)} %source_hbm.1, f32[2,4,64,128]{3,2,1,0:T(8,128)} %medium_hbm.1, s32[1,4,64]{2,1,0:T(4,128)} %depth_hbm.1, ...), custom_call_target="tpu_custom_call" | custom-call | flops 1048576 | bytes 1048576 | tf_op jit(solution)/shard_map/pallas_call | solution.py:432
  1.4 0.9 %shard_map.65 = (f32[512,128]{1,0:T(8,128)S(1)}, f32[904,128]{1,0:T(8,128)S(1)}) custom-call(f32[2,4,64,128]{3,2,1,0:T(8,128)S(1)} %get-tuple-element.17.medium_ref, f32[4,64,128]{2,1,0:T(8,128)S(1)} %get-tuple-element.18.scale_ref, f32[6,4,80,128]{3,2,1,0:T(8,128)S(1)} %get-tuple-element.16.one.base_ref, f32[8,128]{1,0:T(8,128)S(1)} %get-tuple-element.19.meta_ref), custom_call_target="tpu_custom_call" | custom-call | flops 1048576 | bytes 1048576 | tf_op jit(solution)/shard_map/pallas_call | solution.py:432
  2.4 0.0 copy-start.2
  2.4 0.1 collective-permute-start
  2.5 3.4 %collective-permute-start.1 = (f32[392,128]{1,0:T(8,128)S(1)}, f32[392,128]{1,0:T(8,128)S(1)}, u32[]{:S(2)}, u32[]{:S(2)}) collective-permute-start(f32[392,128]{1,0:T(8,128)S(1)} %get-tuple-element.21), channel_id=1, source_target_pairs={{1,2},{2,1},{3,4},{4,3},{5,6},{6,5},{7,8},{8,7},{9,10},{10,9},{11,... | collective-permute-start | bytes 602120 | tf_op jit(solution)/shard_map/ppermute | solution.py:453
  5.9 3.1 %collective-permute-start.2 = (f32[512,128]{1,0:T(8,128)S(1)}, f32[512,128]{1,0:T(8,128)S(1)}, u32[]{:S(2)}, u32[]{:S(2)}) collective-permute-start(f32[512,128]{1,0:T(8,128)S(1)} %get-tuple-element.22), channel_id=1, source_target_pairs={{1,2},{2,1},{3,4},{4,3},{5,6},{6,5},{7,8},{8,7},{9,10},{10,9},{11,... | collective-permute-start | bytes 786440 | tf_op jit(solution)/shard_map/ppermute | solution.py:453
  8.9 0.0 copy-done.2
  9.0 0.0 copy-start.3
  9.0 0.7 %copy-done.3 = s32[4,64]{1,0:T(4,128)S(1)} copy-done((s32[4,64]{1,0:T(4,128)S(1)}, s32[4,64]{1,0:T(4,128)}, u32[]{:S(2)}) %copy-start.3) | copy-done | bytes 1048
  9.7 0.1 compare_select_fusion.owner_ref
  9.8 0.7 %collective-permute-done.1.chip_ref = f32[392,128]{1,0:T(8,128)S(1)} collective-permute-done((f32[392,128]{1,0:T(8,128)S(1)}, f32[392,128]{1,0:T(8,128)S(1)}, u32[]{:S(2)}, u32[]{:S(2)}) %collective-permute-start.1) | collective-permute-done | bytes 200736 | tf_op jit(solution)/shard_map/ppermute | solution.py:453
  10.5 0.0 collective-permute-done.pair_ref
  10.5 0.0 copy-start
  10.5 0.9 %shard_map.66 = (f32[6,4,80,128]{3,2,1,0:T(8,128)S(1)}, f32[16,64,128]{2,1,0:T(8,128)S(1)}) custom-call(f32[2,4,64,128]{3,2,1,0:T(8,128)S(1)} %get-tuple-element.17.medium_ref, f32[4,64,128]{2,1,0:T(8,128)S(1)} %get-tuple-element.18.scale_ref, f32[6,4,80,128]{3,2,1,0:T(8,128)S(1)} %get-tuple-element.16.one.base_ref, ...), custom_call_target="tpu_custom_call" | custom-call | flops 1048576 | bytes 1048576 | tf_op jit(solution)/shard_map/pallas_call | solution.py:432
  11.4 0.1 compare_select_fusion.1.edge_ref
  11.5 3.0 %collective-permute-done.2.chip_ref = f32[512,128]{1,0:T(8,128)S(1)} collective-permute-done((f32[512,128]{1,0:T(8,128)S(1)}, f32[512,128]{1,0:T(8,128)S(1)}, u32[]{:S(2)}, u32[]{:S(2)}) %collective-permute-start.2) | collective-permute-done | bytes 262176 | tf_op jit(solution)/shard_map/ppermute | solution.py:453
  14.6 0.0 copy-done
  14.6 1.3 %shard_map.67 = (f32[3,32,128]{2,1,0:T(8,128)S(1)}, f32[3,32,128]{2,1,0:T(8,128)S(1)}) custom-call(f32[6,4,80,128]{3,2,1,0:T(8,128)S(1)} %get-tuple-element.16.one.base_ref, f32[2,4,64,128]{3,2,1,0:T(8,128)S(1)} %get-tuple-element.17.medium_ref, bf16[1,6,4,64,128]{4,3,2,1,0:T(8,128)(2,1)S(1)} %copy-done, f32[4,64,128]{2,1,0:T(8,128)S(1)} %get-tuple-element.18.scale_ref, ...), custom_call_target="tpu_custom_call" | custom-call | flops 1048576 | bytes 1048576 | tf_op jit(solution)/shard_map/pallas_call | solution.py:432
  15.9 3.2 %collective-permute-start.3 = (f32[3,32,128]{2,1,0:T(8,128)S(1)}, f32[3,32,128]{2,1,0:T(8,128)S(1)}, u32[]{:S(2)}, u32[]{:S(2)}) collective-permute-start(f32[3,32,128]{2,1,0:T(8,128)S(1)} %get-tuple-element.26), channel_id=1, source_target_pairs={{0,1},{1,0},{2,3},{3,2},{4,5},{5,4},{6,7},{7,6},{8,9},{9,8},{10,11... | collective-permute-start | bytes 147464 | tf_op jit(solution)/shard_map/ppermute | solution.py:445
  19.1 0.0 copy-start.1
  19.1 0.9 %collective-permute-done.3 = f32[3,32,128]{2,1,0:T(8,128)S(1)} collective-permute-done((f32[3,32,128]{2,1,0:T(8,128)S(1)}, f32[3,32,128]{2,1,0:T(8,128)S(1)}, u32[]{:S(2)}, u32[]{:S(2)}) %collective-permute-start.3) | collective-permute-done | bytes 49184 | tf_op jit(solution)/shard_map/ppermute | solution.py:445
  20.0 1.5 %collective-permute-start.4 = (f32[32,128]{1,0:T(8,128)S(1)}, f32[32,128]{1,0:T(8,128)S(1)}, u32[]{:S(2)}, u32[]{:S(2)}) collective-permute-start(f32[32,128]{1,0:T(8,128)S(1)} %get-tuple-element.36), channel_id=1, source_target_pairs={{0,2},{1,3},{2,0},{3,1},{4,6},{5,7},{6,4},{7,5},{8,10},{9,11},{10,... | collective-permute-start | bytes 49160 | tf_op jit(solution)/shard_map/ppermute | solution.py:486
  21.5 1.9 %collective-permute-start.5 = (f32[32,128]{1,0:T(8,128)S(1)}, f32[32,128]{1,0:T(8,128)S(1)}, u32[]{:S(2)}, u32[]{:S(2)}) collective-permute-start(f32[32,128]{1,0:T(8,128)S(1)} %get-tuple-element.37), channel_id=1, source_target_pairs={{2,4},{3,5},{4,2},{5,3},{6,8},{7,9},{8,6},{9,7},{10,12},{11,13},{1... | collective-permute-start | bytes 49160 | tf_op jit(solution)/shard_map/ppermute | solution.py:487
  23.4 0.7 %collective-permute-start.6 = (f32[32,128]{1,0:T(8,128)S(1)}, f32[32,128]{1,0:T(8,128)S(1)}, u32[]{:S(2)}, u32[]{:S(2)}) collective-permute-start(f32[32,128]{1,0:T(8,128)S(1)} %slice_bitcast_fusion), channel_id=1, source_target_pairs={{5,1},{7,3},{9,5},{11,7},{13,9},{15,11},{21,17},{23,19},{25,21},{2... | collective-permute-start | bytes 49160 | tf_op jit(solution)/shard_map/ppermute | solution.py:488
  24.1 0.0 collective-permute-done.4
  24.1 3.9 %collective-permute-done.5 = f32[32,128]{1,0:T(8,128)S(1)} collective-permute-done((f32[32,128]{1,0:T(8,128)S(1)}, f32[32,128]{1,0:T(8,128)S(1)}, u32[]{:S(2)}, u32[]{:S(2)}) %collective-permute-start.5) | collective-permute-done | bytes 16416 | tf_op jit(solution)/shard_map/ppermute | solution.py:487
  28.0 0.0 collective-permute-done.6
  28.0 1.6 %collective-permute-start.7 = (f32[32,128]{1,0:T(8,128)S(1)}, f32[32,128]{1,0:T(8,128)S(1)}, u32[]{:S(2)}, u32[]{:S(2)}) collective-permute-start(f32[32,128]{1,0:T(8,128)S(1)} %fusion.17), channel_id=1, source_target_pairs={{0,16},{16,0},{1,17},{17,1},{2,18},{18,2},{3,19},{19,3},{4,20},{20... | collective-permute-start | bytes 49160 | tf_op jit(solution)/shard_map/ppermute | solution.py:462
  29.6 2.2 %collective-permute-done.7 = f32[32,128]{1,0:T(8,128)S(1)} collective-permute-done((f32[32,128]{1,0:T(8,128)S(1)}, f32[32,128]{1,0:T(8,128)S(1)}, u32[]{:S(2)}, u32[]{:S(2)}) %collective-permute-start.7) | collective-permute-done | bytes 16416 | tf_op jit(solution)/shard_map/ppermute | solution.py:462
  31.8 0.0 copy-done.1
  31.9 0.7 %fusion.7 = f32[1,32,128]{2,1,0:T(8,128)} fusion(f32[1,32,128]{2,1,0:T(8,128)S(1)} %get-tuple-element.35, f32[1,32,128]{2,1,0:T(8,128)S(1)} %get-tuple-element.34, f32[1,32,128]{2,1,0:T(8,128)S(1)} %get-tuple-element.33, f32[1,32,128]{2,1,0:T(8,128)S(1)} %get-tuple-element.32, f32[1,32,128]{2,1,0:T(8,128)S(1)} %get-tuple-element.31, ...), kind=kLoop, calls=%fused_computation.17 | loop fusion | flops 36864 | bytes 180224 | tf_op jit(solution)/shard_map/add | solution.py:501
  (10 shorter events, 0.1 us)
Async XLA Ops:
  2.4 6.6 %copy-start.2 = (s32[1,4,64]{2,1,0:T(4,128)S(1)}, s32[1,4,64]{2,1,0:T(4,128)}, u32[]{:S(2)}) copy-start(s32[1,4,64]{2,1,0:T(4,128)} %depth_hbm.1) | copy-start | bytes 3076
  2.4 8.1 %collective-permute-start = (f32[904,128]{1,0:T(8,128)S(1)}, f32[904,128]{1,0:T(8,128)S(1)}, u32[]{:S(2)}, u32[]{:S(2)}) collective-permute-start(f32[904,128]{1,0:T(8,128)S(1)} %get-tuple-element.20), channel_id=1, source_target_pairs={{0,1},{1,0},{2,3},{3,2},{4,5},{5,4},{6,7},{7,6},{8,9},{9,8},{10,11... | collective-permute-start | bytes 1388552 | tf_op jit(solution)/shard_map/ppermute | solution.py:445
  2.5 8.0 %collective-permute-start.1 = (f32[392,128]{1,0:T(8,128)S(1)}, f32[392,128]{1,0:T(8,128)S(1)}, u32[]{:S(2)}, u32[]{:S(2)}) collective-permute-start(f32[392,128]{1,0:T(8,128)S(1)} %get-tuple-element.21), channel_id=1, source_target_pairs={{1,2},{2,1},{3,4},{4,3},{5,6},{6,5},{7,8},{8,7},{9,10},{10,9},{11,... | collective-permute-start | bytes 602120 | tf_op jit(solution)/shard_map/ppermute | solution.py:453
  5.9 8.7 %collective-permute-start.2 = (f32[512,128]{1,0:T(8,128)S(1)}, f32[512,128]{1,0:T(8,128)S(1)}, u32[]{:S(2)}, u32[]{:S(2)}) collective-permute-start(f32[512,128]{1,0:T(8,128)S(1)} %get-tuple-element.22), channel_id=1, source_target_pairs={{1,2},{2,1},{3,4},{4,3},{5,6},{6,5},{7,8},{8,7},{9,10},{10,9},{11,... | collective-permute-start | bytes 786440 | tf_op jit(solution)/shard_map/ppermute | solution.py:453
  9.0 0.7 %copy-start.3 = (s32[4,64]{1,0:T(4,128)S(1)}, s32[4,64]{1,0:T(4,128)}, u32[]{:S(2)}) copy-start(s32[4,64]{1,0:T(4,128)} %map_hbm.1) | copy-start | bytes 3076
  10.5 4.1 %copy-start = (bf16[1,6,4,64,128]{4,3,2,1,0:T(8,128)(2,1)S(1)}, bf16[1,6,4,64,128]{4,3,2,1,0:T(8,128)(2,1)}, u32[]{:S(2)}) copy-start(bf16[1,6,4,64,128]{4,3,2,1,0:T(8,128)(2,1)} %saved_ref.1) | copy-start | bytes 1179652
  15.9 4.1 %collective-permute-start.3 = (f32[3,32,128]{2,1,0:T(8,128)S(1)}, f32[3,32,128]{2,1,0:T(8,128)S(1)}, u32[]{:S(2)}, u32[]{:S(2)}) collective-permute-start(f32[3,32,128]{2,1,0:T(8,128)S(1)} %get-tuple-element.26), channel_id=1, source_target_pairs={{0,1},{1,0},{2,3},{3,2},{4,5},{5,4},{6,7},{7,6},{8,9},{9,8},{10,11... | collective-permute-start | bytes 147464 | tf_op jit(solution)/shard_map/ppermute | solution.py:445
  19.1 12.7 %copy-start.1 = (f32[9,1,32,128]{3,2,1,0:T(8,128)S(1)}, f32[9,1,32,128]{3,2,1,0:T(8,128)}, u32[]{:S(2)}) copy-start(f32[9,1,32,128]{3,2,1,0:T(8,128)} %param.11) | copy-start | bytes 442372
  20.0 4.1 %collective-permute-start.4 = (f32[32,128]{1,0:T(8,128)S(1)}, f32[32,128]{1,0:T(8,128)S(1)}, u32[]{:S(2)}, u32[]{:S(2)}) collective-permute-start(f32[32,128]{1,0:T(8,128)S(1)} %get-tuple-element.36), channel_id=1, source_target_pairs={{0,2},{1,3},{2,0},{3,1},{4,6},{5,7},{6,4},{7,5},{8,10},{9,11},{10,... | collective-permute-start | bytes 49160 | tf_op jit(solution)/shard_map/ppermute | solution.py:486
  21.5 6.5 %collective-permute-start.5 = (f32[32,128]{1,0:T(8,128)S(1)}, f32[32,128]{1,0:T(8,128)S(1)}, u32[]{:S(2)}, u32[]{:S(2)}) collective-permute-start(f32[32,128]{1,0:T(8,128)S(1)} %get-tuple-element.37), channel_id=1, source_target_pairs={{2,4},{3,5},{4,2},{5,3},{6,8},{7,9},{8,6},{9,7},{10,12},{11,13},{1... | collective-permute-start | bytes 49160 | tf_op jit(solution)/shard_map/ppermute | solution.py:487
  23.4 4.6 %collective-permute-start.6 = (f32[32,128]{1,0:T(8,128)S(1)}, f32[32,128]{1,0:T(8,128)S(1)}, u32[]{:S(2)}, u32[]{:S(2)}) collective-permute-start(f32[32,128]{1,0:T(8,128)S(1)} %slice_bitcast_fusion), channel_id=1, source_target_pairs={{5,1},{7,3},{9,5},{11,7},{13,9},{15,11},{21,17},{23,19},{25,21},{2... | collective-permute-start | bytes 49160 | tf_op jit(solution)/shard_map/ppermute | solution.py:488
  28.0 3.8 %collective-permute-start.7 = (f32[32,128]{1,0:T(8,128)S(1)}, f32[32,128]{1,0:T(8,128)S(1)}, u32[]{:S(2)}, u32[]{:S(2)}) collective-permute-start(f32[32,128]{1,0:T(8,128)S(1)} %fusion.17), channel_id=1, source_target_pairs={{0,16},{16,0},{1,17},{17,1},{2,18},{18,2},{3,19},{19,3},{4,20},{20... | collective-permute-start | bytes 49160 | tf_op jit(solution)/shard_map/ppermute | solution.py:462

commit v6 on v5

--- a/solution.py
+++ b/solution.py
@@ -97,6 +97,10 @@
     return out
 
 
+def planes_of(ref):
+    return lambda c, i, row, shift=0: rows_at(ref, (c, i), row, shift)
+
+
 def sweep_slab(state, held, result, base, medium_ref, scale_ref, weight, low, high, first_scale, planes, rows, lane, wanted=None):
     wanted = range(planes) if wanted is None else wanted
     needed = sorted({i for w in wanted for i in (w - 1, w)})
@@ -105,17 +109,17 @@
             if i < 0:
                 for part in (0, 3):
                     gy, gz = low(part, row)
-                    ey, ez = rows_at(state, (part + 1, 0), row), rows_at(state, (part + 2, 0), row)
+                    ey, ez = state(part + 1, 0, row), state(part + 2, 0, row)
                     put(held, (part + 1, 0), row, first_scale * (gz - ez))
                     put(held, (part + 2, 0), row, first_scale * (ey - gy))
                 continue
 
             def ahead_of(c, i=i, row=row):
                 if i + 1 < planes:
-                    return rows_at(state, (c, i + 1), row)
+                    return state(c, i + 1, row)
                 return high(c, row)
 
-            values = curl(lambda c, s: rows_at(state, (c, i), row, s), ahead_of, lane)
+            values = curl(lambda c, s: state(c, i, row, s), ahead_of, lane)
             for c in range(6):
                 put(held, (c, i + 1), row, values[c])
     for i in wanted:
@@ -125,7 +129,7 @@
             )
             here = pl.ds(row, ROWS)
             new = updated(
-                [rows_at(state, (c, i), row) for c in range(6)],
+                [state(c, i, row) for c in range(6)],
                 image,
                 [rows_at(base, (c, i), row) for c in range(6)],
                 weight / sweep_steps[0],
@@ -233,12 +237,12 @@
         return emit
 
     sweep_slab(
-        one, held, two, one, medium_ref, scale_ref, sweep_steps[1], no_sums, no_plane, first_scale,
+        planes_of(one), held, two, one, medium_ref, scale_ref, sweep_steps[1], no_sums, no_plane, first_scale,
         planes, rows, lane,
     )
     emit_level(emitter(6, 0), 0, two, planes, rows, lane)
     sweep_slab(
-        two, held, three, one, medium_ref, scale_ref, sweep_steps[2], no_sums, no_plane, first_scale,
+        planes_of(two), held, three, one, medium_ref, scale_ref, sweep_steps[2], no_sums, no_plane, first_scale,
         planes, rows, lane, wanted=sorted({0, planes - 1}),
     )
     emit_level(emitter(10, 4), 0, three, planes, rows, lane)
@@ -284,12 +288,12 @@
 
 
 def early_kernel(
-    medium_ref, scale_ref, one, pair_ref, chip_ref, two, extra_ref, held, delta_low, delta_high, delta_two,
+    medium_ref, scale_ref, one, pair_ref, chip_ref, three, extra_ref, two, held, delta_low, delta_high, delta_two,
 ):
     planes, rows, width = medium_ref.shape[1:]
     lane = lane_of(width)
     odd, first_scale, last_scale = parity_and_ends()
-    for ref in (two, held, delta_low, delta_high, delta_two):
+    for ref in (two, three, held, delta_low, delta_high, delta_two):
         clear_pads(ref)
     from_below, from_above = readers(odd, pair_ref, 0, chip_ref, 0, rows)
 
@@ -306,7 +310,7 @@
             put(delta_low, (part,), row, scale * ((behind(ez, lane) - ez) + (rows_at(one, (part + 1, 0), row, -1) - ey)))
 
     sweep_slab(
-        one, held, two, one, medium_ref, scale_ref, sweep_steps[1],
+        planes_of(one), held, two, one, medium_ref, scale_ref, sweep_steps[1],
         lambda part, row: (from_below(2 * (part // 3), row), from_below(2 * (part // 3) + 1, row)),
         lambda c, row: from_above(WHERE_YZ[c], row),
         first_scale, planes, rows, lane,
@@ -328,12 +332,9 @@
         for c in range(6):
             put(delta_two, (c,), row, new[c])
     for row in chunks(rows):
-        for level, deltas in enumerate((delta_low, delta_two)):
-            sums = edge_sums(lambda c, s: rows_at(deltas, (c,), row, s), lane)
-            for k in range(4):
-                extra_ref[8 * level + k, pl.ds(row, ROWS), :] = sums[k]
-        for k, c in enumerate((1, 2, 4, 5)):
-            extra_ref[4 + k, pl.ds(row, ROWS), :] = rows_at(delta_high, (c,), row)
+        sums = edge_sums(lambda c, s: rows_at(delta_two, (c,), row, s), lane)
+        for k in range(4):
+            extra_ref[k, pl.ds(row, ROWS), :] = sums[k]
     for row in chunks(rows):
         for part in (0, 3):
             ey, ez = rows_at(delta_high, (part + 1,), row), rows_at(delta_high, (part + 2,), row)
@@ -352,42 +353,70 @@
             image[part + 1] = 2.0 * ey - sums[k] - (behind(hx, lane) - hx)
             image[part + 2] = (rows_at(held, (part, 1), row, -1) - hx) - sums[k + 1] + 2.0 * ez
         for k, c in enumerate((1, 2)):
-            extra_ref[12 + k, here, :] = center[c] - scale * (image[c] + real * center[c] - imag * center[c + 3])
-            extra_ref[14 + k, here, :] = center[c + 3] - scale * (
+            extra_ref[4 + k, here, :] = center[c] - scale * (image[c] + real * center[c] - imag * center[c + 3])
+            extra_ref[6 + k, here, :] = center[c + 3] - scale * (
                 image[c + 3] + real * center[c + 3] + imag * center[c]
             )
 
+    def low(part, row):
+        sums = edge_sums(lambda c, s: rows_at(delta_low, (c,), row, s), lane)
+        return sums[2 * (part // 3)], sums[2 * (part // 3) + 1]
+
+    sweep_slab(
+        planes_of(two), held, three, one, medium_ref, scale_ref, sweep_steps[2], low,
+        lambda c, row: rows_at(delta_high, (c,), row), first_scale, planes, rows, lane,
+    )
+
 
 def last_kernel(
-    base_ref, medium_ref, saved_ref, scale_ref, owner_ref, edge_ref, pair_ref, chip_ref, one, extra_ref,
-    send_ref, stay_ref, two, three, held, moment, window,
+    base_ref, medium_ref, saved_ref, scale_ref, owner_ref, edge_ref, pair_ref, chip_ref, two, extra_ref,
+    send_ref, stay_ref, ends, above, three, held, moment, window,
 ):
     planes, rows, width = medium_ref.shape[1:]
     lane = lane_of(width)
     odd, first_scale, _ = parity_and_ends()
-    for ref in (two, held, moment):
+    for ref in (ends, above, held, moment):
         clear_pads(ref)
-
-    def sweep_with(level, state, result):
-        from_below, from_above = readers(odd, pair_ref, 2 + 4 * level, chip_ref, 4 * level - 4, rows)
-        first = 8 * level - 8
-
-        def low(part, row):
+    last = planes - 1
+
+    from_below, from_above = readers(odd, pair_ref, 6, chip_ref, 0, rows)
+    for row in chunks(rows):
+        for k in range(4):
+            put(above, (k,), row, from_above(k, row))
+    for row in chunks(rows):
+        here = pl.ds(row, ROWS)
+        low_scale = (first_scale * sweep_steps[2]) * scale_ref[0, here, :]
+        high_scale = sweep_steps[2] * scale_ref[last, here, :]
+        for part in (0, 3):
             k = 2 * (part // 3)
-            here = pl.ds(row, ROWS)
-            below = from_below(k, row) + extra_ref[first + k, here, :]
-            return below, from_below(k + 1, row) + extra_ref[first + k + 1, here, :]
-
-        def high(c, row):
-            return from_above(WHERE_YZ[c], row) + extra_ref[first + 4 + WHERE_YZ[c], pl.ds(row, ROWS), :]
-
-        sweep_slab(
-            state, held, result, base_ref, medium_ref, scale_ref, sweep_steps[level + 1], low, high, first_scale,
-            planes, rows, lane,
-        )
-
-    sweep_with(1, one, two)
-    sweep_with(2, two, three)
+            put(ends, (part, 0), row, rows_at(two, (part, 0), row))
+            put(ends, (part + 1, 0), row, rows_at(two, (part + 1, 0), row) + low_scale * from_below(k, row))
+            put(ends, (part + 2, 0), row, rows_at(two, (part + 2, 0), row) + low_scale * from_below(k + 1, row))
+            ey, ez = rows_at(above, (k,), row), rows_at(above, (k + 1,), row)
+            turn = (behind(ez, lane) - ez) + (rows_at(above, (k,), row, -1) - ey)
+            put(ends, (part, 1), row, rows_at(two, (part, last), row) + high_scale * turn)
+            put(ends, (part + 1, 1), row, rows_at(two, (part + 1, last), row) + high_scale * ey)
+            put(ends, (part + 2, 1), row, rows_at(two, (part + 2, last), row) + high_scale * ez)
+
+    def state(c, i, row, shift=0):
+        if i == 0:
+            return rows_at(ends, (c, 0), row, shift)
+        if i == last:
+            return rows_at(ends, (c, 1), row, shift)
+        return rows_at(two, (c, i), row, shift)
+
+    below_two, above_two = readers(odd, pair_ref, 10, chip_ref, 4, rows)
+
+    def low(part, row):
+        k = 2 * (part // 3)
+        here = pl.ds(row, ROWS)
+        return below_two(k, row) + extra_ref[k, here, :], below_two(k + 1, row) + extra_ref[k + 1, here, :]
+
+    sweep_slab(
+        state, held, three, base_ref, medium_ref, scale_ref, sweep_steps[3], low,
+        lambda c, row: above_two(WHERE_YZ[c], row) + extra_ref[4 + WHERE_YZ[c], pl.ds(row, ROWS), :],
+        first_scale, planes, rows, lane,
+    )
     for i in range(planes):
         moments(saved_ref, three, moment, i, rows, lane)
 
@@ -541,14 +570,14 @@
     edge = jnp.where(position[0] < below[0, :rows, None], (below[1, :rows] - here)[:, None], outside)
     first, extra = call(
         early_kernel,
-        [state, (16, rows, width)],
-        [held, (6,) + plane, (6,) + plane, (6,) + plane],
+        [state, (8, rows, width)],
+        [state, held, (6,) + plane, (6,) + plane, (6,) + plane],
         (medium, scales, own, pair, chip),
     )
     send, stay = call(
         last_kernel,
         [(REACH + 1, rows // 2, width), (REACH + 1, rows // 2, width)],
-        [state, state, held, (3, planes) + plane, (2 * REACH + 2, rows, width)],
+        [(6, 2) + plane, (4,) + plane, state, held, (3, planes) + plane, (2 * REACH + 2, rows, width)],
         (own, medium, forward_field, scales, owner, edge, pair, chip_one, first, extra),
     )
     total = sum_over_groups(gather_owned(send, stay))

time: 32.8 us -> 32.4 us (0.988)
  waiting for transfers between devices: 10.8 us -> 10.1 us
    ppermute x2, waiting for transfers between devices: 3.74 us -> 3.09 us  [chip_swap(): return lax.ppermute(value, 'space', pairs)]
  transfers between devices with their start and end apart: 8 -> 8, of which waited for: 5 -> 5; matrix products, arithmetic and copies ran while one was open for 1% -> 1% of each run, Pallas kernels for 3% -> 5%
where the time goes in v6:
time: 32.4 us; the launch traced here: 32.1 us
  starting transfers between devices  15.4 us (48%)
  waiting for transfers between devices  10.1 us (31%)
  Pallas kernels  4.79 us (15%)
  other arithmetic  0.97 us (3%)
  local copies, waits for them, and re-layouts  0.7 us (2%)
    ppermute x2, starting transfers between devices, chip_swap(): return lax.ppermute(value, 'space', pairs)  6.46 us
    pallas_call x4, Pallas kernels, call(): pl.pallas_call(kernel, out_shape=[jax.ShapeDtypeStruct(s, jnp.float32) fo...  4.79 us
    ppermute x1, waiting for transfers between devices, gather_owned(): from_outer = lax.ppermute(jnp.where(upward, below, above), 'space', outer)  3.91 us
    ppermute x2, starting transfers between devices, core_swap(): return lax.ppermute(value, 'space', [(i, i ^ 1) for i in range(size)])  3.32 us
    ppermute x2, waiting for transfers between devices, chip_swap(): return lax.ppermute(value, 'space', pairs)  3.09 us
    ppermute x1, waiting for transfers between devices, sum_over_groups(): lax.ppermute(value, 'src', [(i, i ^ step) for i in range(size)])  2.25 us
    ppermute x1, starting transfers between devices, gather_owned(): from_outer = lax.ppermute(jnp.where(upward, below, above), 'space', outer)  1.91 us
    ppermute x1, starting transfers between devices, sum_over_groups(): lax.ppermute(value, 'src', [(i, i ^ step) for i in range(size)])  1.56 us
  transfers between devices with their start and end apart: 8, of which 5 were waited for; matrix products, arithmetic and copies ran while one was open for 1% of the time, Pallas kernels for 5%

profile of v6, /device:TPU:8, one launch (start us, length us, event | category | flops | bytes accessed | tf_op | source)
XLA Modules:
  0.0 32.1 jit_solution(15884072126174288079)
XLA Ops:
  0.0 1.4 %shard_map.64 = (f32[392,128]{1,0:T(8,128)S(1)}, f32[2,4,64,128]{3,2,1,0:T(8,128)S(1)}, f32[4,64,128]{2,1,0:T(8,128)S(1)}, f32[6,4,80,128]{3,2,1,0:T(8,128)S(1)}, f32[8,128]{1,0:T(8,128)S(1)}) custom-call(f32[1,6,4,64,128]{4,3,2,1,0:T(8,128)} %source_hbm.1, f32[2,4,64,128]{3,2,1,0:T(8,128)} %medium_hbm.1, s32[1,4,64]{2,1,0:T(4,128)} %depth_hbm.1, ...), custom_call_target="tpu_custom_call" | custom-call | flops 1048576 | bytes 1048576 | tf_op jit(solution)/shard_map/pallas_call | solution.py:461
  1.4 0.9 %shard_map.65 = (f32[512,128]{1,0:T(8,128)S(1)}, f32[904,128]{1,0:T(8,128)S(1)}) custom-call(f32[2,4,64,128]{3,2,1,0:T(8,128)S(1)} %get-tuple-element.17.medium_ref, f32[4,64,128]{2,1,0:T(8,128)S(1)} %get-tuple-element.18.scale_ref, f32[6,4,80,128]{3,2,1,0:T(8,128)S(1)} %get-tuple-element.16.one.base_ref, f32[8,128]{1,0:T(8,128)S(1)} %get-tuple-element.19.meta_ref), custom_call_target="tpu_custom_call" | custom-call | flops 1048576 | bytes 1048576 | tf_op jit(solution)/shard_map/pallas_call | solution.py:461
  2.4 0.0 copy-start.2
  2.4 0.1 collective-permute-start
  2.5 3.4 %collective-permute-start.1 = (f32[392,128]{1,0:T(8,128)S(1)}, f32[392,128]{1,0:T(8,128)S(1)}, u32[]{:S(2)}, u32[]{:S(2)}) collective-permute-start(f32[392,128]{1,0:T(8,128)S(1)} %get-tuple-element.21), channel_id=1, source_target_pairs={{1,2},{2,1},{3,4},{4,3},{5,6},{6,5},{7,8},{8,7},{9,10},{10,9},{11,... | collective-permute-start | bytes 602120 | tf_op jit(solution)/shard_map/ppermute | solution.py:482
  5.9 3.1 %collective-permute-start.2 = (f32[512,128]{1,0:T(8,128)S(1)}, f32[512,128]{1,0:T(8,128)S(1)}, u32[]{:S(2)}, u32[]{:S(2)}) collective-permute-start(f32[512,128]{1,0:T(8,128)S(1)} %get-tuple-element.22), channel_id=1, source_target_pairs={{1,2},{2,1},{3,4},{4,3},{5,6},{6,5},{7,8},{8,7},{9,10},{10,9},{11,... | collective-permute-start | bytes 786440 | tf_op jit(solution)/shard_map/ppermute | solution.py:482
  8.9 0.0 copy-done.2
  9.0 0.0 copy-start.3
  9.0 0.7 %copy-done.3 = s32[4,64]{1,0:T(4,128)S(1)} copy-done((s32[4,64]{1,0:T(4,128)S(1)}, s32[4,64]{1,0:T(4,128)}, u32[]{:S(2)}) %copy-start.3) | copy-done | bytes 1048
  9.7 0.1 compare_select_fusion.owner_ref
  9.8 0.7 %collective-permute-done.1.chip_ref = f32[392,128]{1,0:T(8,128)S(1)} collective-permute-done((f32[392,128]{1,0:T(8,128)S(1)}, f32[392,128]{1,0:T(8,128)S(1)}, u32[]{:S(2)}, u32[]{:S(2)}) %collective-permute-start.1) | collective-permute-done | bytes 200736 | tf_op jit(solution)/shard_map/ppermute | solution.py:482
  10.5 0.0 collective-permute-done.pair_ref
  10.5 0.0 copy-start
  10.5 1.6 %shard_map.66 = (f32[6,4,80,128]{3,2,1,0:T(8,128)S(1)}, f32[8,64,128]{2,1,0:T(8,128)S(1)}) custom-call(f32[2,4,64,128]{3,2,1,0:T(8,128)S(1)} %get-tuple-element.17.medium_ref, f32[4,64,128]{2,1,0:T(8,128)S(1)} %get-tuple-element.18.scale_ref, f32[6,4,80,128]{3,2,1,0:T(8,128)S(1)} %get-tuple-element.16.one.base_ref, ...), custom_call_target="tpu_custom_call" | custom-call | flops 1048576 | bytes 1048576 | tf_op jit(solution)/shard_map/pallas_call | solution.py:461
  12.1 0.1 compare_select_fusion.1.edge_ref
  12.2 2.4 %collective-permute-done.2.chip_ref = f32[512,128]{1,0:T(8,128)S(1)} collective-permute-done((f32[512,128]{1,0:T(8,128)S(1)}, f32[512,128]{1,0:T(8,128)S(1)}, u32[]{:S(2)}, u32[]{:S(2)}) %collective-permute-start.2) | collective-permute-done | bytes 262176 | tf_op jit(solution)/shard_map/ppermute | solution.py:482
  14.6 0.0 copy-done
  14.6 0.9 %shard_map.67 = (f32[3,32,128]{2,1,0:T(8,128)S(1)}, f32[3,32,128]{2,1,0:T(8,128)S(1)}) custom-call(f32[6,4,80,128]{3,2,1,0:T(8,128)S(1)} %get-tuple-element.16.one.base_ref, f32[2,4,64,128]{3,2,1,0:T(8,128)S(1)} %get-tuple-element.17.medium_ref, bf16[1,6,4,64,128]{4,3,2,1,0:T(8,128)(2,1)S(1)} %copy-done, f32[4,64,128]{2,1,0:T(8,128)S(1)} %get-tuple-element.18.scale_ref, ...), custom_call_target="tpu_custom_call" | custom-call | flops 1048576 | bytes 1048576 | tf_op jit(solution)/shard_map/pallas_call | solution.py:461
  15.5 3.2 %collective-permute-start.3 = (f32[3,32,128]{2,1,0:T(8,128)S(1)}, f32[3,32,128]{2,1,0:T(8,128)S(1)}, u32[]{:S(2)}, u32[]{:S(2)}) collective-permute-start(f32[3,32,128]{2,1,0:T(8,128)S(1)} %get-tuple-element.26), channel_id=1, source_target_pairs={{0,1},{1,0},{2,3},{3,2},{4,5},{5,4},{6,7},{7,6},{8,9},{9,8},{10,11... | collective-permute-start | bytes 147464 | tf_op jit(solution)/shard_map/ppermute | solution.py:474
  18.7 0.0 copy-start.1
  18.7 0.9 %collective-permute-done.3 = f32[3,32,128]{2,1,0:T(8,128)S(1)} collective-permute-done((f32[3,32,128]{2,1,0:T(8,128)S(1)}, f32[3,32,128]{2,1,0:T(8,128)S(1)}, u32[]{:S(2)}, u32[]{:S(2)}) %collective-permute-start.3) | collective-permute-done | bytes 49184 | tf_op jit(solution)/shard_map/ppermute | solution.py:474
  19.6 1.5 %collective-permute-start.4 = (f32[32,128]{1,0:T(8,128)S(1)}, f32[32,128]{1,0:T(8,128)S(1)}, u32[]{:S(2)}, u32[]{:S(2)}) collective-permute-start(f32[32,128]{1,0:T(8,128)S(1)} %get-tuple-element.36), channel_id=1, source_target_pairs={{0,2},{1,3},{2,0},{3,1},{4,6},{5,7},{6,4},{7,5},{8,10},{9,11},{10,... | collective-permute-start | bytes 49160 | tf_op jit(solution)/shard_map/ppermute | solution.py:515
  21.1 1.9 %collective-permute-start.5 = (f32[32,128]{1,0:T(8,128)S(1)}, f32[32,128]{1,0:T(8,128)S(1)}, u32[]{:S(2)}, u32[]{:S(2)}) collective-permute-start(f32[32,128]{1,0:T(8,128)S(1)} %get-tuple-element.37), channel_id=1, source_target_pairs={{2,4},{3,5},{4,2},{5,3},{6,8},{7,9},{8,6},{9,7},{10,12},{11,13},{1... | collective-permute-start | bytes 49160 | tf_op jit(solution)/shard_map/ppermute | solution.py:516
  23.0 0.7 %collective-permute-start.6 = (f32[32,128]{1,0:T(8,128)S(1)}, f32[32,128]{1,0:T(8,128)S(1)}, u32[]{:S(2)}, u32[]{:S(2)}) collective-permute-start(f32[32,128]{1,0:T(8,128)S(1)} %slice_bitcast_fusion), channel_id=1, source_target_pairs={{5,1},{7,3},{9,5},{11,7},{13,9},{15,11},{21,17},{23,19},{25,21},{2... | collective-permute-start | bytes 49160 | tf_op jit(solution)/shard_map/ppermute | solution.py:517
  23.6 0.0 collective-permute-done.4
  23.7 3.9 %collective-permute-done.5 = f32[32,128]{1,0:T(8,128)S(1)} collective-permute-done((f32[32,128]{1,0:T(8,128)S(1)}, f32[32,128]{1,0:T(8,128)S(1)}, u32[]{:S(2)}, u32[]{:S(2)}) %collective-permute-start.5) | collective-permute-done | bytes 16416 | tf_op jit(solution)/shard_map/ppermute | solution.py:516
  27.6 0.0 collective-permute-done.6
  27.6 1.6 %collective-permute-start.7 = (f32[32,128]{1,0:T(8,128)S(1)}, f32[32,128]{1,0:T(8,128)S(1)}, u32[]{:S(2)}, u32[]{:S(2)}) collective-permute-start(f32[32,128]{1,0:T(8,128)S(1)} %fusion.17), channel_id=1, source_target_pairs={{0,16},{16,0},{1,17},{17,1},{2,18},{18,2},{3,19},{19,3},{4,20},{20... | collective-permute-start | bytes 49160 | tf_op jit(solution)/shard_map/ppermute | solution.py:491
  29.1 2.2 %collective-permute-done.7 = f32[32,128]{1,0:T(8,128)S(1)} collective-permute-done((f32[32,128]{1,0:T(8,128)S(1)}, f32[32,128]{1,0:T(8,128)S(1)}, u32[]{:S(2)}, u32[]{:S(2)}) %collective-permute-start.7) | collective-permute-done | bytes 16416 | tf_op jit(solution)/shard_map/ppermute | solution.py:491
  31.4 0.0 copy-done.1
  31.4 0.7 %fusion.7 = f32[1,32,128]{2,1,0:T(8,128)} fusion(f32[1,32,128]{2,1,0:T(8,128)S(1)} %get-tuple-element.35, f32[1,32,128]{2,1,0:T(8,128)S(1)} %get-tuple-element.34, f32[1,32,128]{2,1,0:T(8,128)S(1)} %get-tuple-element.33, f32[1,32,128]{2,1,0:T(8,128)S(1)} %get-tuple-element.32, f32[1,32,128]{2,1,0:T(8,128)S(1)} %get-tuple-element.31, ...), kind=kLoop, calls=%fused_computation.17 | loop fusion | flops 36864 | bytes 180224 | tf_op jit(solution)/shard_map/add | solution.py:530
  (10 shorter events, 0.1 us)
Async XLA Ops:
  2.4 6.6 %copy-start.2 = (s32[1,4,64]{2,1,0:T(4,128)S(1)}, s32[1,4,64]{2,1,0:T(4,128)}, u32[]{:S(2)}) copy-start(s32[1,4,64]{2,1,0:T(4,128)} %depth_hbm.1) | copy-start | bytes 3076
  2.4 8.1 %collective-permute-start = (f32[904,128]{1,0:T(8,128)S(1)}, f32[904,128]{1,0:T(8,128)S(1)}, u32[]{:S(2)}, u32[]{:S(2)}) collective-permute-start(f32[904,128]{1,0:T(8,128)S(1)} %get-tuple-element.20), channel_id=1, source_target_pairs={{0,1},{1,0},{2,3},{3,2},{4,5},{5,4},{6,7},{7,6},{8,9},{9,8},{10,11... | collective-permute-start | bytes 1388552 | tf_op jit(solution)/shard_map/ppermute | solution.py:474
  2.5 8.0 %collective-permute-start.1 = (f32[392,128]{1,0:T(8,128)S(1)}, f32[392,128]{1,0:T(8,128)S(1)}, u32[]{:S(2)}, u32[]{:S(2)}) collective-permute-start(f32[392,128]{1,0:T(8,128)S(1)} %get-tuple-element.21), channel_id=1, source_target_pairs={{1,2},{2,1},{3,4},{4,3},{5,6},{6,5},{7,8},{8,7},{9,10},{10,9},{11,... | collective-permute-start | bytes 602120 | tf_op jit(solution)/shard_map/ppermute | solution.py:482
  5.9 8.7 %collective-permute-start.2 = (f32[512,128]{1,0:T(8,128)S(1)}, f32[512,128]{1,0:T(8,128)S(1)}, u32[]{:S(2)}, u32[]{:S(2)}) collective-permute-start(f32[512,128]{1,0:T(8,128)S(1)} %get-tuple-element.22), channel_id=1, source_target_pairs={{1,2},{2,1},{3,4},{4,3},{5,6},{6,5},{7,8},{8,7},{9,10},{10,9},{11,... | collective-permute-start | bytes 786440 | tf_op jit(solution)/shard_map/ppermute | solution.py:482
  9.0 0.7 %copy-start.3 = (s32[4,64]{1,0:T(4,128)S(1)}, s32[4,64]{1,0:T(4,128)}, u32[]{:S(2)}) copy-start(s32[4,64]{1,0:T(4,128)} %map_hbm.1) | copy-start | bytes 3076
  10.5 4.1 %copy-start = (bf16[1,6,4,64,128]{4,3,2,1,0:T(8,128)(2,1)S(1)}, bf16[1,6,4,64,128]{4,3,2,1,0:T(8,128)(2,1)}, u32[]{:S(2)}) copy-start(bf16[1,6,4,64,128]{4,3,2,1,0:T(8,128)(2,1)} %saved_ref.1) | copy-start | bytes 1179652
  15.5 4.1 %collective-permute-start.3 = (f32[3,32,128]{2,1,0:T(8,128)S(1)}, f32[3,32,128]{2,1,0:T(8,128)S(1)}, u32[]{:S(2)}, u32[]{:S(2)}) collective-permute-start(f32[3,32,128]{2,1,0:T(8,128)S(1)} %get-tuple-element.26), channel_id=1, source_target_pairs={{0,1},{1,0},{2,3},{3,2},{4,5},{5,4},{6,7},{7,6},{8,9},{9,8},{10,11... | collective-permute-start | bytes 147464 | tf_op jit(solution)/shard_map/ppermute | solution.py:474
  18.7 12.7 %copy-start.1 = (f32[9,1,32,128]{3,2,1,0:T(8,128)S(1)}, f32[9,1,32,128]{3,2,1,0:T(8,128)}, u32[]{:S(2)}) copy-start(f32[9,1,32,128]{3,2,1,0:T(8,128)} %param.11) | copy-start | bytes 442372
  19.6 4.1 %collective-permute-start.4 = (f32[32,128]{1,0:T(8,128)S(1)}, f32[32,128]{1,0:T(8,128)S(1)}, u32[]{:S(2)}, u32[]{:S(2)}) collective-permute-start(f32[32,128]{1,0:T(8,128)S(1)} %get-tuple-element.36), channel_id=1, source_target_pairs={{0,2},{1,3},{2,0},{3,1},{4,6},{5,7},{6,4},{7,5},{8,10},{9,11},{10,... | collective-permute-start | bytes 49160 | tf_op jit(solution)/shard_map/ppermute | solution.py:515
  21.1 6.5 %collective-permute-start.5 = (f32[32,128]{1,0:T(8,128)S(1)}, f32[32,128]{1,0:T(8,128)S(1)}, u32[]{:S(2)}, u32[]{:S(2)}) collective-permute-start(f32[32,128]{1,0:T(8,128)S(1)} %get-tuple-element.37), channel_id=1, source_target_pairs={{2,4},{3,5},{4,2},{5,3},{6,8},{7,9},{8,6},{9,7},{10,12},{11,13},{1... | collective-permute-start | bytes 49160 | tf_op jit(solution)/shard_map/ppermute | solution.py:516
  23.0 4.6 %collective-permute-start.6 = (f32[32,128]{1,0:T(8,128)S(1)}, f32[32,128]{1,0:T(8,128)S(1)}, u32[]{:S(2)}, u32[]{:S(2)}) collective-permute-start(f32[32,128]{1,0:T(8,128)S(1)} %slice_bitcast_fusion), channel_id=1, source_target_pairs={{5,1},{7,3},{9,5},{11,7},{13,9},{15,11},{21,17},{23,19},{25,21},{2... | collective-permute-start | bytes 49160 | tf_op jit(solution)/shard_map/ppermute | solution.py:517
  27.6 3.8 %collective-permute-start.7 = (f32[32,128]{1,0:T(8,128)S(1)}, f32[32,128]{1,0:T(8,128)S(1)}, u32[]{:S(2)}, u32[]{:S(2)}) collective-permute-start(f32[32,128]{1,0:T(8,128)S(1)} %fusion.17), channel_id=1, source_target_pairs={{0,16},{16,0},{1,17},{17,1},{2,18},{18,2},{3,19},{19,3},{4,20},{20... | collective-permute-start | bytes 49160 | tf_op jit(solution)/shard_map/ppermute | solution.py:491

commit v7 on v6

--- a/solution.py
+++ b/solution.py
@@ -156,6 +156,10 @@
     first_scale = jnp.where(index == 0, 0.0, 1.0)
     last_scale = jnp.where(index == lax.axis_size("space") - 1, 0.0, 1.0)
     return odd, first_scale, last_scale
+
+
+def even_group():
+    return lax.rem(lax.axis_index("src"), 2) == 0
 
 
 def emit_level(emit, first, state, planes, rows, lane):
@@ -201,15 +205,16 @@
         first_sweep(fields, medium_ref, scale_ref, one, i, rows)
         if k == 1:
             emit_level(emit, 0, one, planes, rows, lane)
+            first_part = even_group()
             for row in chunks(rows):
                 here = pl.ds(row, ROWS)
-                for part in range(2):
-                    emit(4 + part, row, medium_ref[part, 0, here, :], medium_ref[part, last, here, :])
+                ends = [jnp.where(first_part, medium_ref[0, j, here, :], medium_ref[1, j, here, :]) for j in (0, last)]
+                emit(4, row, ends[0], ends[1])
     for copy in columns:
         copy.wait()
     meta_ref[pl.ds(0, 1), pl.ds(0, rows)] = levels[pl.ds(last, 1), :].astype(jnp.float32)
     meta_ref[pl.ds(1, 1), pl.ds(0, rows)] = owners[pl.ds(last, 1), :].astype(jnp.float32)
-    chip_ref[pl.ds(6 * rows, PAD), :] = meta_ref[...]
+    chip_ref[pl.ds(5 * rows, PAD), :] = meta_ref[...]
 
 
 def no_plane(c, row):
@@ -287,35 +292,49 @@
             put(moment_ref, (c, i), row, value)
 
 
-def early_kernel(
-    medium_ref, scale_ref, one, pair_ref, chip_ref, three, extra_ref, two, held, delta_low, delta_high, delta_two,
+def early_kernel(medium_ref, scale_ref, one, pair_ref, chip_ref, two, held):
+    planes, rows, width = medium_ref.shape[1:]
+    lane = lane_of(width)
+    odd, first_scale, _ = parity_and_ends()
+    for ref in (two, held):
+        clear_pads(ref)
+    from_below, from_above = readers(odd, pair_ref, 0, chip_ref, 0, rows)
+    sweep_slab(
+        planes_of(one), held, two, one, medium_ref, scale_ref, sweep_steps[1],
+        lambda part, row: (from_below(2 * (part // 3), row), from_below(2 * (part // 3) + 1, row)),
+        lambda c, row: from_above(WHERE_YZ[c], row),
+        first_scale, planes, rows, lane,
+    )
+
+
+def second_kernel(
+    medium_ref, scale_ref, one, two, pair_ref, chip_ref, other_ref, three, extra_ref, held, delta_low, delta_high, delta_two,
 ):
     planes, rows, width = medium_ref.shape[1:]
     lane = lane_of(width)
     odd, first_scale, last_scale = parity_and_ends()
-    for ref in (two, three, held, delta_low, delta_high, delta_two):
+    for ref in (three, held, delta_low, delta_high, delta_two):
         clear_pads(ref)
-    from_below, from_above = readers(odd, pair_ref, 0, chip_ref, 0, rows)
+    first_part = even_group()
+
+    def medium_next(above, part, row):
+        pair = pair_ref[message_rows(4 + part, row, rows), :]
+        chip, other = chip_ref[message_rows(4, row, rows), :], other_ref[pl.ds(row, ROWS), :]
+        chip = jnp.where(first_part, chip, other) if part == 0 else jnp.where(first_part, other, chip)
+        return jnp.where(odd, chip, pair) if above else jnp.where(odd, pair, chip)
 
     for row in chunks(rows):
         sums = edge_sums(lambda c, s: rows_at(one, (c, planes - 1), row, s), lane)
-        scale = (sweep_steps[1] * last_scale) / (4.0 + from_above(4, row))
+        scale = (sweep_steps[1] * last_scale) / (4.0 + medium_next(True, 0, row))
         for k, c in enumerate((1, 2, 4, 5)):
             put(delta_high, (c,), row, scale * sums[k])
-        scale = sweep_steps[1] / (4.0 + from_below(4, row))
+        scale = sweep_steps[1] / (4.0 + medium_next(False, 0, row))
         for part in (0, 3):
             ey, ez = rows_at(one, (part + 1, 0), row), rows_at(one, (part + 2, 0), row)
             put(delta_low, (part + 1,), row, scale * ey)
             put(delta_low, (part + 2,), row, scale * ez)
             put(delta_low, (part,), row, scale * ((behind(ez, lane) - ez) + (rows_at(one, (part + 1, 0), row, -1) - ey)))
 
-    sweep_slab(
-        planes_of(one), held, two, one, medium_ref, scale_ref, sweep_steps[1],
-        lambda part, row: (from_below(2 * (part // 3), row), from_below(2 * (part // 3) + 1, row)),
-        lambda c, row: from_above(WHERE_YZ[c], row),
-        first_scale, planes, rows, lane,
-    )
-
     none = [0.0] * 6
     for row in chunks(rows):
         values = curl(lambda c, s: rows_at(delta_low, (c,), row, s), lambda c: rows_at(two, (c, 0), row), lane)
@@ -325,7 +344,7 @@
         before = {1: -rows_at(delta_low, (2,), row), 2: rows_at(delta_low, (1,), row),
                   4: -rows_at(delta_low, (5,), row), 5: rows_at(delta_low, (4,), row)}
         image = curl_back(lambda c, s: rows_at(held, (c, 0), row, s), lambda c: before[c], lane)
-        real, imag = from_below(4, row), from_below(5, row)
+        real, imag = medium_next(False, 0, row), medium_next(False, 1, row)
         new = updated(
             [rows_at(delta_low, (c,), row) for c in range(6)], image, none, 0.0, real, imag, sweep_steps[2] / (4.0 + real)
         )
@@ -342,7 +361,7 @@
     for row in chunks(rows):
         here = pl.ds(row, ROWS)
         sums = edge_sums(lambda c, s: rows_at(two, (c, planes - 1), row, s), lane)
-        real, imag = from_above(4, row), from_above(5, row)
+        real, imag = medium_next(True, 0, row), medium_next(True, 1, row)
         scale = (sweep_steps[2] * last_scale) / (4.0 + real)
         center, image = {}, {}
         for part in (0, 3):
@@ -548,7 +567,7 @@
     given = (adjoint_source, medium, depth, plane_map)
     chip, medium, scales, own, meta = call(
         start_kernel,
-        [(6 * rows + PAD, width), medium.shape, scale, state, (PAD, width)],
+        [(5 * rows + PAD, width), medium.shape, scale, state, (PAD, width)],
         [(6, planes, rows, width), columns, columns, pltpu.SemaphoreType.DMA((2 * planes + 2,))],
         tuple(pltpu.with_memory_space_constraint(a, pltpu.HBM) for a in given),
         in_specs=[hbm] * 4,
@@ -566,19 +585,22 @@
     position = lax.broadcasted_iota(jnp.int32, (planes, rows, width), 2).astype(jnp.float32)
     outside = float(size)
     owner = jnp.where(position < levels[:, :, None], (owners - here)[:, :, None], outside)
-    below = jnp.where(lax.rem(index, 2) == 1, pair[14 * rows :], chip[6 * rows :])
+    below = jnp.where(lax.rem(index, 2) == 1, pair[14 * rows :], chip[5 * rows :])
     edge = jnp.where(position[0] < below[0, :rows, None], (below[1, :rows] - here)[:, None], outside)
-    first, extra = call(
-        early_kernel,
+    groups = lax.axis_size("src")
+    other = lax.ppermute(chip[4 * rows : 5 * rows], "src", [(i, i ^ 1) for i in range(groups)])
+    (first,) = call(early_kernel, [state], [held], (medium, scales, own, pair, chip))
+    second, extra = call(
+        second_kernel,
         [state, (8, rows, width)],
-        [state, held, (6,) + plane, (6,) + plane, (6,) + plane],
-        (medium, scales, own, pair, chip),
+        [held, (6,) + plane, (6,) + plane, (6,) + plane],
+        (medium, scales, own, first, pair, chip, other),
     )
     send, stay = call(
         last_kernel,
         [(REACH + 1, rows // 2, width), (REACH + 1, rows // 2, width)],
         [(6, 2) + plane, (4,) + plane, state, held, (3, planes) + plane, (2 * REACH + 2, rows, width)],
-        (own, medium, forward_field, scales, owner, edge, pair, chip_one, first, extra),
+        (own, medium, forward_field, scales, owner, edge, pair, chip_one, second, extra),
     )
     total = sum_over_groups(gather_owned(send, stay))
     return transposed_smooth(total[None], rough)

time: 32.4 us -> 31.7 us (0.978)
  waiting for transfers between devices: 10.1 us -> 9.24 us
    ppermute x2, waiting for transfers between devices: 3.09 us -> 0.34 us  [chip_swap(): return lax.ppermute(value, 'space', pairs)]
    ppermute x0 -> x1, waiting for transfers between devices: none -> 1.86 us  [slab(): lax.ppermute(chip[4 * rows:5 * rows], 'src', [(i, i ^ 1) for i in range(g...]
    ppermute x0 -> x1, starting transfers between devices: none -> 1.49 us  [slab(): lax.ppermute(chip[4 * rows:5 * rows], 'src', [(i, i ^ 1) for i in range(g...]
    ppermute x2, starting transfers between devices: 3.32 us -> 1.9 us  [core_swap(): return lax.ppermute(value, 'space', [(i, i ^ 1) for i in range(size)])]
    pallas_call x4 -> x5, Pallas kernels: 4.79 us -> 4.89 us  [call(): pl.pallas_call(kernel, out_shape=[jax.ShapeDtypeStruct(s, jnp.float32) fo...]
  transfers between devices with their start and end apart: 8 -> 9, of which waited for: 5 -> 5; matrix products, arithmetic and copies ran while one was open for 1% -> 1% of each run, Pallas kernels for 5% -> 5%
where the time goes in v7:
time: 31.7 us; the launch traced here: 31.4 us
  starting transfers between devices  15.4 us (49%)
  waiting for transfers between devices  9.24 us (29%)
  Pallas kernels  4.89 us (15%)
  other arithmetic  0.97 us (3%)
  local copies, waits for them, and re-layouts  0.7 us (2%)
    ppermute x2, starting transfers between devices, chip_swap(): return lax.ppermute(value, 'space', pairs)  6.46 us
    pallas_call x5, Pallas kernels, call(): pl.pallas_call(kernel, out_shape=[jax.ShapeDtypeStruct(s, jnp.float32) fo...  4.89 us
    ppermute x1, waiting for transfers between devices, gather_owned(): from_outer = lax.ppermute(jnp.where(upward, below, above), 'space', outer)  3.91 us
    ppermute x1, waiting for transfers between devices, sum_over_groups(): lax.ppermute(value, 'src', [(i, i ^ step) for i in range(size)])  2.25 us
    ppermute x1, starting transfers between devices, gather_owned(): from_outer = lax.ppermute(jnp.where(upward, below, above), 'space', outer)  1.91 us
    ppermute x2, starting transfers between devices, core_swap(): return lax.ppermute(value, 'space', [(i, i ^ 1) for i in range(size)])  1.9 us
    ppermute x1, waiting for transfers between devices, slab(): lax.ppermute(chip[4 * rows:5 * rows], 'src', [(i, i ^ 1) for i in range(g...  1.86 us
    ppermute x1, starting transfers between devices, sum_over_groups(): lax.ppermute(value, 'src', [(i, i ^ step) for i in range(size)])  1.56 us
  transfers between devices with their start and end apart: 9, of which 5 were waited for; matrix products, arithmetic and copies ran while one was open for 1% of the time, Pallas kernels for 5%

profile of v7, /device:TPU:8, one launch (start us, length us, event | category | flops | bytes accessed | tf_op | source)
XLA Modules:
  0.0 31.4 jit_solution(18190382459949415072)
XLA Ops:
  0.0 1.4 %shard_map.64 = (f32[328,128]{1,0:T(8,128)S(1)}, f32[2,4,64,128]{3,2,1,0:T(8,128)S(1)}, f32[4,64,128]{2,1,0:T(8,128)S(1)}, f32[6,4,80,128]{3,2,1,0:T(8,128)S(1)}, f32[8,128]{1,0:T(8,128)S(1)}) custom-call(f32[1,6,4,64,128]{4,3,2,1,0:T(8,128)} %source_hbm.1, f32[2,4,64,128]{3,2,1,0:T(8,128)} %medium_hbm.1, s32[1,4,64]{2,1,0:T(4,128)} %depth_hbm.1, ...), custom_call_target="tpu_custom_call" | custom-call | flops 1048576 | bytes 1048576 | tf_op jit(solution)/shard_map/pallas_call | solution.py:480
  1.4 0.9 %shard_map.65 = (f32[512,128]{1,0:T(8,128)S(1)}, f32[904,128]{1,0:T(8,128)S(1)}) custom-call(f32[2,4,64,128]{3,2,1,0:T(8,128)S(1)} %get-tuple-element.17.medium_ref, f32[4,64,128]{2,1,0:T(8,128)S(1)} %get-tuple-element.18.scale_ref, f32[6,4,80,128]{3,2,1,0:T(8,128)S(1)} %get-tuple-element.16.one.base_ref, f32[8,128]{1,0:T(8,128)S(1)} %get-tuple-element.19.meta_ref), custom_call_target="tpu_custom_call" | custom-call | flops 1048576 | bytes 1048576 | tf_op jit(solution)/shard_map/pallas_call | solution.py:480
  2.4 0.0 copy-start.2
  2.4 0.1 collective-permute-start
  2.5 3.4 %collective-permute-start.1 = (f32[328,128]{1,0:T(8,128)S(1)}, f32[328,128]{1,0:T(8,128)S(1)}, u32[]{:S(2)}, u32[]{:S(2)}) collective-permute-start(f32[328,128]{1,0:T(8,128)S(1)} %get-tuple-element.21), channel_id=1, source_target_pairs={{1,2},{2,1},{3,4},{4,3},{5,6},{6,5},{7,8},{8,7},{9,10},{10,9},{11,... | collective-permute-start | bytes 503816 | tf_op jit(solution)/shard_map/ppermute | solution.py:501
  5.9 3.1 %collective-permute-start.2 = (f32[512,128]{1,0:T(8,128)S(1)}, f32[512,128]{1,0:T(8,128)S(1)}, u32[]{:S(2)}, u32[]{:S(2)}) collective-permute-start(f32[512,128]{1,0:T(8,128)S(1)} %get-tuple-element.22), channel_id=1, source_target_pairs={{1,2},{2,1},{3,4},{4,3},{5,6},{6,5},{7,8},{8,7},{9,10},{10,9},{11,... | collective-permute-start | bytes 786440 | tf_op jit(solution)/shard_map/ppermute | solution.py:501
  8.9 0.0 copy-done.2
  9.0 0.0 copy-start.3
  9.0 0.7 %copy-done.3 = s32[4,64]{1,0:T(4,128)S(1)} copy-done((s32[4,64]{1,0:T(4,128)S(1)}, s32[4,64]{1,0:T(4,128)}, u32[]{:S(2)}) %copy-start.3) | copy-done | bytes 1048
  9.7 0.1 compare_select_fusion.owner_ref
  9.8 0.3 %collective-permute-done.1.chip_ref = f32[328,128]{1,0:T(8,128)S(1)} collective-permute-done((f32[328,128]{1,0:T(8,128)S(1)}, f32[328,128]{1,0:T(8,128)S(1)}, u32[]{:S(2)}, u32[]{:S(2)}) %collective-permute-start.1) | collective-permute-done | bytes 167968 | tf_op jit(solution)/shard_map/ppermute | solution.py:501
  10.1 1.5 %collective-permute-start.3 = (f32[64,128]{1,0:T(8,128)S(1)}, f32[64,128]{1,0:T(8,128)S(1)}, u32[]{:S(2)}, u32[]{:S(2)}) collective-permute-start(f32[64,128]{1,0:T(8,128)S(1)} %slice.119), channel_id=1, source_target_pairs={{0,16},{16,0},{1,17},{17,1},{2,18},{18,2},{3,19},{19,3},{4,20},{20... | collective-permute-start | bytes 98312 | tf_op jit(solution)/shard_map/ppermute | solution.py:591
  11.6 0.0 collective-permute-done.pair_ref
  11.7 0.6 %shard_map.66.two = f32[6,4,80,128]{3,2,1,0:T(8,128)S(1)} custom-call(f32[2,4,64,128]{3,2,1,0:T(8,128)S(1)} %get-tuple-element.17.medium_ref, f32[4,64,128]{2,1,0:T(8,128)S(1)} %get-tuple-element.18.scale_ref, f32[6,4,80,128]{3,2,1,0:T(8,128)S(1)} %get-tuple-element.16.one.base_ref, f32[904,128]{1,0:T(8,128)S(1)} %collective-permute-done.pair_ref, ...), custom_call_target="tpu_custom_call" | custom-call | flops 1048576 | bytes 1048576 | tf_op jit(solution)/shard_map/pallas_call | solution.py:480
  12.2 0.0 copy-start
  12.2 1.9 %collective-permute-done.3.other_ref = f32[64,128]{1,0:T(8,128)S(1)} collective-permute-done((f32[64,128]{1,0:T(8,128)S(1)}, f32[64,128]{1,0:T(8,128)S(1)}, u32[]{:S(2)}, u32[]{:S(2)}) %collective-permute-start.3) | collective-permute-done | bytes 32800 | tf_op jit(solution)/shard_map/ppermute | solution.py:591
  14.1 1.1 %shard_map.67 = (f32[6,4,80,128]{3,2,1,0:T(8,128)S(1)}, f32[8,64,128]{2,1,0:T(8,128)S(1)}) custom-call(f32[2,4,64,128]{3,2,1,0:T(8,128)S(1)} %get-tuple-element.17.medium_ref, f32[4,64,128]{2,1,0:T(8,128)S(1)} %get-tuple-element.18.scale_ref, f32[6,4,80,128]{3,2,1,0:T(8,128)S(1)} %get-tuple-element.16.one.base_ref, f32[6,4,80,128]{3,2,1,0:T(8,128)S(1)} %shard_map.66.two, ...), custom_call_target="tpu_custom_call" | custom-call | flops 1048576 | bytes 1048576 | tf_op jit(solution)/shard_map/pallas_call | solution.py:480
  15.2 0.1 compare_select_fusion.1.edge_ref
  15.3 0.0 collective-permute-done.2.chip_ref
  15.3 0.0 copy-done
  15.3 0.9 %shard_map.68 = (f32[3,32,128]{2,1,0:T(8,128)S(1)}, f32[3,32,128]{2,1,0:T(8,128)S(1)}) custom-call(f32[6,4,80,128]{3,2,1,0:T(8,128)S(1)} %get-tuple-element.16.one.base_ref, f32[2,4,64,128]{3,2,1,0:T(8,128)S(1)} %get-tuple-element.17.medium_ref, bf16[1,6,4,64,128]{4,3,2,1,0:T(8,128)(2,1)S(1)} %copy-done, f32[4,64,128]{2,1,0:T(8,128)S(1)} %get-tuple-element.18.scale_ref, ...), custom_call_target="tpu_custom_call" | custom-call | flops 1048576 | bytes 1048576 | tf_op jit(solution)/shard_map/pallas_call | solution.py:480
  16.2 1.8 %collective-permute-start.4 = (f32[3,32,128]{2,1,0:T(8,128)S(1)}, f32[3,32,128]{2,1,0:T(8,128)S(1)}, u32[]{:S(2)}, u32[]{:S(2)}) collective-permute-start(f32[3,32,128]{2,1,0:T(8,128)S(1)} %get-tuple-element.26), channel_id=1, source_target_pairs={{0,1},{1,0},{2,3},{3,2},{4,5},{5,4},{6,7},{7,6},{8,9},{9,8},{10,11... | collective-permute-start | bytes 147464 | tf_op jit(solution)/shard_map/ppermute | solution.py:493
  18.0 0.9 %collective-permute-done.4 = f32[3,32,128]{2,1,0:T(8,128)S(1)} collective-permute-done((f32[3,32,128]{2,1,0:T(8,128)S(1)}, f32[3,32,128]{2,1,0:T(8,128)S(1)}, u32[]{:S(2)}, u32[]{:S(2)}) %collective-permute-start.4) | collective-permute-done | bytes 49184 | tf_op jit(solution)/shard_map/ppermute | solution.py:493
  18.9 1.5 %collective-permute-start.5 = (f32[32,128]{1,0:T(8,128)S(1)}, f32[32,128]{1,0:T(8,128)S(1)}, u32[]{:S(2)}, u32[]{:S(2)}) collective-permute-start(f32[32,128]{1,0:T(8,128)S(1)} %get-tuple-element.36), channel_id=1, source_target_pairs={{0,2},{1,3},{2,0},{3,1},{4,6},{5,7},{6,4},{7,5},{8,10},{9,11},{10,... | collective-permute-start | bytes 49160 | tf_op jit(solution)/shard_map/ppermute | solution.py:534
  20.4 1.9 %collective-permute-start.6 = (f32[32,128]{1,0:T(8,128)S(1)}, f32[32,128]{1,0:T(8,128)S(1)}, u32[]{:S(2)}, u32[]{:S(2)}) collective-permute-start(f32[32,128]{1,0:T(8,128)S(1)} %get-tuple-element.37), channel_id=1, source_target_pairs={{2,4},{3,5},{4,2},{5,3},{6,8},{7,9},{8,6},{9,7},{10,12},{11,13},{1... | collective-permute-start | bytes 49160 | tf_op jit(solution)/shard_map/ppermute | solution.py:535
  22.3 0.7 %collective-permute-start.7 = (f32[32,128]{1,0:T(8,128)S(1)}, f32[32,128]{1,0:T(8,128)S(1)}, u32[]{:S(2)}, u32[]{:S(2)}) collective-permute-start(f32[32,128]{1,0:T(8,128)S(1)} %slice_bitcast_fusion), channel_id=1, source_target_pairs={{5,1},{7,3},{9,5},{11,7},{13,9},{15,11},{21,17},{23,19},{25,21},{2... | collective-permute-start | bytes 49160 | tf_op jit(solution)/shard_map/ppermute | solution.py:536
  23.0 0.0 collective-permute-done.5
  23.0 3.9 %collective-permute-done.6 = f32[32,128]{1,0:T(8,128)S(1)} collective-permute-done((f32[32,128]{1,0:T(8,128)S(1)}, f32[32,128]{1,0:T(8,128)S(1)}, u32[]{:S(2)}, u32[]{:S(2)}) %collective-permute-start.6) | collective-permute-done | bytes 16416 | tf_op jit(solution)/shard_map/ppermute | solution.py:535
  26.9 0.0 collective-permute-done.7
  26.9 1.6 %collective-permute-start.8 = (f32[32,128]{1,0:T(8,128)S(1)}, f32[32,128]{1,0:T(8,128)S(1)}, u32[]{:S(2)}, u32[]{:S(2)}) collective-permute-start(f32[32,128]{1,0:T(8,128)S(1)} %fusion.17), channel_id=1, source_target_pairs={{0,16},{16,0},{1,17},{17,1},{2,18},{18,2},{3,19},{19,3},{4,20},{20... | collective-permute-start | bytes 49160 | tf_op jit(solution)/shard_map/ppermute | solution.py:510
  28.5 2.2 %collective-permute-done.8 = f32[32,128]{1,0:T(8,128)S(1)} collective-permute-done((f32[32,128]{1,0:T(8,128)S(1)}, f32[32,128]{1,0:T(8,128)S(1)}, u32[]{:S(2)}, u32[]{:S(2)}) %collective-permute-start.8) | collective-permute-done | bytes 16416 | tf_op jit(solution)/shard_map/ppermute | solution.py:510
  30.7 0.7 %fusion.7 = f32[1,32,128]{2,1,0:T(8,128)} fusion(f32[1,32,128]{2,1,0:T(8,128)S(1)} %get-tuple-element.35, f32[1,32,128]{2,1,0:T(8,128)S(1)} %get-tuple-element.34, f32[1,32,128]{2,1,0:T(8,128)S(1)} %get-tuple-element.33, f32[1,32,128]{2,1,0:T(8,128)S(1)} %get-tuple-element.32, f32[1,32,128]{2,1,0:T(8,128)S(1)} %get-tuple-element.31, ...), kind=kLoop, calls=%fused_computation.17 | loop fusion | flops 36864 | bytes 180224 | tf_op jit(solution)/shard_map/add | solution.py:549
  (13 shorter events, 0.1 us)
Async XLA Ops:
  2.4 6.6 %copy-start.2 = (s32[1,4,64]{2,1,0:T(4,128)S(1)}, s32[1,4,64]{2,1,0:T(4,128)}, u32[]{:S(2)}) copy-start(s32[1,4,64]{2,1,0:T(4,128)} %depth_hbm.1) | copy-start | bytes 3076
  2.4 9.3 %collective-permute-start = (f32[904,128]{1,0:T(8,128)S(1)}, f32[904,128]{1,0:T(8,128)S(1)}, u32[]{:S(2)}, u32[]{:S(2)}) collective-permute-start(f32[904,128]{1,0:T(8,128)S(1)} %get-tuple-element.20), channel_id=1, source_target_pairs={{0,1},{1,0},{2,3},{3,2},{4,5},{5,4},{6,7},{7,6},{8,9},{9,8},{10,11... | collective-permute-start | bytes 1388552 | tf_op jit(solution)/shard_map/ppermute | solution.py:493
  2.5 7.7 %collective-permute-start.1 = (f32[328,128]{1,0:T(8,128)S(1)}, f32[328,128]{1,0:T(8,128)S(1)}, u32[]{:S(2)}, u32[]{:S(2)}) collective-permute-start(f32[328,128]{1,0:T(8,128)S(1)} %get-tuple-element.21), channel_id=1, source_target_pairs={{1,2},{2,1},{3,4},{4,3},{5,6},{6,5},{7,8},{8,7},{9,10},{10,9},{11,... | collective-permute-start | bytes 503816 | tf_op jit(solution)/shard_map/ppermute | solution.py:501
  5.9 9.4 %collective-permute-start.2 = (f32[512,128]{1,0:T(8,128)S(1)}, f32[512,128]{1,0:T(8,128)S(1)}, u32[]{:S(2)}, u32[]{:S(2)}) collective-permute-start(f32[512,128]{1,0:T(8,128)S(1)} %get-tuple-element.22), channel_id=1, source_target_pairs={{1,2},{2,1},{3,4},{4,3},{5,6},{6,5},{7,8},{8,7},{9,10},{10,9},{11,... | collective-permute-start | bytes 786440 | tf_op jit(solution)/shard_map/ppermute | solution.py:501
  9.0 0.7 %copy-start.3 = (s32[4,64]{1,0:T(4,128)S(1)}, s32[4,64]{1,0:T(4,128)}, u32[]{:S(2)}) copy-start(s32[4,64]{1,0:T(4,128)} %map_hbm.1) | copy-start | bytes 3076
  10.1 3.9 %collective-permute-start.3 = (f32[64,128]{1,0:T(8,128)S(1)}, f32[64,128]{1,0:T(8,128)S(1)}, u32[]{:S(2)}, u32[]{:S(2)}) collective-permute-start(f32[64,128]{1,0:T(8,128)S(1)} %slice.119), channel_id=1, source_target_pairs={{0,16},{16,0},{1,17},{17,1},{2,18},{18,2},{3,19},{19,3},{4,20},{20... | collective-permute-start | bytes 98312 | tf_op jit(solution)/shard_map/ppermute | solution.py:591
  12.2 3.0 %copy-start = (bf16[1,6,4,64,128]{4,3,2,1,0:T(8,128)(2,1)S(1)}, bf16[1,6,4,64,128]{4,3,2,1,0:T(8,128)(2,1)}, u32[]{:S(2)}) copy-start(bf16[1,6,4,64,128]{4,3,2,1,0:T(8,128)(2,1)} %saved_ref.1) | copy-start | bytes 1179652
  16.2 2.7 %collective-permute-start.4 = (f32[3,32,128]{2,1,0:T(8,128)S(1)}, f32[3,32,128]{2,1,0:T(8,128)S(1)}, u32[]{:S(2)}, u32[]{:S(2)}) collective-permute-start(f32[3,32,128]{2,1,0:T(8,128)S(1)} %get-tuple-element.26), channel_id=1, source_target_pairs={{0,1},{1,0},{2,3},{3,2},{4,5},{5,4},{6,7},{7,6},{8,9},{9,8},{10,11... | collective-permute-start | bytes 147464 | tf_op jit(solution)/shard_map/ppermute | solution.py:493
  18.0 12.7 %copy-start.1 = (f32[9,1,32,128]{3,2,1,0:T(8,128)S(1)}, f32[9,1,32,128]{3,2,1,0:T(8,128)}, u32[]{:S(2)}) copy-start(f32[9,1,32,128]{3,2,1,0:T(8,128)} %param.11) | copy-start | bytes 442372
  18.9 4.1 %collective-permute-start.5 = (f32[32,128]{1,0:T(8,128)S(1)}, f32[32,128]{1,0:T(8,128)S(1)}, u32[]{:S(2)}, u32[]{:S(2)}) collective-permute-start(f32[32,128]{1,0:T(8,128)S(1)} %get-tuple-element.36), channel_id=1, source_target_pairs={{0,2},{1,3},{2,0},{3,1},{4,6},{5,7},{6,4},{7,5},{8,10},{9,11},{10,... | collective-permute-start | bytes 49160 | tf_op jit(solution)/shard_map/ppermute | solution.py:534
  20.4 6.5 %collective-permute-start.6 = (f32[32,128]{1,0:T(8,128)S(1)}, f32[32,128]{1,0:T(8,128)S(1)}, u32[]{:S(2)}, u32[]{:S(2)}) collective-permute-start(f32[32,128]{1,0:T(8,128)S(1)} %get-tuple-element.37), channel_id=1, source_target_pairs={{2,4},{3,5},{4,2},{5,3},{6,8},{7,9},{8,6},{9,7},{10,12},{11,13},{1... | collective-permute-start | bytes 49160 | tf_op jit(solution)/shard_map/ppermute | solution.py:535
  22.3 4.6 %collective-permute-start.7 = (f32[32,128]{1,0:T(8,128)S(1)}, f32[32,128]{1,0:T(8,128)S(1)}, u32[]{:S(2)}, u32[]{:S(2)}) collective-permute-start(f32[32,128]{1,0:T(8,128)S(1)} %slice_bitcast_fusion), channel_id=1, source_target_pairs={{5,1},{7,3},{9,5},{11,7},{13,9},{15,11},{21,17},{23,19},{25,21},{2... | collective-permute-start | bytes 49160 | tf_op jit(solution)/shard_map/ppermute | solution.py:536
  26.9 3.8 %collective-permute-start.8 = (f32[32,128]{1,0:T(8,128)S(1)}, f32[32,128]{1,0:T(8,128)S(1)}, u32[]{:S(2)}, u32[]{:S(2)}) collective-permute-start(f32[32,128]{1,0:T(8,128)S(1)} %fusion.17), channel_id=1, source_target_pairs={{0,16},{16,0},{1,17},{17,1},{2,18},{18,2},{3,19},{19,3},{4,20},{20... | collective-permute-start | bytes 49160 | tf_op jit(solution)/shard_map/ppermute | solution.py:510

commit v8 on v7

--- a/solution.py
+++ b/solution.py
@@ -1,5 +1,3 @@
-import functools
-
 import jax
 import jax.numpy as jnp
 from jax import lax
@@ -13,7 +11,7 @@
 sweep_steps = (0.323, 1.658, 0.422, 0.752)
 
 PAD = 8
-ROWS = 16
+ROWS = 32
 
 
 def lane_of(width):
@@ -37,18 +35,25 @@
     ref[index + (pl.ds(PAD + row, ROWS), slice(None))] = value
 
 
-def clear_pads(ref):
-    rows = ref.shape[-2]
-    lead = ref.shape[:-2]
+def indices(lead):
+    out = [()]
+    for size in lead:
+        out = [index + (i,) for index in out for i in range(size)]
+    return out
+
+
+def clear_after(ref, components=(0, 2, 3, 5)):
     zero = jnp.zeros((PAD, ref.shape[-1]), jnp.float32)
-    for flat in range(functools.reduce(lambda a, b: a * b, lead, 1)):
-        index = []
-        rest = flat
-        for size in reversed(lead):
-            index.insert(0, rest % size)
-            rest //= size
-        ref[tuple(index) + (pl.ds(0, PAD), slice(None))] = zero
-        ref[tuple(index) + (pl.ds(rows - PAD, PAD), slice(None))] = zero
+    for index in indices(ref.shape[:-2]):
+        if index[0] in components:
+            ref[index + (pl.ds(ref.shape[-2] - PAD, PAD), slice(None))] = zero
+
+
+def clear_before(ref, components=(0, 2, 3, 5)):
+    zero = jnp.zeros((PAD, ref.shape[-1]), jnp.float32)
+    for index in indices(ref.shape[:-2]):
+        if index[0] in components:
+            ref[index + (pl.ds(0, PAD), slice(None))] = zero
 
 
 def chunks(total):
@@ -101,7 +106,7 @@
     return lambda c, i, row, shift=0: rows_at(ref, (c, i), row, shift)
 
 
-def sweep_slab(state, held, result, base, medium_ref, scale_ref, weight, low, high, first_scale, planes, rows, lane, wanted=None):
+def sweep_slab(state, held, result, base, medium_ref, scale_ref, weight, low, high, first_scale, planes, rows, lane, wanted=None, skip=()):
     wanted = range(planes) if wanted is None else wanted
     needed = sorted({i for w in wanted for i in (w - 1, w)})
     for i in needed:
@@ -120,7 +125,7 @@
                 return high(c, row)
 
             values = curl(lambda c, s: state(c, i, row, s), ahead_of, lane)
-            for c in range(6):
+            for c in range(6) if i in wanted else (1, 2, 4, 5):
                 put(held, (c, i + 1), row, values[c])
     for i in wanted:
         for row in chunks(rows):
@@ -138,7 +143,8 @@
                 weight * scale_ref[i, here, :],
             )
             for c in range(6):
-                put(result, (c, i), row, new[c])
+                if (c, i) not in skip:
+                    put(result, (c, i), row, new[c])
 
 
 def first_sweep(fields, medium_ref, scale_ref, state, i, rows):
@@ -193,7 +199,8 @@
     ]
     for copy in copies + columns:
         copy.start()
-    clear_pads(one)
+    clear_after(one)
+    clear_before(one, (1, 4))
     meta_ref[...] = jnp.zeros_like(meta_ref)
 
     def emit(slot, row, below, above):
@@ -229,9 +236,9 @@
     planes, rows, width = medium_ref.shape[1:]
     lane = lane_of(width)
     odd, first_scale, _ = parity_and_ends()
-    clear_pads(two)
-    clear_pads(three)
-    clear_pads(held)
+    clear_after(two)
+    clear_after(three, (0, 3))
+    clear_before(held)
 
     def emitter(slots, to_chip):
         def emit(slot, row, below, above):
@@ -241,14 +248,15 @@
 
         return emit
 
+    last = planes - 1
     sweep_slab(
         planes_of(one), held, two, one, medium_ref, scale_ref, sweep_steps[1], no_sums, no_plane, first_scale,
-        planes, rows, lane,
+        planes, rows, lane, wanted=sorted({0, 1, last - 1, last}), skip=[(c, 1) for c in (0, 3) if 1 < last - 1],
     )
     emit_level(emitter(6, 0), 0, two, planes, rows, lane)
     sweep_slab(
         planes_of(two), held, three, one, medium_ref, scale_ref, sweep_steps[2], no_sums, no_plane, first_scale,
-        planes, rows, lane, wanted=sorted({0, planes - 1}),
+        planes, rows, lane, wanted=sorted({0, last}), skip=[(c, 0) for c in (0, 3)],
     )
     emit_level(emitter(10, 4), 0, three, planes, rows, lane)
     emit_level(emitter(0, None), 0, one, planes, rows, lane)
@@ -296,8 +304,8 @@
     planes, rows, width = medium_ref.shape[1:]
     lane = lane_of(width)
     odd, first_scale, _ = parity_and_ends()
-    for ref in (two, held):
-        clear_pads(ref)
+    clear_after(two)
+    clear_before(held)
     from_below, from_above = readers(odd, pair_ref, 0, chip_ref, 0, rows)
     sweep_slab(
         planes_of(one), held, two, one, medium_ref, scale_ref, sweep_steps[1],
@@ -313,8 +321,10 @@
     planes, rows, width = medium_ref.shape[1:]
     lane = lane_of(width)
     odd, first_scale, last_scale = parity_and_ends()
-    for ref in (three, held, delta_low, delta_high, delta_two):
-        clear_pads(ref)
+    for ref in (three, delta_low, delta_high):
+        clear_after(ref)
+    clear_after(delta_two, (0, 3))
+    clear_before(held)
     first_part = even_group()
 
     def medium_next(above, part, row):
@@ -394,8 +404,10 @@
     planes, rows, width = medium_ref.shape[1:]
     lane = lane_of(width)
     odd, first_scale, _ = parity_and_ends()
-    for ref in (ends, above, held, moment):
-        clear_pads(ref)
+    clear_after(ends)
+    clear_before(above, (0, 2))
+    clear_before(held)
+    clear_after(moment, (0, 2))
     last = planes - 1
 
     from_below, from_above = readers(odd, pair_ref, 6, chip_ref, 0, rows)

time: 31.7 us -> 31.6 us (level)
  no operation moved by 1% of the time
where the time goes in v8:
time: 31.6 us; the launch traced here: 31.4 us
  starting transfers between devices  15.4 us (49%)
  waiting for transfers between devices  9.24 us (29%)
  Pallas kernels  4.87 us (15%)
  other arithmetic  0.97 us (3%)
  local copies, waits for them, and re-layouts  0.7 us (2%)
    ppermute x2, starting transfers between devices, chip_swap(): return lax.ppermute(value, 'space', pairs)  6.46 us
    pallas_call x5, Pallas kernels, call(): pl.pallas_call(kernel, out_shape=[jax.ShapeDtypeStruct(s, jnp.float32) fo...  4.87 us
    ppermute x1, waiting for transfers between devices, gather_owned(): from_outer = lax.ppermute(jnp.where(upward, below, above), 'space', outer)  3.91 us
    ppermute x1, waiting for transfers between devices, sum_over_groups(): lax.ppermute(value, 'src', [(i, i ^ step) for i in range(size)])  2.25 us
    ppermute x1, starting transfers between devices, gather_owned(): from_outer = lax.ppermute(jnp.where(upward, below, above), 'space', outer)  1.91 us
    ppermute x2, starting transfers between devices, core_swap(): return lax.ppermute(value, 'space', [(i, i ^ 1) for i in range(size)])  1.91 us
    ppermute x1, waiting for transfers between devices, slab(): lax.ppermute(chip[4 * rows:5 * rows], 'src', [(i, i ^ 1) for i in range(g...  1.85 us
    ppermute x1, starting transfers between devices, sum_over_groups(): lax.ppermute(value, 'src', [(i, i ^ step) for i in range(size)])  1.56 us
  transfers between devices with their start and end apart: 9, of which 5 were waited for; matrix products, arithmetic and copies ran while one was open for 1% of the time, Pallas kernels for 5%

profile of v8, /device:TPU:8, one launch (start us, length us, event | category | flops | bytes accessed | tf_op | source)
XLA Modules:
  0.0 31.4 jit_solution(18444771713635647736)
XLA Ops:
  0.0 1.4 %shard_map.64 = (f32[328,128]{1,0:T(8,128)S(1)}, f32[2,4,64,128]{3,2,1,0:T(8,128)S(1)}, f32[4,64,128]{2,1,0:T(8,128)S(1)}, f32[6,4,80,128]{3,2,1,0:T(8,128)S(1)}, f32[8,128]{1,0:T(8,128)S(1)}) custom-call(f32[1,6,4,64,128]{4,3,2,1,0:T(8,128)} %source_hbm.1, f32[2,4,64,128]{3,2,1,0:T(8,128)} %medium_hbm.1, s32[1,4,64]{2,1,0:T(4,128)} %depth_hbm.1, ...), custom_call_target="tpu_custom_call" | custom-call | flops 1048576 | bytes 1048576 | tf_op jit(solution)/shard_map/pallas_call | solution.py:492
  1.4 0.9 %shard_map.65 = (f32[512,128]{1,0:T(8,128)S(1)}, f32[904,128]{1,0:T(8,128)S(1)}) custom-call(f32[2,4,64,128]{3,2,1,0:T(8,128)S(1)} %get-tuple-element.17.medium_ref, f32[4,64,128]{2,1,0:T(8,128)S(1)} %get-tuple-element.18.scale_ref, f32[6,4,80,128]{3,2,1,0:T(8,128)S(1)} %get-tuple-element.16.one.base_ref, f32[8,128]{1,0:T(8,128)S(1)} %get-tuple-element.19.meta_ref), custom_call_target="tpu_custom_call" | custom-call | flops 1048576 | bytes 1048576 | tf_op jit(solution)/shard_map/pallas_call | solution.py:492
  2.4 0.0 copy-start.2
  2.4 0.1 collective-permute-start
  2.5 3.4 %collective-permute-start.1 = (f32[328,128]{1,0:T(8,128)S(1)}, f32[328,128]{1,0:T(8,128)S(1)}, u32[]{:S(2)}, u32[]{:S(2)}) collective-permute-start(f32[328,128]{1,0:T(8,128)S(1)} %get-tuple-element.21), channel_id=1, source_target_pairs={{1,2},{2,1},{3,4},{4,3},{5,6},{6,5},{7,8},{8,7},{9,10},{10,9},{11,... | collective-permute-start | bytes 503816 | tf_op jit(solution)/shard_map/ppermute | solution.py:513
  5.9 3.1 %collective-permute-start.2 = (f32[512,128]{1,0:T(8,128)S(1)}, f32[512,128]{1,0:T(8,128)S(1)}, u32[]{:S(2)}, u32[]{:S(2)}) collective-permute-start(f32[512,128]{1,0:T(8,128)S(1)} %get-tuple-element.22), channel_id=1, source_target_pairs={{1,2},{2,1},{3,4},{4,3},{5,6},{6,5},{7,8},{8,7},{9,10},{10,9},{11,... | collective-permute-start | bytes 786440 | tf_op jit(solution)/shard_map/ppermute | solution.py:513
  8.9 0.0 copy-done.2
  9.0 0.0 copy-start.3
  9.0 0.7 %copy-done.3 = s32[4,64]{1,0:T(4,128)S(1)} copy-done((s32[4,64]{1,0:T(4,128)S(1)}, s32[4,64]{1,0:T(4,128)}, u32[]{:S(2)}) %copy-start.3) | copy-done | bytes 1048
  9.7 0.1 compare_select_fusion.owner_ref
  9.8 0.3 %collective-permute-done.1.chip_ref = f32[328,128]{1,0:T(8,128)S(1)} collective-permute-done((f32[328,128]{1,0:T(8,128)S(1)}, f32[328,128]{1,0:T(8,128)S(1)}, u32[]{:S(2)}, u32[]{:S(2)}) %collective-permute-start.1) | collective-permute-done | bytes 167968 | tf_op jit(solution)/shard_map/ppermute | solution.py:513
  10.1 1.5 %collective-permute-start.3 = (f32[64,128]{1,0:T(8,128)S(1)}, f32[64,128]{1,0:T(8,128)S(1)}, u32[]{:S(2)}, u32[]{:S(2)}) collective-permute-start(f32[64,128]{1,0:T(8,128)S(1)} %slice.119), channel_id=1, source_target_pairs={{0,16},{16,0},{1,17},{17,1},{2,18},{18,2},{3,19},{19,3},{4,20},{20... | collective-permute-start | bytes 98312 | tf_op jit(solution)/shard_map/ppermute | solution.py:603
  11.6 0.0 collective-permute-done.pair_ref
  11.6 0.6 %shard_map.66.two = f32[6,4,80,128]{3,2,1,0:T(8,128)S(1)} custom-call(f32[2,4,64,128]{3,2,1,0:T(8,128)S(1)} %get-tuple-element.17.medium_ref, f32[4,64,128]{2,1,0:T(8,128)S(1)} %get-tuple-element.18.scale_ref, f32[6,4,80,128]{3,2,1,0:T(8,128)S(1)} %get-tuple-element.16.one.base_ref, f32[904,128]{1,0:T(8,128)S(1)} %collective-permute-done.pair_ref, ...), custom_call_target="tpu_custom_call" | custom-call | flops 1048576 | bytes 1048576 | tf_op jit(solution)/shard_map/pallas_call | solution.py:492
  12.2 0.0 copy-start
  12.2 1.9 %collective-permute-done.3.other_ref = f32[64,128]{1,0:T(8,128)S(1)} collective-permute-done((f32[64,128]{1,0:T(8,128)S(1)}, f32[64,128]{1,0:T(8,128)S(1)}, u32[]{:S(2)}, u32[]{:S(2)}) %collective-permute-start.3) | collective-permute-done | bytes 32800 | tf_op jit(solution)/shard_map/ppermute | solution.py:603
  14.1 1.1 %shard_map.67 = (f32[6,4,80,128]{3,2,1,0:T(8,128)S(1)}, f32[8,64,128]{2,1,0:T(8,128)S(1)}) custom-call(f32[2,4,64,128]{3,2,1,0:T(8,128)S(1)} %get-tuple-element.17.medium_ref, f32[4,64,128]{2,1,0:T(8,128)S(1)} %get-tuple-element.18.scale_ref, f32[6,4,80,128]{3,2,1,0:T(8,128)S(1)} %get-tuple-element.16.one.base_ref, f32[6,4,80,128]{3,2,1,0:T(8,128)S(1)} %shard_map.66.two, ...), custom_call_target="tpu_custom_call" | custom-call | flops 1048576 | bytes 1048576 | tf_op jit(solution)/shard_map/pallas_call | solution.py:492
  15.2 0.1 compare_select_fusion.1.edge_ref
  15.2 0.0 collective-permute-done.2.chip_ref
  15.3 0.9 %shard_map.68 = (f32[3,32,128]{2,1,0:T(8,128)S(1)}, f32[3,32,128]{2,1,0:T(8,128)S(1)}) custom-call(f32[6,4,80,128]{3,2,1,0:T(8,128)S(1)} %get-tuple-element.16.one.base_ref, f32[2,4,64,128]{3,2,1,0:T(8,128)S(1)} %get-tuple-element.17.medium_ref, bf16[1,6,4,64,128]{4,3,2,1,0:T(8,128)(2,1)S(1)} %copy-done, f32[4,64,128]{2,1,0:T(8,128)S(1)} %get-tuple-element.18.scale_ref, ...), custom_call_target="tpu_custom_call" | custom-call | flops 1048576 | bytes 1048576 | tf_op jit(solution)/shard_map/pallas_call | solution.py:492
  16.2 1.8 %collective-permute-start.4 = (f32[3,32,128]{2,1,0:T(8,128)S(1)}, f32[3,32,128]{2,1,0:T(8,128)S(1)}, u32[]{:S(2)}, u32[]{:S(2)}) collective-permute-start(f32[3,32,128]{2,1,0:T(8,128)S(1)} %get-tuple-element.26), channel_id=1, source_target_pairs={{0,1},{1,0},{2,3},{3,2},{4,5},{5,4},{6,7},{7,6},{8,9},{9,8},{10,11... | collective-permute-start | bytes 147464 | tf_op jit(solution)/shard_map/ppermute | solution.py:505
  18.0 0.9 %collective-permute-done.4 = f32[3,32,128]{2,1,0:T(8,128)S(1)} collective-permute-done((f32[3,32,128]{2,1,0:T(8,128)S(1)}, f32[3,32,128]{2,1,0:T(8,128)S(1)}, u32[]{:S(2)}, u32[]{:S(2)}) %collective-permute-start.4) | collective-permute-done | bytes 49184 | tf_op jit(solution)/shard_map/ppermute | solution.py:505
  18.9 1.5 %collective-permute-start.5 = (f32[32,128]{1,0:T(8,128)S(1)}, f32[32,128]{1,0:T(8,128)S(1)}, u32[]{:S(2)}, u32[]{:S(2)}) collective-permute-start(f32[32,128]{1,0:T(8,128)S(1)} %get-tuple-element.36), channel_id=1, source_target_pairs={{0,2},{1,3},{2,0},{3,1},{4,6},{5,7},{6,4},{7,5},{8,10},{9,11},{10,... | collective-permute-start | bytes 49160 | tf_op jit(solution)/shard_map/ppermute | solution.py:546
  20.3 1.9 %collective-permute-start.6 = (f32[32,128]{1,0:T(8,128)S(1)}, f32[32,128]{1,0:T(8,128)S(1)}, u32[]{:S(2)}, u32[]{:S(2)}) collective-permute-start(f32[32,128]{1,0:T(8,128)S(1)} %get-tuple-element.37), channel_id=1, source_target_pairs={{2,4},{3,5},{4,2},{5,3},{6,8},{7,9},{8,6},{9,7},{10,12},{11,13},{1... | collective-permute-start | bytes 49160 | tf_op jit(solution)/shard_map/ppermute | solution.py:547
  22.3 0.7 %collective-permute-start.7 = (f32[32,128]{1,0:T(8,128)S(1)}, f32[32,128]{1,0:T(8,128)S(1)}, u32[]{:S(2)}, u32[]{:S(2)}) collective-permute-start(f32[32,128]{1,0:T(8,128)S(1)} %slice_bitcast_fusion), channel_id=1, source_target_pairs={{5,1},{7,3},{9,5},{11,7},{13,9},{15,11},{21,17},{23,19},{25,21},{2... | collective-permute-start | bytes 49160 | tf_op jit(solution)/shard_map/ppermute | solution.py:548
  22.9 0.0 collective-permute-done.5
  22.9 3.9 %collective-permute-done.6 = f32[32,128]{1,0:T(8,128)S(1)} collective-permute-done((f32[32,128]{1,0:T(8,128)S(1)}, f32[32,128]{1,0:T(8,128)S(1)}, u32[]{:S(2)}, u32[]{:S(2)}) %collective-permute-start.6) | collective-permute-done | bytes 16416 | tf_op jit(solution)/shard_map/ppermute | solution.py:547
  26.9 0.0 collective-permute-done.7
  26.9 1.6 %collective-permute-start.8 = (f32[32,128]{1,0:T(8,128)S(1)}, f32[32,128]{1,0:T(8,128)S(1)}, u32[]{:S(2)}, u32[]{:S(2)}) collective-permute-start(f32[32,128]{1,0:T(8,128)S(1)} %fusion.17), channel_id=1, source_target_pairs={{0,16},{16,0},{1,17},{17,1},{2,18},{18,2},{3,19},{19,3},{4,20},{20... | collective-permute-start | bytes 49160 | tf_op jit(solution)/shard_map/ppermute | solution.py:522
  28.4 2.2 %collective-permute-done.8 = f32[32,128]{1,0:T(8,128)S(1)} collective-permute-done((f32[32,128]{1,0:T(8,128)S(1)}, f32[32,128]{1,0:T(8,128)S(1)}, u32[]{:S(2)}, u32[]{:S(2)}) %collective-permute-start.8) | collective-permute-done | bytes 16416 | tf_op jit(solution)/shard_map/ppermute | solution.py:522
  30.7 0.0 copy-done.1
  30.7 0.7 %fusion.7 = f32[1,32,128]{2,1,0:T(8,128)} fusion(f32[1,32,128]{2,1,0:T(8,128)S(1)} %get-tuple-element.35, f32[1,32,128]{2,1,0:T(8,128)S(1)} %get-tuple-element.34, f32[1,32,128]{2,1,0:T(8,128)S(1)} %get-tuple-element.33, f32[1,32,128]{2,1,0:T(8,128)S(1)} %get-tuple-element.32, f32[1,32,128]{2,1,0:T(8,128)S(1)} %get-tuple-element.31, ...), kind=kLoop, calls=%fused_computation.17 | loop fusion | flops 36864 | bytes 180224 | tf_op jit(solution)/shard_map/add | solution.py:561
  (13 shorter events, 0.1 us)
Async XLA Ops:
  2.4 6.6 %copy-start.2 = (s32[1,4,64]{2,1,0:T(4,128)S(1)}, s32[1,4,64]{2,1,0:T(4,128)}, u32[]{:S(2)}) copy-start(s32[1,4,64]{2,1,0:T(4,128)} %depth_hbm.1) | copy-start | bytes 3076
  2.4 9.3 %collective-permute-start = (f32[904,128]{1,0:T(8,128)S(1)}, f32[904,128]{1,0:T(8,128)S(1)}, u32[]{:S(2)}, u32[]{:S(2)}) collective-permute-start(f32[904,128]{1,0:T(8,128)S(1)} %get-tuple-element.20), channel_id=1, source_target_pairs={{0,1},{1,0},{2,3},{3,2},{4,5},{5,4},{6,7},{7,6},{8,9},{9,8},{10,11... | collective-permute-start | bytes 1388552 | tf_op jit(solution)/shard_map/ppermute | solution.py:505
  2.5 7.7 %collective-permute-start.1 = (f32[328,128]{1,0:T(8,128)S(1)}, f32[328,128]{1,0:T(8,128)S(1)}, u32[]{:S(2)}, u32[]{:S(2)}) collective-permute-start(f32[328,128]{1,0:T(8,128)S(1)} %get-tuple-element.21), channel_id=1, source_target_pairs={{1,2},{2,1},{3,4},{4,3},{5,6},{6,5},{7,8},{8,7},{9,10},{10,9},{11,... | collective-permute-start | bytes 503816 | tf_op jit(solution)/shard_map/ppermute | solution.py:513
  5.9 9.4 %collective-permute-start.2 = (f32[512,128]{1,0:T(8,128)S(1)}, f32[512,128]{1,0:T(8,128)S(1)}, u32[]{:S(2)}, u32[]{:S(2)}) collective-permute-start(f32[512,128]{1,0:T(8,128)S(1)} %get-tuple-element.22), channel_id=1, source_target_pairs={{1,2},{2,1},{3,4},{4,3},{5,6},{6,5},{7,8},{8,7},{9,10},{10,9},{11,... | collective-permute-start | bytes 786440 | tf_op jit(solution)/shard_map/ppermute | solution.py:513
  9.0 0.7 %copy-start.3 = (s32[4,64]{1,0:T(4,128)S(1)}, s32[4,64]{1,0:T(4,128)}, u32[]{:S(2)}) copy-start(s32[4,64]{1,0:T(4,128)} %map_hbm.1) | copy-start | bytes 3076
  10.1 3.9 %collective-permute-start.3 = (f32[64,128]{1,0:T(8,128)S(1)}, f32[64,128]{1,0:T(8,128)S(1)}, u32[]{:S(2)}, u32[]{:S(2)}) collective-permute-start(f32[64,128]{1,0:T(8,128)S(1)} %slice.119), channel_id=1, source_target_pairs={{0,16},{16,0},{1,17},{17,1},{2,18},{18,2},{3,19},{19,3},{4,20},{20... | collective-permute-start | bytes 98312 | tf_op jit(solution)/shard_map/ppermute | solution.py:603
  12.2 3.0 %copy-start = (bf16[1,6,4,64,128]{4,3,2,1,0:T(8,128)(2,1)S(1)}, bf16[1,6,4,64,128]{4,3,2,1,0:T(8,128)(2,1)}, u32[]{:S(2)}) copy-start(bf16[1,6,4,64,128]{4,3,2,1,0:T(8,128)(2,1)} %saved_ref.1) | copy-start | bytes 1179652
  16.2 2.7 %collective-permute-start.4 = (f32[3,32,128]{2,1,0:T(8,128)S(1)}, f32[3,32,128]{2,1,0:T(8,128)S(1)}, u32[]{:S(2)}, u32[]{:S(2)}) collective-permute-start(f32[3,32,128]{2,1,0:T(8,128)S(1)} %get-tuple-element.26), channel_id=1, source_target_pairs={{0,1},{1,0},{2,3},{3,2},{4,5},{5,4},{6,7},{7,6},{8,9},{9,8},{10,11... | collective-permute-start | bytes 147464 | tf_op jit(solution)/shard_map/ppermute | solution.py:505
  18.0 12.7 %copy-start.1 = (f32[9,1,32,128]{3,2,1,0:T(8,128)S(1)}, f32[9,1,32,128]{3,2,1,0:T(8,128)}, u32[]{:S(2)}) copy-start(f32[9,1,32,128]{3,2,1,0:T(8,128)} %param.11) | copy-start | bytes 442372
  18.9 4.1 %collective-permute-start.5 = (f32[32,128]{1,0:T(8,128)S(1)}, f32[32,128]{1,0:T(8,128)S(1)}, u32[]{:S(2)}, u32[]{:S(2)}) collective-permute-start(f32[32,128]{1,0:T(8,128)S(1)} %get-tuple-element.36), channel_id=1, source_target_pairs={{0,2},{1,3},{2,0},{3,1},{4,6},{5,7},{6,4},{7,5},{8,10},{9,11},{10,... | collective-permute-start | bytes 49160 | tf_op jit(solution)/shard_map/ppermute | solution.py:546
  20.3 6.5 %collective-permute-start.6 = (f32[32,128]{1,0:T(8,128)S(1)}, f32[32,128]{1,0:T(8,128)S(1)}, u32[]{:S(2)}, u32[]{:S(2)}) collective-permute-start(f32[32,128]{1,0:T(8,128)S(1)} %get-tuple-element.37), channel_id=1, source_target_pairs={{2,4},{3,5},{4,2},{5,3},{6,8},{7,9},{8,6},{9,7},{10,12},{11,13},{1... | collective-permute-start | bytes 49160 | tf_op jit(solution)/shard_map/ppermute | solution.py:547
  22.3 4.6 %collective-permute-start.7 = (f32[32,128]{1,0:T(8,128)S(1)}, f32[32,128]{1,0:T(8,128)S(1)}, u32[]{:S(2)}, u32[]{:S(2)}) collective-permute-start(f32[32,128]{1,0:T(8,128)S(1)} %slice_bitcast_fusion), channel_id=1, source_target_pairs={{5,1},{7,3},{9,5},{11,7},{13,9},{15,11},{21,17},{23,19},{25,21},{2... | collective-permute-start | bytes 49160 | tf_op jit(solution)/shard_map/ppermute | solution.py:548
  26.9 3.8 %collective-permute-start.8 = (f32[32,128]{1,0:T(8,128)S(1)}, f32[32,128]{1,0:T(8,128)S(1)}, u32[]{:S(2)}, u32[]{:S(2)}) collective-permute-start(f32[32,128]{1,0:T(8,128)S(1)} %fusion.17), channel_id=1, source_target_pairs={{0,16},{16,0},{1,17},{17,1},{2,18},{18,2},{3,19},{19,3},{4,20},{20... | collective-permute-start | bytes 49160 | tf_op jit(solution)/shard_map/ppermute | solution.py:522
